TPU v7x, 16 devices: a whole 2x2x2 slice. The times are simulated.
16 devices in a mesh: dp: 2 (over z), fsdp: 8 (over y, x, core).
Axes of the slice: x: 2, y: 2, z: 2, core: 2. Of those that a mesh axis runs over, the one named last changes fastest.
Arguments:
- tokens: bfloat16 [256, 128, 2560], P(('dp', 'fsdp')), parts along dimension 0
- gain_in: bfloat16 [2560], P('fsdp')
- w_dq: bfloat16 [2560, 768], P('fsdp')
- gain_q: bfloat16 [768], P('fsdp')
- w_uq: bfloat16 [768, 3840], P('fsdp')
- w_dkv: bfloat16 [2560, 288], P('fsdp')
- gain_kv: bfloat16 [256], P('fsdp')
- w_ukv: bfloat16 [256, 5120], P('fsdp')
- w_out: bfloat16 [2560, 2560], P('fsdp')
Outputs:
- output 1: bfloat16 [256, 128, 2560], P(('dp', 'fsdp')), parts along dimension 0
- output 2: bfloat16 [256, 128, 256], P(('dp', 'fsdp')), parts along dimension 0
- output 3: bfloat16 [256, 128, 32], P(('dp', 'fsdp')), parts along dimension 0
There are 2 independent parts. A program takes and returns all parts, laid end to end along the dimension named above; an argument that names none is the same for every part.
All inputs are finite; a program needn't handle non-finite values.
Results may differ from a plain program's by a relative error of at most 0.00647502.
Values are sent between devices in bfloat16 or wider.
A program may use at most 1 GiB of HBM per device.

v0:
```python
import jax
import jax.numpy as jnp
from jax import lax
from jax.sharding import PartitionSpec as P, NamedSharding

EPSILON = 1e-6
ROPE_THETA = 10000.0


def rms_scale(values_in, gain_vec):
    values_f32 = values_in.astype(jnp.float32)
    inv_rms = lax.rsqrt(jnp.mean(values_f32 * values_f32, axis=-1, keepdims=True) + EPSILON)
    return values_f32 * inv_rms * gain_vec.astype(jnp.float32)


def rope_tables(seq_len, rope_dim):
    half_dim = rope_dim // 2
    inv_freq = ROPE_THETA ** (-2.0 * jnp.arange(half_dim, dtype=jnp.float32) / rope_dim)
    angles = jnp.arange(seq_len, dtype=jnp.float32)[:, None] * inv_freq[None, :]
    return jnp.cos(angles), jnp.sin(angles)


def apply_rope(values_in, cos_t, sin_t):
    half_dim = values_in.shape[-1] // 2
    lo_half = values_in[..., :half_dim]
    hi_half = values_in[..., half_dim:]
    return jnp.concatenate([lo_half * cos_t - hi_half * sin_t, hi_half * cos_t + lo_half * sin_t], axis=-1)


def head_dims(w_uq, w_dkv, gain_kv, w_ukv, w_out):
    rope_dim = w_dkv.shape[1] - gain_kv.shape[0]
    nope_total = w_ukv.shape[1] - w_out.shape[0]
    n_heads = (w_uq.shape[1] - nope_total) // rope_dim
    return n_heads, nope_total // n_heads, rope_dim, w_out.shape[0] // n_heads


def latents(tokens, gain_in, w_dq, gain_q, w_dkv, gain_kv, cos_t, sin_t):
    kv_rank = gain_kv.shape[0]
    normed = rms_scale(tokens, gain_in).astype(jnp.bfloat16)
    q_down = jnp.einsum('btd,dr->btr', normed, w_dq, preferred_element_type=jnp.float32)
    q_lat = rms_scale(q_down, gain_q).astype(jnp.bfloat16)
    kv_down = jnp.einsum('btd,dr->btr', normed, w_dkv, preferred_element_type=jnp.float32)
    latent = rms_scale(kv_down[:, :, :kv_rank], gain_kv).astype(jnp.bfloat16)
    k_pe = apply_rope(kv_down[:, :, kv_rank:], cos_t, sin_t).astype(jnp.bfloat16)
    return q_lat, latent, k_pe


def attend(q_lat, latent, k_pe, w_uq, w_ukv, w_out, head_info, cos_t, sin_t):
    n_heads, nope_dim, rope_dim, v_dim = head_info
    n_prompts = q_lat.shape[0]
    seq_len = q_lat.shape[1]
    q_full = jnp.einsum('btr,rc->btc', q_lat, w_uq, preferred_element_type=jnp.float32)
    q_full = q_full.reshape(n_prompts, seq_len, n_heads, nope_dim + rope_dim)
    q_nope = q_full[..., :nope_dim].astype(jnp.bfloat16)
    q_pe = apply_rope(q_full[..., nope_dim:], cos_t[:, None, :], sin_t[:, None, :]).astype(jnp.bfloat16)
    kv_up = jnp.einsum('btr,rc->btc', latent, w_ukv, preferred_element_type=jnp.float32).astype(jnp.bfloat16)
    kv_up = kv_up.reshape(n_prompts, seq_len, n_heads, nope_dim + v_dim)
    k_nope = kv_up[..., :nope_dim]
    values = kv_up[..., nope_dim:]
    score_scale = (nope_dim + rope_dim) ** -0.5
    scores = jnp.einsum('bqhd,bkhd->bhqk', q_nope, k_nope, preferred_element_type=jnp.float32)
    scores = scores + jnp.einsum('crie,cle->cirl', q_pe, k_pe, preferred_element_type=jnp.float32)
    causal = jnp.arange(seq_len)[:, None] >= jnp.arange(seq_len)[None, :]
    scores = jnp.where(causal, scores * score_scale, -1e30)
    attn_probs = jax.nn.softmax(scores, axis=-1).astype(jnp.bfloat16)
    attn_out = jnp.einsum('bhqk,bkhd->bqhd', attn_probs, values, preferred_element_type=jnp.float32).astype(jnp.bfloat16)
    attn_out = attn_out.reshape(n_prompts, seq_len, n_heads * v_dim)
    return jnp.einsum('btc,cd->btd', attn_out, w_out, preferred_element_type=jnp.float32)


def attend_each(q_lat, latent, k_pe, w_uq, w_ukv, w_out, head_info, cos_t, sin_t):
    def one_prompt(operands):
        q_one, lat_one, pe_one = operands
        return attend(q_one[None], lat_one[None], pe_one[None], w_uq, w_ukv, w_out, head_info, cos_t, sin_t)[0]

    return lax.map(one_prompt, (q_lat, latent, k_pe))


def solution(mesh):
    batch_spec = P(('dp', 'fsdp'))
    row_spec = P('fsdp')
    mat_spec = P('fsdp', None)

    def run_block(tokens, gain_in, w_dq, gain_q, w_uq, w_dkv, gain_kv, w_ukv, w_out):
        head_info = head_dims(w_uq, w_dkv, gain_kv, w_ukv, w_out)
        seq_len = tokens.shape[1]

        def local_block(tok_blk, gain_in_s, w_dq_s, gain_q_s, w_uq_s, w_dkv_s, gain_kv_s, w_ukv_s, w_out_s):
            cos_t, sin_t = rope_tables(seq_len, head_info[2])
            gain_in_all = lax.all_gather(gain_in_s, 'fsdp', tiled=True)
            w_dq_all = lax.all_gather(w_dq_s, 'fsdp', tiled=True)
            gain_q_all = lax.all_gather(gain_q_s, 'fsdp', tiled=True)
            w_dkv_all = lax.all_gather(w_dkv_s, 'fsdp', tiled=True)
            gain_kv_all = lax.all_gather(gain_kv_s, 'fsdp', tiled=True)
            q_lat, latent, k_pe = latents(tok_blk, gain_in_all, w_dq_all, gain_q_all, w_dkv_all, gain_kv_all, cos_t, sin_t)
            w_uq_all = lax.all_gather(w_uq_s, 'fsdp', tiled=True)
            w_ukv_all = lax.all_gather(w_ukv_s, 'fsdp', tiled=True)
            w_out_all = lax.all_gather(w_out_s, 'fsdp', tiled=True)
            proj_out = attend_each(q_lat, latent, k_pe, w_uq_all, w_ukv_all, w_out_all, head_info, cos_t, sin_t)
            y_blk = (tok_blk.astype(jnp.float32) + proj_out).astype(jnp.bfloat16)
            return y_blk, latent, k_pe

        mapped = jax.shard_map(
            local_block,
            mesh=mesh,
            in_specs=(batch_spec, row_spec, mat_spec, row_spec, mat_spec, mat_spec, row_spec, mat_spec, mat_spec),
            out_specs=(batch_spec, batch_spec, batch_spec),
            check_vma=False,
        )
        return mapped(tokens, gain_in, w_dq, gain_q, w_uq, w_dkv, gain_kv, w_ukv, w_out)

    return run_block
```

profile of v0, /device:TPU:0, one launch (start us, length us, event | category | flops | bytes accessed | tf_op | source)
XLA Modules:
  0.0 457.8 jit_solution(16700815692165806814)
XLA Ops:
  13.9 16.2 %all-reduce.3 = (bf16[2560]{0:T(1024)(128)(2,1)S(1)}, bf16[256]{0:T(256)(128)(2,1)S(1)}, bf16[768]{0:T(1024)(128)(2,1)S(1)}) all-reduce(bf16[2560]{0:T(1024)(128)(2,1)S(1)} %dynamic-update-slice, bf16[256]{0:T(256)(128)(2,1)S(1)} %dynamic-update-slice.1, bf16[768]{0:T(1024)(128)(2,1)S(1)} %dynamic-update-slice.2), channel_id=1, replica_groups=mesh['dp'=2,'fsdp'=8] {'fsdp'}, use_global_device_ids=true, to_apply=%add | all-reduce | flops 3584 | bytes 14336
  30.2 6.1 %fusion.29 = f32[16,128]{1,0:T(8,128)S(1)} fusion(bf16[16,128,2560]{2,1,0:T(8,128)(2,1)} %param.11), kind=kLoop, calls=%fused_computation.43 | loop fusion | flops 15726592 | bytes 10493952 | tf_op jit(solution)/shard_map/reduce_sum | solution.py:12
  36.4 2.1 copy.22
  38.5 2.3 reshape.199
  40.8 6.6 %fusion.35 = f32[16,128,288]{1,2,0:T(8,128)S(1)} fusion(bf16[2560,288,1]{0,1,2:T(8,128)(2,1)} %reshape.199, bf16[16,128,2560]{2,1,0:T(8,128)(2,1)} %param.11, f32[2560]{0:T(1024)S(1)} %convert_element_type.48, f32[16,128]{1,0:T(8,128)S(1)} %add_rsqrt_fusion.2), kind=kOutput, calls=%fused_computation.48 | convolution fusion | flops 3040870400 | bytes 14338048 | tf_op jit(solution)/shard_map/btd,dr->btr/dot_general | solution.py:42
  47.9 1.3 copy.23
  49.3 19.4 %all-gather.9.cloned.1.call-done = bf16[2560,768]{1,0:T(8,128)(2,1)} async-done(((bf16[320,768]{1,0:T(8,128)(2,1)}), bf16[2560,768]{1,0:T(8,128)(2,1)}) %all-gather.9.cloned.1.call-update) | async-done | bytes 3932176 | tf_op jit(solution)/shard_map/all_gather | solution.py:91
  68.7 12.5 %multiply_reduce_fusion = (f32[16,128]{1,0:T(8,128)S(1)}, f32[16,128,768]{2,1,0:T(8,128)S(1)}) fusion(bf16[2560,768]{1,0:T(8,128)(2,1)} %all-gather.9.cloned.1.call-done, bf16[16,128,2560]{2,1,0:T(8,128)(2,1)} %param.11, f32[2560]{0:T(1024)S(1)} %convert_element_type.48, f32[16,128]{1,0:T(8,128)S(1)} %add_rsqrt_fusion.2), kind=kOutput, calls=%fused_computation.50 | convolution fusion | flops 8077178880 | bytes 20736000 | tf_op jit(solution)/shard_map/btd,dr->btr/dot_general | solution.py:40
  81.2 2.2 multiply_convert_fusion
  83.5 26.8 %all-gather.11.cloned.1.call-done = bf16[768,3840]{1,0:T(8,128)(2,1)} async-done(((bf16[96,3840]{1,0:T(8,128)(2,1)}), bf16[768,3840]{1,0:T(8,128)(2,1)}) %all-gather.11.cloned.1.call-update) | async-done | bytes 5898256 | tf_op jit(solution)/shard_map/all_gather | solution.py:96
  110.3 8.4 %copy.24 = bf16[768,3840]{0,1:T(8,128)(2,1)} copy(bf16[768,3840]{1,0:T(8,128)(2,1)} %all-gather.11.cloned.1.call-done) | data formatting | bytes 11796480
  118.7 19.2 %all-gather.7.cloned.1.call-done = bf16[256,5120]{1,0:T(8,128)(2,1)} async-done(((bf16[32,5120]{1,0:T(8,128)(2,1)}), bf16[256,5120]{1,0:T(8,128)(2,1)}) %all-gather.7.cloned.1.call-update) | async-done | bytes 2621456 | tf_op jit(solution)/shard_map/all_gather | solution.py:97
  138.0 72.0 %all-gather.13.cloned.1.call-done = bf16[2560,2560]{1,0:T(8,128)(2,1)} async-done(((bf16[320,2560]{1,0:T(8,128)(2,1)}), bf16[2560,2560]{1,0:T(8,128)(2,1)}) %all-gather.13.cloned.1.call-update) | async-done | bytes 13107216 | tf_op jit(solution)/shard_map/all_gather | solution.py:98
  210.0 225.6 %while.13 = (s32[]{:T(128)}, f32[16,128,2560]{2,1,0:T(8,128)}, bf16[16,128,256]{2,1,0:T(8,128)(2,1)}, bf16[256,5120]{1,0:T(8,128)(2,1)}, bf16[16,128,768]{2,1,0:...) while((s32[]{:T(128)}, f32[16,128,2560]{2,1,0:T(8,128)}, ...), condition=%wide.region_6.7_spmd.clone.clone.clone, body=%wide.region_3.6_spmd.clone.clone.clone.sunk | while | flops 2986156032 | bytes 86292232 | solution.py:76
  210.0 2.3 convolution_convert_fusion.4
  213.1 4.7 %convolution_bitcast_fusion.3 = f32[1,128,40,96]{1,3,2,0:T(8,128)S(1)} fusion(bf16[40,96,768]{2,1,0:T(8,128)(2,1)} %bitcast.106, bf16[16,128,768]{2,1,0:T(8,128)(2,1)} %get-tuple-element.285, s32[]{:T(128)} %get-tuple-element.271), kind=kOutput, calls=%fused_computation.11.clone.1 | convolution fusion | flops 754974720 | bytes 8061440 | tf_op jit(solution)/shard_map/while/body/eval_jaxpr/btr,rc->btc/dot_general | solution.py:52
  221.1 3.0 fusion.73
  224.1 2.3 convolution_convert_fusion.4
  226.4 0.8 copy.29
  227.3 4.7 %convolution_bitcast_fusion.3 = f32[1,128,40,96]{1,3,2,0:T(8,128)S(1)} fusion(bf16[40,96,768]{2,1,0:T(8,128)(2,1)} %bitcast.106, bf16[16,128,768]{2,1,0:T(8,128)(2,1)} %get-tuple-element.285, s32[]{:T(128)} %get-tuple-element.271), kind=kOutput, calls=%fused_computation.11.clone.1 | convolution fusion | flops 754974720 | bytes 8061440 | tf_op jit(solution)/shard_map/while/body/eval_jaxpr/btr,rc->btc/dot_general | solution.py:52
  235.3 3.0 fusion.73
  238.2 2.3 convolution_convert_fusion.4
  241.3 4.7 %convolution_bitcast_fusion.3 = f32[1,128,40,96]{1,3,2,0:T(8,128)S(1)} fusion(bf16[40,96,768]{2,1,0:T(8,128)(2,1)} %bitcast.106, bf16[16,128,768]{2,1,0:T(8,128)(2,1)} %get-tuple-element.285, s32[]{:T(128)} %get-tuple-element.271), kind=kOutput, calls=%fused_computation.11.clone.1 | convolution fusion | flops 754974720 | bytes 8061440 | tf_op jit(solution)/shard_map/while/body/eval_jaxpr/btr,rc->btc/dot_general | solution.py:52
  249.3 3.0 fusion.73
  252.3 2.3 convolution_convert_fusion.4
  255.4 4.7 %convolution_bitcast_fusion.3 = f32[1,128,40,96]{1,3,2,0:T(8,128)S(1)} fusion(bf16[40,96,768]{2,1,0:T(8,128)(2,1)} %bitcast.106, bf16[16,128,768]{2,1,0:T(8,128)(2,1)} %get-tuple-element.285, s32[]{:T(128)} %get-tuple-element.271), kind=kOutput, calls=%fused_computation.11.clone.1 | convolution fusion | flops 754974720 | bytes 8061440 | tf_op jit(solution)/shard_map/while/body/eval_jaxpr/btr,rc->btc/dot_general | solution.py:52
  263.4 3.0 fusion.73
  266.4 2.3 convolution_convert_fusion.4
  269.5 4.7 %convolution_bitcast_fusion.3 = f32[1,128,40,96]{1,3,2,0:T(8,128)S(1)} fusion(bf16[40,96,768]{2,1,0:T(8,128)(2,1)} %bitcast.106, bf16[16,128,768]{2,1,0:T(8,128)(2,1)} %get-tuple-element.285, s32[]{:T(128)} %get-tuple-element.271), kind=kOutput, calls=%fused_computation.11.clone.1 | convolution fusion | flops 754974720 | bytes 8061440 | tf_op jit(solution)/shard_map/while/body/eval_jaxpr/btr,rc->btc/dot_general | solution.py:52
  277.5 3.0 fusion.73
  280.5 2.3 convolution_convert_fusion.4
  283.6 4.7 %convolution_bitcast_fusion.3 = f32[1,128,40,96]{1,3,2,0:T(8,128)S(1)} fusion(bf16[40,96,768]{2,1,0:T(8,128)(2,1)} %bitcast.106, bf16[16,128,768]{2,1,0:T(8,128)(2,1)} %get-tuple-element.285, s32[]{:T(128)} %get-tuple-element.271), kind=kOutput, calls=%fused_computation.11.clone.1 | convolution fusion | flops 754974720 | bytes 8061440 | tf_op jit(solution)/shard_map/while/body/eval_jaxpr/btr,rc->btc/dot_general | solution.py:52
  291.6 3.0 fusion.73
  294.6 2.3 convolution_convert_fusion.4
  297.7 4.7 %convolution_bitcast_fusion.3 = f32[1,128,40,96]{1,3,2,0:T(8,128)S(1)} fusion(bf16[40,96,768]{2,1,0:T(8,128)(2,1)} %bitcast.106, bf16[16,128,768]{2,1,0:T(8,128)(2,1)} %get-tuple-element.285, s32[]{:T(128)} %get-tuple-element.271), kind=kOutput, calls=%fused_computation.11.clone.1 | convolution fusion | flops 754974720 | bytes 8061440 | tf_op jit(solution)/shard_map/while/body/eval_jaxpr/btr,rc->btc/dot_general | solution.py:52
  305.7 3.1 fusion.73
  308.8 2.3 convolution_convert_fusion.4
  311.9 4.7 %convolution_bitcast_fusion.3 = f32[1,128,40,96]{1,3,2,0:T(8,128)S(1)} fusion(bf16[40,96,768]{2,1,0:T(8,128)(2,1)} %bitcast.106, bf16[16,128,768]{2,1,0:T(8,128)(2,1)} %get-tuple-element.285, s32[]{:T(128)} %get-tuple-element.271), kind=kOutput, calls=%fused_computation.11.clone.1 | convolution fusion | flops 754974720 | bytes 8061440 | tf_op jit(solution)/shard_map/while/body/eval_jaxpr/btr,rc->btc/dot_general | solution.py:52
  319.9 3.0 fusion.73
  322.9 2.3 convolution_convert_fusion.4
  326.0 4.7 %convolution_bitcast_fusion.3 = f32[1,128,40,96]{1,3,2,0:T(8,128)S(1)} fusion(bf16[40,96,768]{2,1,0:T(8,128)(2,1)} %bitcast.106, bf16[16,128,768]{2,1,0:T(8,128)(2,1)} %get-tuple-element.285, s32[]{:T(128)} %get-tuple-element.271), kind=kOutput, calls=%fused_computation.11.clone.1 | convolution fusion | flops 754974720 | bytes 8061440 | tf_op jit(solution)/shard_map/while/body/eval_jaxpr/btr,rc->btc/dot_general | solution.py:52
  334.0 3.0 fusion.73
  336.9 2.3 convolution_convert_fusion.4
  340.1 4.7 %convolution_bitcast_fusion.3 = f32[1,128,40,96]{1,3,2,0:T(8,128)S(1)} fusion(bf16[40,96,768]{2,1,0:T(8,128)(2,1)} %bitcast.106, bf16[16,128,768]{2,1,0:T(8,128)(2,1)} %get-tuple-element.285, s32[]{:T(128)} %get-tuple-element.271), kind=kOutput, calls=%fused_computation.11.clone.1 | convolution fusion | flops 754974720 | bytes 8061440 | tf_op jit(solution)/shard_map/while/body/eval_jaxpr/btr,rc->btc/dot_general | solution.py:52
  348.1 3.0 fusion.73
  351.1 2.3 convolution_convert_fusion.4
  354.2 4.7 %convolution_bitcast_fusion.3 = f32[1,128,40,96]{1,3,2,0:T(8,128)S(1)} fusion(bf16[40,96,768]{2,1,0:T(8,128)(2,1)} %bitcast.106, bf16[16,128,768]{2,1,0:T(8,128)(2,1)} %get-tuple-element.285, s32[]{:T(128)} %get-tuple-element.271), kind=kOutput, calls=%fused_computation.11.clone.1 | convolution fusion | flops 754974720 | bytes 8061440 | tf_op jit(solution)/shard_map/while/body/eval_jaxpr/btr,rc->btc/dot_general | solution.py:52
  362.2 3.0 fusion.73
  365.2 2.3 convolution_convert_fusion.4
  368.3 4.7 %convolution_bitcast_fusion.3 = f32[1,128,40,96]{1,3,2,0:T(8,128)S(1)} fusion(bf16[40,96,768]{2,1,0:T(8,128)(2,1)} %bitcast.106, bf16[16,128,768]{2,1,0:T(8,128)(2,1)} %get-tuple-element.285, s32[]{:T(128)} %get-tuple-element.271), kind=kOutput, calls=%fused_computation.11.clone.1 | convolution fusion | flops 754974720 | bytes 8061440 | tf_op jit(solution)/shard_map/while/body/eval_jaxpr/btr,rc->btc/dot_general | solution.py:52
  376.3 3.0 fusion.73
  379.3 2.3 convolution_convert_fusion.4
  382.4 4.7 %convolution_bitcast_fusion.3 = f32[1,128,40,96]{1,3,2,0:T(8,128)S(1)} fusion(bf16[40,96,768]{2,1,0:T(8,128)(2,1)} %bitcast.106, bf16[16,128,768]{2,1,0:T(8,128)(2,1)} %get-tuple-element.285, s32[]{:T(128)} %get-tuple-element.271), kind=kOutput, calls=%fused_computation.11.clone.1 | convolution fusion | flops 754974720 | bytes 8061440 | tf_op jit(solution)/shard_map/while/body/eval_jaxpr/btr,rc->btc/dot_general | solution.py:52
  390.4 3.0 fusion.73
  393.3 2.3 convolution_convert_fusion.4
  396.5 4.7 %convolution_bitcast_fusion.3 = f32[1,128,40,96]{1,3,2,0:T(8,128)S(1)} fusion(bf16[40,96,768]{2,1,0:T(8,128)(2,1)} %bitcast.106, bf16[16,128,768]{2,1,0:T(8,128)(2,1)} %get-tuple-element.285, s32[]{:T(128)} %get-tuple-element.271), kind=kOutput, calls=%fused_computation.11.clone.1 | convolution fusion | flops 754974720 | bytes 8061440 | tf_op jit(solution)/shard_map/while/body/eval_jaxpr/btr,rc->btc/dot_general | solution.py:52
  404.5 3.0 fusion.73
  407.4 2.3 convolution_convert_fusion.4
  410.5 4.7 %convolution_bitcast_fusion.3 = f32[1,128,40,96]{1,3,2,0:T(8,128)S(1)} fusion(bf16[40,96,768]{2,1,0:T(8,128)(2,1)} %bitcast.106, bf16[16,128,768]{2,1,0:T(8,128)(2,1)} %get-tuple-element.285, s32[]{:T(128)} %get-tuple-element.271), kind=kOutput, calls=%fused_computation.11.clone.1 | convolution fusion | flops 754974720 | bytes 8061440 | tf_op jit(solution)/shard_map/while/body/eval_jaxpr/btr,rc->btc/dot_general | solution.py:52
  418.5 3.0 fusion.73
  421.5 2.3 convolution_convert_fusion.4
  424.6 4.7 %convolution_bitcast_fusion.3 = f32[1,128,40,96]{1,3,2,0:T(8,128)S(1)} fusion(bf16[40,96,768]{2,1,0:T(8,128)(2,1)} %bitcast.106, bf16[16,128,768]{2,1,0:T(8,128)(2,1)} %get-tuple-element.285, s32[]{:T(128)} %get-tuple-element.271), kind=kOutput, calls=%fused_computation.11.clone.1 | convolution fusion | flops 754974720 | bytes 8061440 | tf_op jit(solution)/shard_map/while/body/eval_jaxpr/btr,rc->btc/dot_general | solution.py:52
  432.6 3.0 fusion.73
  435.6 15.7 %fusion.32 = bf16[16,128,2560]{2,1,0:T(8,128)(2,1)} fusion(f32[16,128,2560]{2,1,0:T(8,128)} %get-tuple-element.61, bf16[16,128,2560]{2,1,0:T(8,128)(2,1)} %param.11), kind=kLoop, calls=%fused_computation.46 | loop fusion | flops 15728640 | bytes 41943040 | tf_op jit(solution)/shard_map/convert_element_type | solution.py:100
  (312 shorter events, 69.4 us)
Async XLA Ops:
  7.2 3.5 copy-start.4
  7.2 6.0 %copy-start.1 = (bf16[320]{0:T(512)(128)(2,1)S(1)}, bf16[320]{0:T(512)(128)(2,1)}, u32[]{:S(2)}) copy-start(bf16[320]{0:T(512)(128)(2,1)} %param.12) | copy-start | bytes 1924
  7.2 6.2 %copy-start.2 = (bf16[96]{0:T(256)(128)(2,1)S(1)}, bf16[96]{0:T(256)(128)(2,1)}, u32[]{:S(2)}) copy-start(bf16[96]{0:T(256)(128)(2,1)} %param.14) | copy-start | bytes 580
  7.2 6.5 %copy-start.3 = (bf16[32]{0:T(256)(128)(2,1)S(1)}, bf16[32]{0:T(256)(128)(2,1)}, u32[]{:S(2)}) copy-start(bf16[32]{0:T(256)(128)(2,1)} %param.17) | copy-start | bytes 196
  7.2 29.2 %all-gather.15.cloned.1.call-start = ((), (), s32[]{:S(2)}) async-start(), calls=%async_computation.4 | async-start | bytes 1990656 | tf_op jit(solution)/shard_map/all_gather | solution.py:93
  7.9 60.8 %all-gather.9.cloned.1.call-start = ((), (), s32[]{:S(2)}) async-start(), calls=%async_computation.1 | async-start | bytes 4423680 | tf_op jit(solution)/shard_map/all_gather | solution.py:91
  8.7 101.6 %all-gather.11.cloned.1.call-start = ((), (), s32[]{:S(2)}) async-start(), calls=%async_computation.2 | async-start | bytes 6635520 | tf_op jit(solution)/shard_map/all_gather | solution.py:96
  9.4 128.6 %all-gather.7.cloned.1.call-start = ((), (), s32[]{:S(2)}) async-start(), calls=%async_computation | async-start | bytes 2949120 | tf_op jit(solution)/shard_map/all_gather | solution.py:97
  10.0 200.0 %all-gather.13.cloned.1.call-start = ((), (), s32[]{:S(2)}) async-start(), calls=%async_computation.3 | async-start | bytes 14745600 | tf_op jit(solution)/shard_map/all_gather | solution.py:98
  213.1 7.3 %slice-start = ((s8[13107200]{0:T(1024)(128)(4,1)}), s8[4194304]{0:T(1024)(128)(4,1)S(1)}, s32[]{:S(2)}) async-start(s8[13107200]{0:T(1024)(128)(4,1)} %bitcast.104), calls=%async_computation.5 | async-start | bytes 8388608 | tf_op jit(solution)/shard_map/while
  213.1 7.3 %slice-start.1 = ((s8[13107200]{0:T(1024)(128)(4,1)}), s8[4194304]{0:T(1024)(128)(4,1)S(1)}, s32[]{:S(2)}) async-start(s8[13107200]{0:T(1024)(128)(4,1)} %bitcast.104), calls=%async_computation.6 | async-start | bytes 8388608 | tf_op jit(solution)/shard_map/while
  218.6 2.2 slice-start.2
  219.8 1.3 slice-start.3
  227.2 7.3 %slice-start = ((s8[13107200]{0:T(1024)(128)(4,1)}), s8[4194304]{0:T(1024)(128)(4,1)S(1)}, s32[]{:S(2)}) async-start(s8[13107200]{0:T(1024)(128)(4,1)} %bitcast.104), calls=%async_computation.5 | async-start | bytes 8388608 | tf_op jit(solution)/shard_map/while
  227.2 7.3 %slice-start.1 = ((s8[13107200]{0:T(1024)(128)(4,1)}), s8[4194304]{0:T(1024)(128)(4,1)S(1)}, s32[]{:S(2)}) async-start(s8[13107200]{0:T(1024)(128)(4,1)} %bitcast.104), calls=%async_computation.6 | async-start | bytes 8388608 | tf_op jit(solution)/shard_map/while
  232.7 2.2 slice-start.2
  241.3 7.3 %slice-start = ((s8[13107200]{0:T(1024)(128)(4,1)}), s8[4194304]{0:T(1024)(128)(4,1)S(1)}, s32[]{:S(2)}) async-start(s8[13107200]{0:T(1024)(128)(4,1)} %bitcast.104), calls=%async_computation.5 | async-start | bytes 8388608 | tf_op jit(solution)/shard_map/while
  241.3 7.3 %slice-start.1 = ((s8[13107200]{0:T(1024)(128)(4,1)}), s8[4194304]{0:T(1024)(128)(4,1)S(1)}, s32[]{:S(2)}) async-start(s8[13107200]{0:T(1024)(128)(4,1)} %bitcast.104), calls=%async_computation.6 | async-start | bytes 8388608 | tf_op jit(solution)/shard_map/while
  246.8 2.2 slice-start.2
  248.0 1.3 slice-start.3
  255.4 7.3 %slice-start = ((s8[13107200]{0:T(1024)(128)(4,1)}), s8[4194304]{0:T(1024)(128)(4,1)S(1)}, s32[]{:S(2)}) async-start(s8[13107200]{0:T(1024)(128)(4,1)} %bitcast.104), calls=%async_computation.5 | async-start | bytes 8388608 | tf_op jit(solution)/shard_map/while
  255.4 7.3 %slice-start.1 = ((s8[13107200]{0:T(1024)(128)(4,1)}), s8[4194304]{0:T(1024)(128)(4,1)S(1)}, s32[]{:S(2)}) async-start(s8[13107200]{0:T(1024)(128)(4,1)} %bitcast.104), calls=%async_computation.6 | async-start | bytes 8388608 | tf_op jit(solution)/shard_map/while
  260.9 2.2 slice-start.2
  269.5 7.3 %slice-start = ((s8[13107200]{0:T(1024)(128)(4,1)}), s8[4194304]{0:T(1024)(128)(4,1)S(1)}, s32[]{:S(2)}) async-start(s8[13107200]{0:T(1024)(128)(4,1)} %bitcast.104), calls=%async_computation.5 | async-start | bytes 8388608 | tf_op jit(solution)/shard_map/while
  269.5 7.3 %slice-start.1 = ((s8[13107200]{0:T(1024)(128)(4,1)}), s8[4194304]{0:T(1024)(128)(4,1)S(1)}, s32[]{:S(2)}) async-start(s8[13107200]{0:T(1024)(128)(4,1)} %bitcast.104), calls=%async_computation.6 | async-start | bytes 8388608 | tf_op jit(solution)/shard_map/while
  275.0 2.2 slice-start.2
  276.2 1.3 slice-start.3
  283.6 7.3 %slice-start = ((s8[13107200]{0:T(1024)(128)(4,1)}), s8[4194304]{0:T(1024)(128)(4,1)S(1)}, s32[]{:S(2)}) async-start(s8[13107200]{0:T(1024)(128)(4,1)} %bitcast.104), calls=%async_computation.5 | async-start | bytes 8388608 | tf_op jit(solution)/shard_map/while
  283.6 7.3 %slice-start.1 = ((s8[13107200]{0:T(1024)(128)(4,1)}), s8[4194304]{0:T(1024)(128)(4,1)S(1)}, s32[]{:S(2)}) async-start(s8[13107200]{0:T(1024)(128)(4,1)} %bitcast.104), calls=%async_computation.6 | async-start | bytes 8388608 | tf_op jit(solution)/shard_map/while
  289.1 2.2 slice-start.2
  297.7 7.3 %slice-start = ((s8[13107200]{0:T(1024)(128)(4,1)}), s8[4194304]{0:T(1024)(128)(4,1)S(1)}, s32[]{:S(2)}) async-start(s8[13107200]{0:T(1024)(128)(4,1)} %bitcast.104), calls=%async_computation.5 | async-start | bytes 8388608 | tf_op jit(solution)/shard_map/while
  297.7 7.3 %slice-start.1 = ((s8[13107200]{0:T(1024)(128)(4,1)}), s8[4194304]{0:T(1024)(128)(4,1)S(1)}, s32[]{:S(2)}) async-start(s8[13107200]{0:T(1024)(128)(4,1)} %bitcast.104), calls=%async_computation.6 | async-start | bytes 8388608 | tf_op jit(solution)/shard_map/while
  303.2 2.2 slice-start.2
  304.4 1.3 slice-start.3
  311.9 7.3 %slice-start = ((s8[13107200]{0:T(1024)(128)(4,1)}), s8[4194304]{0:T(1024)(128)(4,1)S(1)}, s32[]{:S(2)}) async-start(s8[13107200]{0:T(1024)(128)(4,1)} %bitcast.104), calls=%async_computation.5 | async-start | bytes 8388608 | tf_op jit(solution)/shard_map/while
  311.9 7.3 %slice-start.1 = ((s8[13107200]{0:T(1024)(128)(4,1)}), s8[4194304]{0:T(1024)(128)(4,1)S(1)}, s32[]{:S(2)}) async-start(s8[13107200]{0:T(1024)(128)(4,1)} %bitcast.104), calls=%async_computation.6 | async-start | bytes 8388608 | tf_op jit(solution)/shard_map/while
  317.4 2.2 slice-start.2
  326.0 7.3 %slice-start = ((s8[13107200]{0:T(1024)(128)(4,1)}), s8[4194304]{0:T(1024)(128)(4,1)S(1)}, s32[]{:S(2)}) async-start(s8[13107200]{0:T(1024)(128)(4,1)} %bitcast.104), calls=%async_computation.5 | async-start | bytes 8388608 | tf_op jit(solution)/shard_map/while
  326.0 7.3 %slice-start.1 = ((s8[13107200]{0:T(1024)(128)(4,1)}), s8[4194304]{0:T(1024)(128)(4,1)S(1)}, s32[]{:S(2)}) async-start(s8[13107200]{0:T(1024)(128)(4,1)} %bitcast.104), calls=%async_computation.6 | async-start | bytes 8388608 | tf_op jit(solution)/shard_map/while
  331.5 2.2 slice-start.2
  332.6 1.3 slice-start.3
  340.0 7.3 %slice-start = ((s8[13107200]{0:T(1024)(128)(4,1)}), s8[4194304]{0:T(1024)(128)(4,1)S(1)}, s32[]{:S(2)}) async-start(s8[13107200]{0:T(1024)(128)(4,1)} %bitcast.104), calls=%async_computation.5 | async-start | bytes 8388608 | tf_op jit(solution)/shard_map/while
  340.0 7.3 %slice-start.1 = ((s8[13107200]{0:T(1024)(128)(4,1)}), s8[4194304]{0:T(1024)(128)(4,1)S(1)}, s32[]{:S(2)}) async-start(s8[13107200]{0:T(1024)(128)(4,1)} %bitcast.104), calls=%async_computation.6 | async-start | bytes 8388608 | tf_op jit(solution)/shard_map/while
  345.5 2.2 slice-start.2
  346.7 1.3 slice-start.3
  354.2 7.3 %slice-start = ((s8[13107200]{0:T(1024)(128)(4,1)}), s8[4194304]{0:T(1024)(128)(4,1)S(1)}, s32[]{:S(2)}) async-start(s8[13107200]{0:T(1024)(128)(4,1)} %bitcast.104), calls=%async_computation.5 | async-start | bytes 8388608 | tf_op jit(solution)/shard_map/while
  354.2 7.3 %slice-start.1 = ((s8[13107200]{0:T(1024)(128)(4,1)}), s8[4194304]{0:T(1024)(128)(4,1)S(1)}, s32[]{:S(2)}) async-start(s8[13107200]{0:T(1024)(128)(4,1)} %bitcast.104), calls=%async_computation.6 | async-start | bytes 8388608 | tf_op jit(solution)/shard_map/while
  359.7 2.2 slice-start.2
  368.3 7.3 %slice-start = ((s8[13107200]{0:T(1024)(128)(4,1)}), s8[4194304]{0:T(1024)(128)(4,1)S(1)}, s32[]{:S(2)}) async-start(s8[13107200]{0:T(1024)(128)(4,1)} %bitcast.104), calls=%async_computation.5 | async-start | bytes 8388608 | tf_op jit(solution)/shard_map/while
  368.3 7.3 %slice-start.1 = ((s8[13107200]{0:T(1024)(128)(4,1)}), s8[4194304]{0:T(1024)(128)(4,1)S(1)}, s32[]{:S(2)}) async-start(s8[13107200]{0:T(1024)(128)(4,1)} %bitcast.104), calls=%async_computation.6 | async-start | bytes 8388608 | tf_op jit(solution)/shard_map/while
  373.8 2.2 slice-start.2
  382.4 7.3 %slice-start = ((s8[13107200]{0:T(1024)(128)(4,1)}), s8[4194304]{0:T(1024)(128)(4,1)S(1)}, s32[]{:S(2)}) async-start(s8[13107200]{0:T(1024)(128)(4,1)} %bitcast.104), calls=%async_computation.5 | async-start | bytes 8388608 | tf_op jit(solution)/shard_map/while
  382.4 7.3 %slice-start.1 = ((s8[13107200]{0:T(1024)(128)(4,1)}), s8[4194304]{0:T(1024)(128)(4,1)S(1)}, s32[]{:S(2)}) async-start(s8[13107200]{0:T(1024)(128)(4,1)} %bitcast.104), calls=%async_computation.6 | async-start | bytes 8388608 | tf_op jit(solution)/shard_map/while
  387.9 2.2 slice-start.2
  396.4 7.3 %slice-start = ((s8[13107200]{0:T(1024)(128)(4,1)}), s8[4194304]{0:T(1024)(128)(4,1)S(1)}, s32[]{:S(2)}) async-start(s8[13107200]{0:T(1024)(128)(4,1)} %bitcast.104), calls=%async_computation.5 | async-start | bytes 8388608 | tf_op jit(solution)/shard_map/while
  396.4 7.3 %slice-start.1 = ((s8[13107200]{0:T(1024)(128)(4,1)}), s8[4194304]{0:T(1024)(128)(4,1)S(1)}, s32[]{:S(2)}) async-start(s8[13107200]{0:T(1024)(128)(4,1)} %bitcast.104), calls=%async_computation.6 | async-start | bytes 8388608 | tf_op jit(solution)/shard_map/while
  401.9 2.2 slice-start.2
  410.5 7.3 %slice-start = ((s8[13107200]{0:T(1024)(128)(4,1)}), s8[4194304]{0:T(1024)(128)(4,1)S(1)}, s32[]{:S(2)}) async-start(s8[13107200]{0:T(1024)(128)(4,1)} %bitcast.104), calls=%async_computation.5 | async-start | bytes 8388608 | tf_op jit(solution)/shard_map/while
  410.5 7.3 %slice-start.1 = ((s8[13107200]{0:T(1024)(128)(4,1)}), s8[4194304]{0:T(1024)(128)(4,1)S(1)}, s32[]{:S(2)}) async-start(s8[13107200]{0:T(1024)(128)(4,1)} %bitcast.104), calls=%async_computation.6 | async-start | bytes 8388608 | tf_op jit(solution)/shard_map/while
  416.0 2.2 slice-start.2
  424.6 7.3 %slice-start = ((s8[13107200]{0:T(1024)(128)(4,1)}), s8[4194304]{0:T(1024)(128)(4,1)S(1)}, s32[]{:S(2)}) async-start(s8[13107200]{0:T(1024)(128)(4,1)} %bitcast.104), calls=%async_computation.5 | async-start | bytes 8388608 | tf_op jit(solution)/shard_map/while
  424.6 7.3 %slice-start.1 = ((s8[13107200]{0:T(1024)(128)(4,1)}), s8[4194304]{0:T(1024)(128)(4,1)S(1)}, s32[]{:S(2)}) async-start(s8[13107200]{0:T(1024)(128)(4,1)} %bitcast.104), calls=%async_computation.6 | async-start | bytes 8388608 | tf_op jit(solution)/shard_map/while
  430.1 2.2 slice-start.2
  435.6 15.7 %copy-start = (bf16[16,128,32]{1,2,0:T(8,128)(2,1)}, bf16[16,128,32]{1,2,0:T(8,128)(2,1)S(1)}, u32[]{:S(2)}) copy-start(bf16[16,128,32]{1,2,0:T(8,128)(2,1)S(1)} %get-tuple-element.309) | copy-start | bytes 393220
  (10 other events, 13.4 us)
Sparse Core Ops, SparseCore 0:
  9.9 25.6 all-gather.14
  37.4 31.3 all-gather.8
  70.6 39.6 all-gather.10
  112.0 25.9 all-gather.6
  139.7 70.3 all-gather.12
where the time goes:
time: 459 us; the launch traced here: 458 us
  matrix products  206 us (45%)
  waiting for transfers between devices  141 us (31%)
  local copies, waits for them, and re-layouts  40 us (9%)
  other arithmetic  36.9 us (8%)
  blocking collectives  16.2 us (4%)
  between operations  15.9 us (3%)
    dot_general x16, matrix products, attend(): jnp.einsum('btr,rc->btc', q_lat, w_uq, preferred_element_type=jnp.float32)  74.5 us
    all_gather x1, waiting for transfers between devices, local_block(): w_out_all = lax.all_gather(w_out_s, 'fsdp', tiled=True)  72 us
    dot_general x16, matrix products, attend(): jnp.einsum('btc,cd->btd', attn_out, w_out, preferred_element_type=jnp.flo...  47.8 us
    dot_general x16, matrix products, attend(): jnp.einsum('btr,rc->btc', latent, w_ukv, preferred_element_type=jnp.float32)  36.7 us
    all_gather x1, waiting for transfers between devices, local_block(): w_uq_all = lax.all_gather(w_uq_s, 'fsdp', tiled=True)  26.8 us
    all_gather x1, waiting for transfers between devices, local_block(): w_dq_all = lax.all_gather(w_dq_s, 'fsdp', tiled=True)  19.4 us
    all_gather x1, waiting for transfers between devices, local_block(): w_ukv_all = lax.all_gather(w_ukv_s, 'fsdp', tiled=True)  19.2 us
    unnamed x1, blocking collectives  16.2 us
  transfers between devices with their start and end apart: 5, of which 4 were waited for; matrix products, arithmetic and copies ran while one was open for 10% of the time, Pallas kernels for 0%

commit v1 on v0

v1 whole, which is shorter than its diff:
```python
import functools
import jax, jax.numpy as jnp
from jax import lax
from jax.experimental import pallas as pl
from jax.experimental.pallas import tpu as pltpu
F32, BF16 = jnp.float32, jnp.bfloat16
EPS = 1e-6
T, D, QR, KR, RD, H, ND, VD = 2048, 2560, 768, 256, 32, 40, 64, 64
S = 128
LOG2E = 1.4426950408889634
SC = (ND + RD) ** -0.5 * LOG2E

def dot(a, b):
    return jnp.dot(a, b, preferred_element_type=F32)

def down_kernel(x_ref, g1_ref, wdq_ref, gq_ref, wkv_ref, gkv_ref, cos_ref, sin_ref, cqT_ref, c_ref, cT_ref, r_ref):
    x = x_ref[...].astype(F32)
    inv = lax.rsqrt(jnp.mean(x * x, axis=-1, keepdims=True) + EPS)
    a = (x * inv * g1_ref[...].astype(F32)).astype(BF16)
    qd = dot(a, wdq_ref[...])
    inv = lax.rsqrt(jnp.mean(qd * qd, axis=-1, keepdims=True) + EPS)
    cq = (qd * inv * gq_ref[...].astype(F32)).astype(BF16)
    cqT_ref[...] = cq.T
    kd = dot(a, wkv_ref[...])
    kc = kd[:, :KR]
    inv = lax.rsqrt(jnp.mean(kc * kc, axis=-1, keepdims=True) + EPS)
    c = (kc * inv * gkv_ref[...].astype(F32)).astype(BF16)
    c_ref[...] = c
    cT_ref[...] = c.T
    kp = kd[:, KR:]
    lo, hi = kp[:, :16], kp[:, 16:]
    co, si = cos_ref[...], sin_ref[...]
    r_ref[...] = jnp.concatenate([lo * co - hi * si, hi * co + lo * si], axis=-1).astype(BF16)

def down(x, g1, wdq, gq, wkv, gkv, cos, sin, tm=256):
    full = lambda shape: pl.BlockSpec(shape, lambda i: (0, 0))
    cos = jnp.tile(cos, (tm // S, 1)); sin = jnp.tile(sin, (tm // S, 1))
    return pl.pallas_call(
        down_kernel, grid=(T // tm,), name="down", cost_estimate=pl.CostEstimate(flops=2 * T * D * 1056, bytes_accessed=20 << 20, transcendentals=0),
        in_specs=[pl.BlockSpec((tm, D), lambda i: (i, 0)), full((1, D)), full((D, QR)), full((1, QR)), full((D, KR + RD)), full((1, KR)), full((tm, 16)), full((tm, 16))],
        out_specs=[pl.BlockSpec((QR, tm), lambda i: (0, i)), pl.BlockSpec((tm, KR), lambda i: (i, 0)), pl.BlockSpec((KR, tm), lambda i: (0, i)), pl.BlockSpec((tm, RD), lambda i: (i, 0))],
        out_shape=[jax.ShapeDtypeStruct((QR, T), BF16), jax.ShapeDtypeStruct((T, KR), BF16), jax.ShapeDtypeStruct((KR, T), BF16), jax.ShapeDtypeStruct((T, RD), BF16)],
        compiler_params=pltpu.CompilerParams(vmem_limit_bytes=60 << 20),
    )(x, g1, wdq, gq, wkv, gkv, cos, sin)

HG = 8
TC = 512
def attn_unit(k, qT, vT, keep):
    s = dot(k, qT) * SC
    s = jnp.where(keep, s, -1e30)
    m = jnp.max(s, axis=0, keepdims=True)
    e = jnp.exp2(s - m)
    p = (e * (1.0 / jnp.sum(e, axis=0, keepdims=True))).astype(BF16)
    return dot(vT, p)

def attn_kernel(cqT_ref, c_ref, cT_ref, r_ref, wuq_ref, wukv_ref, cosT_ref, sinT_ref, o_ref, wqT, wk, wvT, qT, kbuf, vT):
    g = pl.program_id(0)
    wqT[...] = wuq_ref[...].T
    for j in range(HG // 2):
        t0 = wukv_ref[:, 256 * j:256 * j + 128]
        t1 = wukv_ref[:, 256 * j + 128:256 * j + 256]
        wk[:, 128 * j:128 * j + 128] = jnp.concatenate([t0[:, :64], t1[:, :64]], axis=1)
        wvT[128 * j:128 * j + 128, :] = jnp.concatenate([t0[:, 64:], t1[:, 64:]], axis=1).T
    for h in range(HG):
        z = 128 * h + (96 if h % 2 == 0 else 32)
        qT[z:z + 32, :] = jnp.zeros((32, TC), BF16)
    keep = lax.broadcasted_iota(jnp.int32, (S, S), 0) <= lax.broadcasted_iota(jnp.int32, (S, S), 1)
    lane = lax.broadcasted_iota(jnp.int32, (S, 128), 1)
    co, si = cosT_ref[...], sinT_ref[...]

    def chunk(tc, _):
        tok = pl.multiple_of(tc * TC, TC)
        for n in range(TC // 256):
            q = dot(wqT[...], cqT_ref[:, pl.ds(tok + 256 * n, 256)])
            cols = slice(256 * n, 256 * n + 256)
            for h in range(HG):
                nope = q[96 * h:96 * h + 64]
                lo, hi = q[96 * h + 64:96 * h + 80], q[96 * h + 80:96 * h + 96]
                b = 128 * h
                qn, qp = (b, b + 64) if h % 2 == 0 else (b + 64, b)
                qT[qn:qn + 64, cols] = nope.astype(BF16)
                qT[qp:qp + 16, cols] = (lo * co - hi * si).astype(BF16)
                qT[qp + 16:qp + 32, cols] = (hi * co + lo * si).astype(BF16)
        kbuf[...] = dot(c_ref[pl.ds(tok, TC), :], wk[...]).astype(BF16)
        vT[...] = dot(wvT[...], cT_ref[:, pl.ds(tok, TC)]).astype(BF16)

        for p in range(TC // S):
            row = p * S
            r = r_ref[pl.ds(tok + row, S), :]
            z32 = jnp.zeros((S, 32), BF16)
            z64 = jnp.zeros((S, 64), BF16)
            r_hi = jnp.concatenate([z64, r, z32], axis=1)
            r_lo = jnp.concatenate([r, z32, z64], axis=1)
            for j in range(HG // 2):
                k2 = kbuf[row:row + S, 128 * j:128 * j + 128]
                outs = []
                for par in range(2):
                    h = 2 * j + par
                    k = jnp.where(lane < 64, k2, r_hi) if par == 0 else jnp.where(lane < 64, r_lo, k2)
                    outs.append(attn_unit(k, qT[128 * h:128 * h + 128, row:row + S], vT[64 * h:64 * h + 64, row:row + S], keep))
                oT = jnp.concatenate(outs, axis=0)
                o_ref[pl.ds(tok + row, S), 128 * j:128 * j + 128] = oT.astype(BF16).T
        return 0
    lax.fori_loop(0, T // TC, chunk, 0)

def attn(cqT, c, cT, r, wuq, wukv, cosT, sinT):
    full = lambda shape: pl.BlockSpec(shape, lambda g: (0, 0))
    return pl.pallas_call(
        attn_kernel, grid=(H // HG,), name="attn", cost_estimate=pl.CostEstimate(flops=40 * 10**9, bytes_accessed=24 << 20, transcendentals=0),
        in_specs=[full((QR, T)), full((T, KR)), full((KR, T)), full((T, RD)),
                  pl.BlockSpec((QR, HG * 96), lambda g: (0, g)), pl.BlockSpec((KR, HG * 128), lambda g: (0, g)), full((16, 256)), full((16, 256))],
        out_specs=pl.BlockSpec((T, HG * 64), lambda g: (0, g)),
        out_shape=jax.ShapeDtypeStruct((T, H * VD), BF16),
        scratch_shapes=[pltpu.VMEM((HG * 96, QR), BF16), pltpu.VMEM((KR, HG * 64), BF16), pltpu.VMEM((HG * 64, KR), BF16),
                        pltpu.VMEM((HG * 128, TC), BF16), pltpu.VMEM((TC, HG * 64), BF16), pltpu.VMEM((HG * 64, TC), BF16)],
        compiler_params=pltpu.CompilerParams(vmem_limit_bytes=60 << 20),
    )(cqT, c, cT, r, wuq, wukv, cosT, sinT)

def out_kernel(o_ref, w_ref, x_ref, y_ref):
    y_ref[...] = (x_ref[...].astype(F32) + dot(o_ref[...], w_ref[...])).astype(BF16)

def outp(o, w, x, tm=512, tn=512):
    return pl.pallas_call(
        out_kernel, grid=(T // tm, D // tn), name="outp", cost_estimate=pl.CostEstimate(flops=2 * T * D * D, bytes_accessed=40 << 20, transcendentals=0),
        in_specs=[pl.BlockSpec((tm, D), lambda i, j: (i, 0)), pl.BlockSpec((D, tn), lambda i, j: (0, j)), pl.BlockSpec((tm, tn), lambda i, j: (i, j))],
        out_specs=pl.BlockSpec((tm, tn), lambda i, j: (i, j)),
        out_shape=jax.ShapeDtypeStruct((T, D), BF16),
        compiler_params=pltpu.CompilerParams(vmem_limit_bytes=60 << 20),
    )(o, w, x)

def tables():
    half = RD // 2
    inv_freq = 10000.0 ** (-2.0 * jnp.arange(half, dtype=F32) / RD)
    ang = jnp.arange(S, dtype=F32)[:, None] * inv_freq[None, :]
    return jnp.cos(ang), jnp.sin(ang)


def solution(mesh):
    from jax.sharding import PartitionSpec as P
    batch, row, mat = P(('dp', 'fsdp')), P('fsdp'), P('fsdp', None)

    def local(tok, g1, wdq, gq, wuq, wkv, gkv, wukv, wo):
        cos, sin = tables()
        gains = lax.all_gather(jnp.concatenate([g1, gq, gkv]), 'fsdp')
        g1a, gqa, gkva = (gains[:, :320].reshape(1, D), gains[:, 320:416].reshape(1, QR), gains[:, 416:].reshape(1, KR))
        ag = lambda w: lax.all_gather(w, 'fsdp', tiled=True)
        x = tok.reshape(T, D)
        cqT, c, cT, r = down(x, g1a, ag(wdq), gqa, ag(wkv), gkva, cos, sin)
        o = attn(cqT, c, cT, r, ag(wuq), ag(wukv), jnp.tile(cos.T, (1, 2)), jnp.tile(sin.T, (1, 2)))
        y = outp(o, ag(wo), x)
        return y.reshape(tok.shape), c.reshape(-1, S, KR), r.reshape(-1, S, RD)

    return jax.shard_map(local, mesh=mesh, in_specs=(batch, row, mat, row, mat, mat, row, mat, mat),
                         out_specs=(batch,) * 3, check_vma=False)
```

time: 459 us -> 258 us (0.56)
  matrix products: 206 us -> 0 us
  Pallas kernels: 0 us -> 111 us
  waiting for transfers between devices: 141 us -> 103 us
  other arithmetic: 36.9 us -> 1.18 us
  local copies, waits for them, and re-layouts: 40 us -> 11.4 us
    dot_general x98 -> x0, matrix products: 206 us -> none  [the longest x16 74.5 us: attend(): jnp.einsum('btr,rc->btc', q_lat, w_uq, preferred_element_type=jnp.float32)]
    pallas_call x0 -> x3, Pallas kernels: none -> 111 us  [the longest x1 47.8 us: attn(): pl.pallas_call(attn_kernel, grid=(H // HG,), name='attn', cost_estimate=p...]
    all_gather x5, waiting for transfers between devices: 138 us -> 100 us  [local(): ag = lambda w: lax.all_gather(w, 'fsdp', tiled=True)]
    convert_element_type x6 -> x0, other arithmetic: 18.2 us -> none  [the longest x1 15.7 us: local_block(): y_blk = (tok_blk.astype(jnp.float32) + proj_out).astype(jnp.bfloat16)]
    reduce_sum x18 -> x0, other arithmetic: 14.8 us -> none  [the longest x16 8.58 us: attend(): attn_probs = jax.nn.softmax(scores, axis=-1).astype(jnp.bfloat16)]
    while x128 -> x0, local copies, waits for them, and re-layouts: 12 us -> none
    reshape x16 -> x3, local copies, waits for them, and re-layouts: 12.5 us -> 1.98 us  [the longest x1 0.68 us: local(): gains[:, 320:416].reshape(1, QR)]
    unnamed x20 -> x4, local copies, waits for them, and re-layouts: 13.4 us -> 3.34 us
  transfers between devices with their start and end apart: 5 -> 5, of which waited for: 4 -> 5; matrix products, arithmetic and copies ran while one was open for 10% -> 5% of each run, Pallas kernels for 0% -> 27%
where the time goes in v1:
time: 258 us; the launch traced here: 257 us
  Pallas kernels  111 us (43%)
  waiting for transfers between devices  103 us (40%)
  blocking collectives  15.9 us (6%)
  between operations  14.5 us (6%)
  local copies, waits for them, and re-layouts  11.4 us (4%)
    all_gather x5, waiting for transfers between devices, local(): ag = lambda w: lax.all_gather(w, 'fsdp', tiled=True)  100 us
    pallas_call x1, Pallas kernels, attn(): pl.pallas_call(attn_kernel, grid=(H // HG,), name='attn', cost_estimate=p...  47.8 us
    pallas_call x1, Pallas kernels, outp(): pl.pallas_call(out_kernel, grid=(T // tm, D // tn), name='outp', cost_est...  41 us
    pallas_call x1, Pallas kernels, down(): pl.pallas_call(down_kernel, grid=(T // tm,), name='down', cost_estimate=p...  22.1 us
    unnamed x1, blocking collectives  15.9 us
  transfers between devices with their start and end apart: 5, of which 5 were waited for; matrix products, arithmetic and copies ran while one was open for 5% of the time, Pallas kernels for 27%

profile of v1, /device:TPU:0, one launch (start us, length us, event | category | flops | bytes accessed | tf_op | source)
XLA Modules:
  0.0 257.3 jit_solution(18163030592585254562)
XLA Ops:
  7.2 0.0 all-gather.16.cloned.1.call-start
  7.2 0.7 all-gather.16.cloned.1.call-update
  7.9 0.0 all-gather.8.cloned.1.call-start
  7.9 0.7 all-gather.8.cloned.1.call-update
  8.6 0.0 all-gather.12.cloned.1.call-start
  8.7 0.7 all-gather.12.cloned.1.call-update
  9.4 0.0 all-gather.10.cloned.1.call-start
  9.4 0.5 all-gather.10.cloned.1.call-update
  10.0 0.0 all-gather.14.cloned.1.call-start
  10.0 0.5 all-gather.14.cloned.1.call-update
  10.5 1.2 dynamic-slice
  12.4 0.8 pad_maximum_fusion
  13.2 0.2 dynamic-update-slice
  13.5 15.9 %all-reduce = bf16[3584]{0:T(1024)(128)(2,1)S(1)} all-reduce(bf16[3584]{0:T(1024)(128)(2,1)S(1)} %dynamic-update-slice), channel_id=2, replica_groups=mesh['dp'=2,'fsdp'=8] {'fsdp'}, use_global_device_ids=true, to_apply=%add | all-reduce | flops 3584 | bytes 14336
  29.4 0.1 reshape.127
  29.5 0.1 slice.13
  29.5 0.1 slice.14
  29.6 0.7 reshape.121.g1_ref
  30.3 0.7 reshape.122.gq_ref
  31.0 0.6 reshape.123.gkv_ref
  31.6 0.1 fusion.2
  31.8 0.6 copy_bitcast_fusion
  32.4 0.3 fusion
  32.6 2.6 %all-gather.16.cloned.1.call-done = bf16[8,320,288]{1,2,0:T(8,128)(2,1)} async-done(((bf16[1,320,288]{1,2,0:T(8,128)(2,1)}), bf16[8,320,288]{1,2,0:T(8,128)(2,1)}) %all-gather.16.cloned.1.call-update) | async-done | bytes 1474576 | tf_op jit(solution)/shard_map/all_gather | solution.py:146
  35.2 3.9 %copy.14 = bf16[8,320,288]{2,1,0:T(8,128)(2,1)} copy(bf16[8,320,288]{1,2,0:T(8,128)(2,1)} %all-gather.16.cloned.1.call-done) | data formatting | bytes 2949120 | tf_op jit(solution)/shard_map/all_gather | solution.py:146
  39.1 29.3 %all-gather.8.cloned.1.call-done.wdq_ref = bf16[2560,768]{1,0:T(8,128)(2,1)} async-done(((bf16[320,768]{1,0:T(8,128)(2,1)}), bf16[2560,768]{1,0:T(8,128)(2,1)}) %all-gather.8.cloned.1.call-update) | async-done | bytes 3932176 | tf_op jit(solution)/shard_map/all_gather | solution.py:146
  68.5 0.7 tile.16
  69.1 0.7 tile.18
  69.8 22.1 %down.1 = (bf16[768,2048]{1,0:T(8,128)(2,1)}, bf16[2048,256]{1,0:T(8,128)(2,1)}, bf16[256,2048]{1,0:T(8,128)(2,1)}, bf16[2048,32]{1,0:T(8,128)(2,1)}) custom-call(bf16[2048,2560]{1,0:T(8,128)(2,1)} %bitcast.22, bf16[1,2560]{1,0:T(2,128)(2,1)} %reshape.121.g1_ref, bf16[2560,768]{1,0:T(8,128)(2,1)} %all-gather.8.cloned.1.call-done.wdq_ref, ...), custom_call_target="tpu_custom_call" | custom-call | flops 11072962560 | bytes 20971520 | tf_op jit(solution)/shard_map/down/pallas_call | solution.py:38
  91.9 1.9 copy.15
  93.8 2.5 all-gather.12.cloned.1.call-done.wukv_ref
  96.3 41.4 %all-gather.10.cloned.1.call-done.wuq_ref = bf16[768,3840]{1,0:T(8,128)(2,1)} async-done(((bf16[96,3840]{1,0:T(8,128)(2,1)}), bf16[768,3840]{1,0:T(8,128)(2,1)}) %all-gather.10.cloned.1.call-update) | async-done | bytes 5898256 | tf_op jit(solution)/shard_map/all_gather | solution.py:146
  137.7 47.8 %attn.1.o_ref = bf16[2048,2560]{1,0:T(8,128)(2,1)} custom-call(bf16[768,2048]{1,0:T(8,128)(2,1)} %get-tuple-element.7.cqT_ref, bf16[2048,256]{1,0:T(8,128)(2,1)} %get-tuple-element.8.c_ref, bf16[256,2048]{1,0:T(8,128)(2,1)} %get-tuple-element.9.cT_ref, bf16[2048,32]{1,0:T(8,128)(2,1)} %get-tuple-element.10.r_ref, ...), custom_call_target="tpu_custom_call" | custom-call | flops 40000000000 | bytes 25165824 | tf_op jit(solution)/shard_map/attn/pallas_call | solution.py:108
  185.5 24.2 %all-gather.14.cloned.1.call-done.w_ref = bf16[2560,2560]{1,0:T(8,128)(2,1)} async-done(((bf16[320,2560]{1,0:T(8,128)(2,1)}), bf16[2560,2560]{1,0:T(8,128)(2,1)}) %all-gather.14.cloned.1.call-update) | async-done | bytes 13107216 | tf_op jit(solution)/shard_map/all_gather | solution.py:146
  209.8 41.0 %outp.1 = bf16[2048,2560]{1,0:T(8,128)(2,1)} custom-call(bf16[2048,2560]{1,0:T(8,128)(2,1)} %attn.1.o_ref, bf16[2560,2560]{1,0:T(8,128)(2,1)} %all-gather.14.cloned.1.call-done.w_ref, bf16[2048,2560]{1,0:T(8,128)(2,1)} %bitcast.23), custom_call_target="tpu_custom_call" | custom-call | flops 26843545600 | bytes 41943040 | tf_op jit(solution)/shard_map/outp/pallas_call | solution.py:123
  (5 shorter events, 0.0 us)
Async XLA Ops:
  7.2 28.1 %all-gather.16.cloned.1.call-start = ((), (), s32[]{:S(2)}) async-start(), calls=%async_computation.4 | async-start | bytes 1990656 | tf_op jit(solution)/shard_map/all_gather | solution.py:146
  7.9 60.6 %all-gather.8.cloned.1.call-start = ((), (), s32[]{:S(2)}) async-start(), calls=%async_computation | async-start | bytes 4423680 | tf_op jit(solution)/shard_map/all_gather | solution.py:146
  8.6 87.7 %all-gather.12.cloned.1.call-start = ((), (), s32[]{:S(2)}) async-start(), calls=%async_computation.2 | async-start | bytes 2949120 | tf_op jit(solution)/shard_map/all_gather | solution.py:146
  9.4 128.3 %all-gather.10.cloned.1.call-start = ((), (), s32[]{:S(2)}) async-start(), calls=%async_computation.1 | async-start | bytes 6635520 | tf_op jit(solution)/shard_map/all_gather | solution.py:146
  10.0 199.8 %all-gather.14.cloned.1.call-start = ((), (), s32[]{:S(2)}) async-start(), calls=%async_computation.3 | async-start | bytes 14745600 | tf_op jit(solution)/shard_map/all_gather | solution.py:146
Sparse Core Ops, SparseCore 0:
  9.8 25.3 all-gather.15
  37.1 31.3 all-gather.7
  70.3 25.9 all-gather.11
  98.0 39.6 all-gather.9
  139.4 70.3 all-gather.13

commit v2 on v1

v2 whole, which is shorter than its diff:
```python
import functools
import numpy as np
import jax
import jax.numpy as jnp
from jax import lax
from jax.experimental import pallas as pl
from jax.experimental.pallas import tpu as pltpu
from jax.sharding import PartitionSpec as P

F32, BF16 = jnp.float32, jnp.bfloat16
MESH = pl.DeviceIdType.MESH
EPS = 1e-6
T, D, QR, KR, RD, H, ND, VD = 2048, 2560, 768, 256, 32, 40, 64, 64
S = 128
SC = (ND + RD) ** -0.5 * 1.4426950408889634
HG, TC = 8, 512
NCH = T // TC
STEPS = (H // HG) * NCH
TA = 256


def dot(a, b):
    return jnp.dot(a, b, preferred_element_type=F32)


def rms(v):
    return lax.rsqrt(jnp.mean(v * v, axis=-1, keepdims=True) + EPS)


def attn_unit(k, qT, vT, keep):
    s = dot(k, qT) * SC
    s = jnp.where(keep, s, -1e30)
    m = jnp.max(s, axis=0, keepdims=True)
    e = jnp.exp2(s - m)
    p = (e * (1.0 / jnp.sum(e, axis=0, keepdims=True))).astype(BF16)
    return dot(vT, p)


PIECES = (
    ('dq', 'dq', False, 320, 0, 768, 96),
    ('dkv', 'dkv', False, 320, 0, 288, 96),
    ('uq0', 'uq', False, 96, 0, 768, 32),
    ('ukv0', 'ukv', True, 32, 0, 1024, 384),
    ('uq1', 'uq', False, 96, 768, 1536, 32),
    ('ukv1', 'ukv', True, 32, 1024, 2048, 640),
    ('uq2', 'uq', False, 96, 2304, 1536, 32),
    ('ukv2', 'ukv', True, 32, 3072, 2048, 640),
    ('o', 'o', False, 320, 0, 2560, 112),
)
PIDX = {p[0]: i for i, p in enumerate(PIECES)}
KINDS = ('XE', 'YE', 'XS', 'YS', 'S0', 'Z1', 'Z2', 'DY', 'DX', 'Z3', 'S1', 'S2', 'S3')
KIDX = {k: i for i, k in enumerate(KINDS)}
D0, U0, U1, U2, O0 = ('dq', 'dkv'), ('uq0', 'ukv0'), ('uq1', 'ukv1'), ('uq2', 'ukv2'), ('o',)


def front_kernel(x_hbm, g1_s, gq_s, gkv_s, dq_s, dkv_s, uq_s, ukv_s, o_s, cos_ref, sin_ref, cosT_ref, sinT_ref,
                 attn_hbm, wo_hbm, c_hbm, r_hbm,
                 xa, wdq, wdkv, wuq, wukv, ostage, g1b, gqb, gkvb, accq, acck, cqT, cbuf, cT, rbuf,
                 wqT, wk, wvT, qT, kbuf, vT, obuf,
                 ssem, rsem, lsem, gss, grs, xsem, osem, csem):
    z, f = lax.axis_index('dp'), lax.axis_index('fsdp')
    core, xx, yy = f % 2, (f // 2) % 2, f // 4

    def idx(dx, dy, dc):
        return ((yy + dy) % 2) * 4 + ((xx + dx) % 2) * 2 + (core + dc) % 2

    fx, fy, fd = idx(1, 0, 0), idx(0, 1, 0), idx(1, 1, 0)
    dev = {'X': (z, fx), 'Y': (z, fy), 'Z': (1 - z, f), 'S': (z, idx(0, 0, 1))}
    plane = [idx(dx, dy, dc) for dx in range(2) for dy in range(2) for dc in range(2) if dx + dy + dc]
    src = {'dq': dq_s, 'dkv': dkv_s, 'uq': uq_s, 'ukv': ukv_s, 'o': ostage}
    buf = {'dq': wdq, 'dkv': wdkv, 'uq': wuq, 'ukv': wukv, 'o': wo_hbm}

    def region(piece, shard, part, base):
        name, arr, bycol, rows, c0, nc, e = piece
        n = nc if bycol else rows
        off, size = {'E': (z * (n - e), e), 'S': (e, n - 2 * e), 'A': (0, n)}[part]
        if bycol:
            row = shard * rows if base else 0
            return pl.ds(pl.multiple_of(row, 16), rows), pl.ds(pl.multiple_of(c0 + off, 128), size)
        row = (shard * rows if base else 0) + off
        return pl.ds(pl.multiple_of(row, 16), size), pl.ds(c0, nc)

    def copy(name, kind):
        piece = PIECES[PIDX[name]]
        arr = piece[1]
        shard = {'X': f, 'Y': f}.get(kind[0]) if kind in ('XE', 'YE', 'XS', 'YS') else None
        if kind in ('XE', 'YE', 'XS', 'YS', 'S0'):
            part = 'A' if kind == 'S0' else kind[1]
            r0, c0 = region(piece, f, part, False)
            r1, c1 = region(piece, f, part, True)
            s_ref, d_ref = src[arr].at[r0, c0], buf[arr].at[r1, c1]
            to = dev[kind[0]]
        else:
            shard, part, to = {'Z1': (fx, 'E', 'Z'), 'Z2': (fy, 'E', 'Z'), 'Z3': (fd, 'E', 'Z'), 'DY': (fx, 'E', 'Y'),
                               'DX': (fy, 'S', 'X'), 'S1': (fx, 'A', 'S'), 'S2': (fy, 'A', 'S'), 'S3': (fd, 'A', 'S')}[kind]
            to = dev[to]
            r1, c1 = region(piece, shard, part, True)
            s_ref = d_ref = buf[arr].at[r1, c1]
        i, j = PIDX[name], KIDX[kind]
        return pltpu.make_async_remote_copy(src_ref=s_ref, dst_ref=d_ref, send_sem=ssem.at[i, j], recv_sem=rsem.at[i, j],
                                            device_id=to, device_id_type=MESH)

    def local(name):
        piece = PIECES[PIDX[name]]
        r0, c0 = region(piece, f, 'A', False)
        r1, c1 = region(piece, f, 'A', True)
        return pltpu.make_async_copy(src[piece[1]].at[r0, c0], buf[piece[1]].at[r1, c1], lsem.at[PIDX[name]])

    def start(names, *kinds):
        for k in kinds:
            for n in names:
                copy(n, k).start()

    def recv(names, *kinds):
        for k in kinds:
            for n in names:
                copy(n, k).wait_recv()

    def st0(names):
        start(names, 'XE', 'YE', 'XS', 'YS', 'S0')
        for n in names:
            local(n).start()

    def st1(names):
        recv(names, 'XE', 'YE')
        start(names, 'Z1', 'Z2', 'DY')

    def st2(names):
        recv(names, 'XS', 'YS')
        start(names, 'DX')

    def st3(names):
        recv(names, 'DY')
        start(names, 'Z3')

    def st4(names):
        recv(names, 'Z1')
        start(names, 'S1')
        recv(names, 'Z2')
        start(names, 'S2')

    def st5(names):
        recv(names, 'DX', 'Z3')
        start(names, 'S3')

    def stage(names):
        stage_o.wait()

    def fin(names):
        for n in names:
            local(n).wait()
        recv(names, 'S0', 'S1', 'S2', 'S3')

    for i in range(T // TA):
        pltpu.make_async_copy(x_hbm.at[pl.ds(i * TA, TA)], xa.at[pl.ds(i * TA, TA)], xsem.at[i]).start()
    stage_o = pltpu.make_async_copy(o_s, ostage, osem.at[2])
    stage_o.start()

    barrier = pltpu.get_barrier_semaphore()
    for p in plane:
        pl.semaphore_signal(barrier, inc=1, device_id=(z, p), device_id_type=MESH)
    pl.semaphore_signal(barrier, inc=1, device_id=dev['Z'], device_id_type=MESH)
    pl.semaphore_wait(barrier, 8)

    gains = []
    for j, (gs, gb) in enumerate(((g1_s, g1b), (gq_s, gqb), (gkv_s, gkvb))):
        for i, p in enumerate(plane):
            gains.append(pltpu.make_async_remote_copy(src_ref=gs, dst_ref=gb.at[f], send_sem=gss.at[j, i], recv_sem=grs.at[j, i],
                                                      device_id=(z, p), device_id_type=MESH))
            gains[-1].start()
        own = pltpu.make_async_copy(gs, gb.at[f], gss.at[j, 7])
        own.start()
        gains.append(own)
    st0(D0)
    for g in gains:
        g.wait()

    def row_of(gb):
        return jnp.concatenate([gb[i].astype(F32) for i in range(8)], axis=-1)

    g1, gq, gkv = row_of(g1b), row_of(gqb), row_of(gkvb)

    def norm_tile(i, _):
        pltpu.make_async_copy(x_hbm.at[pl.ds(i * TA, TA)], xa.at[pl.ds(i * TA, TA)], xsem.at[i]).wait()
        for h in range(TA // 64):
            rows = pl.ds(pl.multiple_of(i * TA + h * 64, 64), 64)
            v = xa[rows, :].astype(F32)
            xa[rows, :] = (v * rms(v) * g1).astype(BF16)
        return 0

    def part(quarter, first):
        cols = pl.ds(pl.multiple_of(quarter * 640, 128), 640)

        def tile(i, _):
            rows = pl.ds(pl.multiple_of(i * TA, TA), TA)
            a = xa[rows, cols]
            pq, pk = dot(a, wdq[cols, :]), dot(a, wdkv[cols, :])
            if first:
                accq[rows, :], acck[rows, :] = pq, pk
            else:
                accq[rows, :] += pq
                acck[rows, :] += pk
            return 0
        lax.fori_loop(0, T // TA, tile, 0)

    cos2 = jnp.concatenate([cos_ref[...]] * (TA // S), axis=0)
    sin2 = jnp.concatenate([sin_ref[...]] * (TA // S), axis=0)

    def last_part(quarter):
        cols = pl.ds(pl.multiple_of(quarter * 640, 128), 640)

        def tile(i, _):
            rows = pl.ds(pl.multiple_of(i * TA, TA), TA)
            a = xa[rows, cols]
            qd = accq[rows, :] + dot(a, wdq[cols, :])
            kd = acck[rows, :] + dot(a, wdkv[cols, :])
            cqT[:, rows] = (qd * rms(qd) * gq).astype(BF16).T
            kc = kd[:, :KR]
            c = (kc * rms(kc) * gkv).astype(BF16)
            cbuf[rows, :] = c
            cT[:, rows] = c.T
            lo, hi = kd[:, KR:KR + 16], kd[:, KR + 16:]
            rbuf[rows, :] = jnp.concatenate([lo * cos2 - hi * sin2, hi * cos2 + lo * sin2], axis=-1).astype(BF16)
            return 0
        lax.fori_loop(0, T // TA, tile, 0)

    lax.fori_loop(0, 4, norm_tile, 0)
    st1(D0)
    lax.fori_loop(4, 8, norm_tile, 0)
    for n in D0:
        local(n).wait()
    recv(D0, 'S0')
    part(f // 2, True)
    st2(D0)
    st0(U0)
    st3(D0)
    st4(D0)
    recv(D0, 'S1')
    part(fx // 2, False)
    st5(D0)
    st1(U0)
    recv(D0, 'S2')
    part(fy // 2, False)
    st2(U0)
    st0(U1)
    st3(U0)
    recv(D0, 'S3')
    last_part(fd // 2)
    outs = [pltpu.make_async_copy(cbuf, c_hbm, csem.at[0]), pltpu.make_async_copy(rbuf, r_hbm, csem.at[1])]
    for o in outs:
        o.start()
    st4(U0)
    st5(U0)
    fin(U0)

    keep = lax.broadcasted_iota(jnp.int32, (S, S), 0) <= lax.broadcasted_iota(jnp.int32, (S, S), 1)
    lane = lax.broadcasted_iota(jnp.int32, (S, 128), 1)
    co, si = cosT_ref[...], sinT_ref[...]
    for h in range(HG):
        zr = 128 * h + (96 if h % 2 == 0 else 32)
        qT[zr:zr + 32, :] = jnp.zeros((32, TC), BF16)

    def load_group(g):
        uc = pl.ds(pl.multiple_of(g * (HG * 96), 128), HG * 96)
        wqT[...] = wuq[:, uc].T
        for j in range(HG // 2):
            t0 = wukv[:, pl.ds(pl.multiple_of(g * (HG * 128) + 256 * j, 128), 128)]
            t1 = wukv[:, pl.ds(pl.multiple_of(g * (HG * 128) + 256 * j + 128, 128), 128)]
            wk[:, 128 * j:128 * j + 128] = jnp.concatenate([t0[:, :64], t1[:, :64]], axis=1)
            wvT[128 * j:128 * j + 128, :] = jnp.concatenate([t0[:, 64:], t1[:, 64:]], axis=1).T

    def out_copy(i):
        g, tc = i // NCH, i % NCH
        return pltpu.make_async_copy(obuf.at[i % 2], attn_hbm.at[pl.ds(pl.multiple_of(tc * TC, TC), TC), pl.ds(pl.multiple_of(g * (HG * 64), 128), HG * 64)], osem.at[i % 2])

    sched = {
        0: ((st1, U1),),
        1: ((st2, U1), (st0, U2), (st3, U1)),
        2: ((st4, U1), (st5, U1), (st1, U2)),
        3: ((st2, U2), (stage, O0), (st0, O0), (st3, U2)),
        4: ((fin, U1), (st4, U2), (st5, U2)),
        6: ((fin, U2),),
        7: ((st1, O0),),
        10: ((st2, O0), (st3, O0)),
        13: ((st4, O0),),
        15: ((st5, O0),),
    }

    def act(todo):
        for fn, names in todo:
            fn(names)

    def step(i, _):
        g, tc = i // NCH, i % NCH
        tok = pl.multiple_of(tc * TC, TC)
        for s, todo in sched.items():
            pl.when(i == s)(functools.partial(act, todo))

        @pl.when(tc == 0)
        def _():
            load_group(g)

        @pl.when(i >= 2)
        def _():
            out_copy(i - 2).wait()

        slot = i % 2
        for n in range(TC // 256):
            q = dot(wqT[...], cqT[:, pl.ds(tok + 256 * n, 256)])
            cols = slice(256 * n, 256 * n + 256)
            for h in range(HG):
                nope = q[96 * h:96 * h + 64]
                lo, hi = q[96 * h + 64:96 * h + 80], q[96 * h + 80:96 * h + 96]
                b = 128 * h
                qn, qp = (b, b + 64) if h % 2 == 0 else (b + 64, b)
                qT[qn:qn + 64, cols] = nope.astype(BF16)
                qT[qp:qp + 16, cols] = (lo * co - hi * si).astype(BF16)
                qT[qp + 16:qp + 32, cols] = (hi * co + lo * si).astype(BF16)
        kbuf[...] = dot(cbuf[pl.ds(tok, TC), :], wk[...]).astype(BF16)
        vT[...] = dot(wvT[...], cT[:, pl.ds(tok, TC)]).astype(BF16)

        for p in range(TC // S):
            row = p * S
            r = rbuf[pl.ds(tok + row, S), :]
            z32, z64 = jnp.zeros((S, 32), BF16), jnp.zeros((S, 64), BF16)
            r_hi = jnp.concatenate([z64, r, z32], axis=1)
            r_lo = jnp.concatenate([r, z32, z64], axis=1)
            for j in range(HG // 2):
                k2 = kbuf[row:row + S, 128 * j:128 * j + 128]
                both = []
                for par in range(2):
                    h = 2 * j + par
                    k = jnp.where(lane < 64, k2, r_hi) if par == 0 else jnp.where(lane < 64, r_lo, k2)
                    both.append(attn_unit(k, qT[128 * h:128 * h + 128, row:row + S], vT[64 * h:64 * h + 64, row:row + S], keep))
                obuf[slot, row:row + S, 128 * j:128 * j + 128] = jnp.concatenate(both, axis=0).astype(BF16).T
        out_copy(i).start()
        return 0

    lax.fori_loop(0, STEPS, step, 0)
    fin(O0)
    for i in (STEPS - 2, STEPS - 1):
        out_copy(i).wait()
    for o in outs:
        o.wait()
    for p in PIECES:
        for k in KINDS:
            copy(p[0], k).wait_send()


def front(x, gains, ws, cos, sin):
    anyspace, vm = pl.BlockSpec(memory_space=pl.ANY), pl.BlockSpec(memory_space=pltpu.VMEM)
    V = pltpu.VMEM
    dma = pltpu.SemaphoreType.DMA
    tab = [cos, sin, np.tile(cos.T, (1, 2)), np.tile(sin.T, (1, 2))]
    return pl.pallas_call(
        front_kernel, name='front',
        in_specs=[anyspace] + [vm] * 3 + [anyspace] * 5 + [vm] * 4,
        out_specs=[anyspace] * 4,
        out_shape=[jax.ShapeDtypeStruct((T, H * VD), BF16), jax.ShapeDtypeStruct((H * VD, D), BF16), jax.ShapeDtypeStruct((T, KR), BF16), jax.ShapeDtypeStruct((T, RD), BF16)],
        scratch_shapes=[
            V((T, D), BF16), V((D, QR), BF16), V((D, KR + RD), BF16), V((QR, H * 96), BF16), V((KR, H * 128), BF16), V((320, D), BF16),
            V((8, 1, 320), BF16), V((8, 1, 96), BF16), V((8, 1, 32), BF16), V((T, QR), F32), V((T, KR + RD), F32),
            V((QR, T), BF16), V((T, KR), BF16), V((KR, T), BF16), V((T, RD), BF16),
            V((HG * 96, QR), BF16), V((KR, HG * 64), BF16), V((HG * 64, KR), BF16), V((HG * 128, TC), BF16), V((TC, HG * 64), BF16), V((HG * 64, TC), BF16), V((2, TC, HG * 64), BF16),
            dma((len(PIECES), len(KINDS))), dma((len(PIECES), len(KINDS))), dma((len(PIECES),)), dma((3, 8)), dma((3, 7)), dma((T // TA,)), dma((3,)), dma((2,)),
        ],
        compiler_params=pltpu.CompilerParams(collective_id=0, has_side_effects=True, vmem_limit_bytes=63 << 20),
    )(x, *gains, *ws, *(jnp.asarray(t) for t in tab))


def out_kernel(o_ref, w_ref, x_ref, c_ref, r_ref, y_ref, c_out, r_out):
    y_ref[...] = (x_ref[...].astype(F32) + dot(o_ref[...], w_ref[...])).astype(BF16)

    @pl.when(pl.program_id(1) == 0)
    def _():
        c_out[...] = c_ref[...]
        r_out[...] = r_ref[...]


def outp(o, w, x, c, r, tm=512, tn=512):
    return pl.pallas_call(
        out_kernel, grid=(T // tm, D // tn), name='outp',
        in_specs=[pl.BlockSpec((tm, D), lambda i, j: (i, 0)), pl.BlockSpec((D, tn), lambda i, j: (0, j)), pl.BlockSpec((tm, tn), lambda i, j: (i, j)),
                  pl.BlockSpec((tm, KR), lambda i, j: (i, 0)), pl.BlockSpec((tm, RD), lambda i, j: (i, 0))],
        out_specs=[pl.BlockSpec((tm, tn), lambda i, j: (i, j)), pl.BlockSpec((tm, KR), lambda i, j: (i, 0)), pl.BlockSpec((tm, RD), lambda i, j: (i, 0))],
        out_shape=[jax.ShapeDtypeStruct((T, D), BF16), jax.ShapeDtypeStruct((T, KR), BF16), jax.ShapeDtypeStruct((T, RD), BF16)],
        compiler_params=pltpu.CompilerParams(vmem_limit_bytes=60 << 20),
    )(o, w, x, c, r)


def tables():
    half = RD // 2
    freq = np.float32(10000.0) ** (np.float32(-2.0) * np.arange(half, dtype=np.float32) / np.float32(RD))
    ang = np.arange(S, dtype=np.float32)[:, None] * freq[None, :].astype(np.float32)
    return np.cos(ang).astype(np.float32), np.sin(ang).astype(np.float32)


def solution(mesh):
    batch, row, mat = P(('dp', 'fsdp')), P('fsdp'), P('fsdp', None)

    def local(tok, g1, wdq, gq, wuq, wkv, gkv, wukv, wo):
        cos, sin = tables()
        x = tok.reshape(T, D)
        o, w, c, r = front(x, (g1[None], gq[None], gkv[None]), (wdq, wkv, wuq, wukv, wo), cos, sin)
        y, c, r = outp(o, w, x, c, r)
        return y.reshape(tok.shape), c.reshape(-1, S, KR), r.reshape(-1, S, RD)

    return jax.shard_map(local, mesh=mesh, in_specs=(batch, row, mat, row, mat, mat, row, mat, mat),
                         out_specs=(batch,) * 3, check_vma=False)
```

time: 258 us -> 178 us (0.69)
  waiting for transfers between devices: 103 us -> 0 us
  Pallas kernels: 111 us -> 172 us
  blocking collectives: 15.9 us -> 0 us
  between operations: 14.5 us -> 0.64 us
  local copies, waits for them, and re-layouts: 11.4 us -> 4.9 us
    all_gather x5 -> x0, waiting for transfers between devices: 100 us -> none  [local(): ag = lambda w: lax.all_gather(w, 'fsdp', tiled=True)]
    pallas_call x3 -> x2, Pallas kernels: 111 us -> 172 us  [the longest x1 130 us: front(): pl.pallas_call(front_kernel, name='front', in_specs=[anyspace] + [vm] * 3...]
    unnamed x1 -> x0, blocking collectives: 15.9 us -> none
    all_gather x2 -> x0, local copies, waits for them, and re-layouts: 3.99 us -> none  [the longest x1 3.9 us: local(): ag = lambda w: lax.all_gather(w, 'fsdp', tiled=True)]
    unnamed x5 -> x0, waiting for transfers between devices: 3.11 us -> none
  transfers between devices with their start and end apart: 5 -> 0, of which waited for: 5 -> 0; matrix products, arithmetic and copies ran while one was open for 5% -> 0% of each run, Pallas kernels for 27% -> 0%
where the time goes in v2:
time: 178 us
  Pallas kernels  172 us (97%)
  local copies, waits for them, and re-layouts  4.9 us (3%)
    pallas_call x1, Pallas kernels, front(): pl.pallas_call(front_kernel, name='front', in_specs=[anyspace] + [vm] * 3...  130 us
    pallas_call x1, Pallas kernels, outp(): pl.pallas_call(out_kernel, grid=(T // tm, D // tn), name='outp', in_specs...  42.3 us
    unnamed x2, local copies, waits for them, and re-layouts  3.66 us

profile of v2, /device:TPU:0, one launch (start us, length us, event | category | flops | bytes accessed | tf_op | source)
XLA Modules:
  0.0 177.8 jit_solution(7414287254001993508)
XLA Ops:
  0.6 1.2 broadcast_in_dim.9.g1_s
  1.9 1.8 %copy.16.dkv_s = bf16[320,288]{1,0:T(8,128)(2,1)} copy(bf16[320,288]{0,1:T(8,128)(2,1)} %param.18) | data formatting | bytes 368640 | tf_op args[5]
  3.7 129.9 %front.1 = (bf16[2048,2560]{1,0:T(8,128)(2,1)}, bf16[2560,2560]{1,0:T(8,128)(2,1)}, bf16[2048,256]{1,0:T(8,128)(2,1)}, bf16[2048,32]{1,0:T(8,128)(2,1)}) custom-call(bf16[2048,2560]{1,0:T(8,128)(2,1)} %bitcast.6, bf16[1,320]{1,0:T(2,128)(2,1)} %broadcast_in_dim.9.g1_s, bf16[1,96]{1,0:T(2,128)(2,1)} %bitcast.9, bf16[1,32]{1,0:T(2,128)(2,1)} %bitcast.10, ...), custom_call_target="tpu_custom_call" | custom-call | tf_op jit(solution)/shard_map/front/pallas_call | solution.py:355
  133.6 42.3 %outp.1 = (bf16[2048,2560]{1,0:T(8,128)(2,1)}, bf16[2048,256]{1,0:T(8,128)(2,1)}, bf16[2048,32]{1,0:T(8,128)(2,1)}) custom-call(bf16[2048,2560]{1,0:T(8,128)(2,1)} %get-tuple-element.10.o_ref, bf16[2560,2560]{1,0:T(8,128)(2,1)} %get-tuple-element.11.w_ref, bf16[2048,2560]{1,0:T(8,128)(2,1)} %bitcast.7, bf16[2048,256]{1,0:T(8,128)(2,1)} %get-tuple-element.12.c_ref, ...), custom_call_target="tpu_custom_call" | custom-call | tf_op jit(solution)/shard_map/outp/pallas_call | solution.py:381
  175.9 1.9 %copy.17 = bf16[16,128,32]{1,2,0:T(8,128)(2,1)} copy(bf16[16,128,32]{2,1,0:T(8,128)(2,1)} %bitcast.8) | data formatting | bytes 262144

commit v3 on v2

--- a/solution.py
+++ b/solution.py
@@ -45,17 +45,21 @@
     ('ukv1', 'ukv', True, 32, 1024, 2048, 640),
     ('uq2', 'uq', False, 96, 2304, 1536, 32),
     ('ukv2', 'ukv', True, 32, 3072, 2048, 640),
-    ('o', 'o', False, 320, 0, 2560, 112),
+    ('o0', 'o', False, 320, 0, 640, 112),
+    ('o1', 'o', False, 320, 640, 640, 112),
+    ('o2', 'o', False, 320, 1280, 640, 112),
+    ('o3', 'o', False, 320, 1920, 640, 112),
 )
 PIDX = {p[0]: i for i, p in enumerate(PIECES)}
 KINDS = ('XE', 'YE', 'XS', 'YS', 'S0', 'Z1', 'Z2', 'DY', 'DX', 'Z3', 'S1', 'S2', 'S3')
 KIDX = {k: i for i, k in enumerate(KINDS)}
-D0, U0, U1, U2, O0 = ('dq', 'dkv'), ('uq0', 'ukv0'), ('uq1', 'ukv1'), ('uq2', 'ukv2'), ('o',)
+D0, U0, U1, U2 = ('dq', 'dkv'), ('uq0', 'ukv0'), ('uq1', 'ukv1'), ('uq2', 'ukv2')
+O0, O1, O2, O3 = ('o0',), ('o1',), ('o2',), ('o3',)
 
 
 def front_kernel(x_hbm, g1_s, gq_s, gkv_s, dq_s, dkv_s, uq_s, ukv_s, o_s, cos_ref, sin_ref, cosT_ref, sinT_ref,
                  attn_hbm, wo_hbm, c_hbm, r_hbm,
-                 xa, wdq, wdkv, wuq, wukv, ostage, g1b, gqb, gkvb, accq, acck, cqT, cbuf, cT, rbuf,
+                 xa, wdq, wdkv, wuq, wukv, ostage, g1b, gqb, gkvb, accq, acck, inv, cqT, cbuf, cT, rbuf, rT,
                  wqT, wk, wvT, qT, kbuf, vT, obuf,
                  ssem, rsem, lsem, gss, grs, xsem, osem, csem):
     z, f = lax.axis_index('dp'), lax.axis_index('fsdp')
@@ -133,11 +137,17 @@
         recv(names, 'DY')
         start(names, 'Z3')
 
-    def st4(names):
+    def st4x(names):
         recv(names, 'Z1')
         start(names, 'S1')
+
+    def st4y(names):
         recv(names, 'Z2')
         start(names, 'S2')
+
+    def st4(names):
+        st4x(names)
+        st4y(names)
 
     def st5(names):
         recv(names, 'DX', 'Z3')
@@ -151,16 +161,22 @@
             local(n).wait()
         recv(names, 'S0', 'S1', 'S2', 'S3')
 
+    def act(*todo):
+        stages = {'st0': st0, 'st1': st1, 'st2': st2, 'st3': st3, 'st4': st4, 'st4x': st4x, 'st4y': st4y, 'st5': st5, 'fin': fin, 'stage': stage}
+        for k in range(0, len(todo), 2):
+            stages[todo[k]](todo[k + 1])
+
     for i in range(T // TA):
         pltpu.make_async_copy(x_hbm.at[pl.ds(i * TA, TA)], xa.at[pl.ds(i * TA, TA)], xsem.at[i]).start()
     stage_o = pltpu.make_async_copy(o_s, ostage, osem.at[2])
     stage_o.start()
 
     barrier = pltpu.get_barrier_semaphore()
-    for p in plane:
-        pl.semaphore_signal(barrier, inc=1, device_id=(z, p), device_id_type=MESH)
-    pl.semaphore_signal(barrier, inc=1, device_id=dev['Z'], device_id_type=MESH)
-    pl.semaphore_wait(barrier, 8)
+    with jax.named_scope('barrier'):
+        for p in plane:
+            pl.semaphore_signal(barrier, inc=1, device_id=(z, p), device_id_type=MESH)
+        pl.semaphore_signal(barrier, inc=1, device_id=dev['Z'], device_id_type=MESH)
+        pl.semaphore_wait(barrier, 8)
 
     gains = []
     for j, (gs, gb) in enumerate(((g1_s, g1b), (gq_s, gqb), (gkv_s, gkvb))):
@@ -172,27 +188,39 @@
         own.start()
         gains.append(own)
     st0(D0)
-    for g in gains:
-        g.wait()
-
-    def row_of(gb):
-        return jnp.concatenate([gb[i].astype(F32) for i in range(8)], axis=-1)
-
-    g1, gq, gkv = row_of(g1b), row_of(gqb), row_of(gkvb)
-
-    def norm_tile(i, _):
+
+    def stat_tile(i, _):
         pltpu.make_async_copy(x_hbm.at[pl.ds(i * TA, TA)], xa.at[pl.ds(i * TA, TA)], xsem.at[i]).wait()
         for h in range(TA // 64):
             rows = pl.ds(pl.multiple_of(i * TA + h * 64, 64), 64)
-            v = xa[rows, :].astype(F32)
-            xa[rows, :] = (v * rms(v) * g1).astype(BF16)
+            inv[rows, :] = jnp.broadcast_to(rms(xa[rows, :].astype(F32)), (64, 128))
         return 0
 
-    def part(quarter, first):
+    with jax.named_scope('stats'):
+        lax.fori_loop(0, T // TA, stat_tile, 0)
+    with jax.named_scope('gains'):
+        for g in gains:
+            g.wait()
+
+    def row_of(gb):
+        return jnp.concatenate([gb[i].astype(F32) for i in range(8)], axis=-1)
+
+    g1, gq, gkv = row_of(g1b), row_of(gqb), row_of(gkvb)
+
+    def norm_tile(i, _):
+        for h in range(TA // 64):
+            rows = pl.ds(pl.multiple_of(i * TA + h * 64, 64), 64)
+            scale = inv[rows, :]
+            for j in range(D // 128):
+                cols = slice(128 * j, 128 * j + 128)
+                xa[rows, cols] = (xa[rows, cols].astype(F32) * scale * g1[:, cols]).astype(BF16)
+        return 0
+
+    def part(quarter, first, lo, hi):
         cols = pl.ds(pl.multiple_of(quarter * 640, 128), 640)
 
         def tile(i, _):
-            rows = pl.ds(pl.multiple_of(i * TA, TA), TA)
+            rows = pl.ds(pl.multiple_of(i * 512, 512), 512)
             a = xa[rows, cols]
             pq, pk = dot(a, wdq[cols, :]), dot(a, wdkv[cols, :])
             if first:
@@ -201,12 +229,12 @@
                 accq[rows, :] += pq
                 acck[rows, :] += pk
             return 0
-        lax.fori_loop(0, T // TA, tile, 0)
+        lax.fori_loop(lo, hi, tile, 0)
 
     cos2 = jnp.concatenate([cos_ref[...]] * (TA // S), axis=0)
     sin2 = jnp.concatenate([sin_ref[...]] * (TA // S), axis=0)
 
-    def last_part(quarter):
+    def last_part(quarter, a0, a1):
         cols = pl.ds(pl.multiple_of(quarter * 640, 128), 640)
 
         def tile(i, _):
@@ -221,37 +249,43 @@
             cT[:, rows] = c.T
             lo, hi = kd[:, KR:KR + 16], kd[:, KR + 16:]
             rbuf[rows, :] = jnp.concatenate([lo * cos2 - hi * sin2, hi * cos2 + lo * sin2], axis=-1).astype(BF16)
+            for h in range(TA // S):
+                rT[i * (TA // S) + h] = rbuf[pl.ds(pl.multiple_of(i * TA + h * S, S), S), :].T
             return 0
-        lax.fori_loop(0, T // TA, tile, 0)
-
-    lax.fori_loop(0, 4, norm_tile, 0)
-    st1(D0)
-    lax.fori_loop(4, 8, norm_tile, 0)
+        lax.fori_loop(a0, a1, tile, 0)
+
+    def run(name, fn, *args):
+        with jax.named_scope(name):
+            fn(*args)
+
+    run('norm_a', lax.fori_loop, 0, 4, norm_tile, 0)
+    run('c_a', act, 'st1', D0, 'st0', U0)
+    run('norm_b', lax.fori_loop, 4, 8, norm_tile, 0)
     for n in D0:
         local(n).wait()
-    recv(D0, 'S0')
-    part(f // 2, True)
-    st2(D0)
-    st0(U0)
-    st3(D0)
-    st4(D0)
-    recv(D0, 'S1')
-    part(fx // 2, False)
-    st5(D0)
-    st1(U0)
-    recv(D0, 'S2')
-    part(fy // 2, False)
-    st2(U0)
-    st0(U1)
-    st3(U0)
-    recv(D0, 'S3')
-    last_part(fd // 2)
-    outs = [pltpu.make_async_copy(cbuf, c_hbm, csem.at[0]), pltpu.make_async_copy(rbuf, r_hbm, csem.at[1])]
+    run('c_b', recv, D0, 'S0')
+    run('own_a', part, f // 2, True, 0, 2)
+    run('c_c', act, 'st2', D0, 'st4x', D0)
+    run('own_b', part, f // 2, True, 2, 4)
+    run('c_d', act, 'st0', U1, 'st4y', D0)
+    run('c_e', recv, D0, 'S1')
+    run('x_a', part, fx // 2, False, 0, 2)
+    run('c_f', act, 'st3', D0, 'st1', U0)
+    run('x_b', part, fx // 2, False, 2, 4)
+    run('c_g', recv, D0, 'S2')
+    run('y_a', part, fy // 2, False, 0, 2)
+    run('c_h', act, 'st5', D0, 'st2', U0, 'st0', U2)
+    run('y_b', part, fy // 2, False, 2, 4)
+    run('c_i', act, 'st3', U0, 'st4', U0)
+    run('c_j', recv, D0, 'S3')
+    run('d_a', last_part, fd // 2, 0, 4)
+    run('c_k', act, 'st1', U1, 'stage', O0, 'st0', O0)
+    run('d_b', last_part, fd // 2, 4, 8)
+    run('c_l', act, 'st5', U0, 'st2', U1)
+    outs = [pltpu.make_async_copy(cbuf, c_hbm, csem.at[0]), pltpu.make_async_copy(rT, r_hbm, csem.at[1])]
     for o in outs:
         o.start()
-    st4(U0)
-    st5(U0)
-    fin(U0)
+    run('c_m', fin, U0)
 
     keep = lax.broadcasted_iota(jnp.int32, (S, S), 0) <= lax.broadcasted_iota(jnp.int32, (S, S), 1)
     lane = lax.broadcasted_iota(jnp.int32, (S, 128), 1)
@@ -274,31 +308,30 @@
         return pltpu.make_async_copy(obuf.at[i % 2], attn_hbm.at[pl.ds(pl.multiple_of(tc * TC, TC), TC), pl.ds(pl.multiple_of(g * (HG * 64), 128), HG * 64)], osem.at[i % 2])
 
     sched = {
-        0: ((st1, U1),),
-        1: ((st2, U1), (st0, U2), (st3, U1)),
-        2: ((st4, U1), (st5, U1), (st1, U2)),
-        3: ((st2, U2), (stage, O0), (st0, O0), (st3, U2)),
-        4: ((fin, U1), (st4, U2), (st5, U2)),
-        6: ((fin, U2),),
-        7: ((st1, O0),),
-        10: ((st2, O0), (st3, O0)),
-        13: ((st4, O0),),
-        15: ((st5, O0),),
+        1: ('st3', U1, 'st4', U1, 'st1', U2),
+        2: ('st2', U2, 'st0', O1, 'st5', U1),
+        3: ('fin', U1, 'st3', U2, 'st4', U2),
+        5: ('st1', O0, 'st5', U2, 'st0', O2),
+        6: ('fin', U2, 'st2', O0),
+        8: ('st3', O0, 'st4', O0, 'st1', O1),
+        9: ('st0', O3, 'st2', O1),
+        11: ('st5', O0, 'st3', O1, 'st4', O1),
+        13: ('st1', O2, 'st2', O2, 'st5', O1),
+        15: ('st3', O2, 'st4', O2, 'st1', O3),
+        17: ('st2', O3, 'st5', O2),
+        18: ('st3', O3, 'st4', O3),
     }
-
-    def act(todo):
-        for fn, names in todo:
-            fn(names)
 
     def step(i, _):
         g, tc = i // NCH, i % NCH
         tok = pl.multiple_of(tc * TC, TC)
         for s, todo in sched.items():
-            pl.when(i == s)(functools.partial(act, todo))
+            pl.when(i == s)(functools.partial(run, f'comm_{s}', act, *todo))
 
         @pl.when(tc == 0)
         def _():
-            load_group(g)
+            with jax.named_scope('load_group'):
+                load_group(g)
 
         @pl.when(i >= 2)
         def _():
@@ -337,7 +370,10 @@
         return 0
 
     lax.fori_loop(0, STEPS, step, 0)
-    fin(O0)
+    with jax.named_scope('fin_O'):
+        st5(O3)
+        for names in (O0, O1, O2, O3):
+            fin(names)
     for i in (STEPS - 2, STEPS - 1):
         out_copy(i).wait()
     for o in outs:
@@ -356,11 +392,11 @@
         front_kernel, name='front',
         in_specs=[anyspace] + [vm] * 3 + [anyspace] * 5 + [vm] * 4,
         out_specs=[anyspace] * 4,
-        out_shape=[jax.ShapeDtypeStruct((T, H * VD), BF16), jax.ShapeDtypeStruct((H * VD, D), BF16), jax.ShapeDtypeStruct((T, KR), BF16), jax.ShapeDtypeStruct((T, RD), BF16)],
+        out_shape=[jax.ShapeDtypeStruct((T, H * VD), BF16), jax.ShapeDtypeStruct((H * VD, D), BF16), jax.ShapeDtypeStruct((T, KR), BF16), jax.ShapeDtypeStruct((T // S, RD, S), BF16)],
         scratch_shapes=[
             V((T, D), BF16), V((D, QR), BF16), V((D, KR + RD), BF16), V((QR, H * 96), BF16), V((KR, H * 128), BF16), V((320, D), BF16),
-            V((8, 1, 320), BF16), V((8, 1, 96), BF16), V((8, 1, 32), BF16), V((T, QR), F32), V((T, KR + RD), F32),
-            V((QR, T), BF16), V((T, KR), BF16), V((KR, T), BF16), V((T, RD), BF16),
+            V((8, 1, 320), BF16), V((8, 1, 96), BF16), V((8, 1, 32), BF16), V((T, QR), F32), V((T, KR + RD), F32), V((T, 128), F32),
+            V((QR, T), BF16), V((T, KR), BF16), V((KR, T), BF16), V((T, RD), BF16), V((T // S, RD, S), BF16),
             V((HG * 96, QR), BF16), V((KR, HG * 64), BF16), V((HG * 64, KR), BF16), V((HG * 128, TC), BF16), V((TC, HG * 64), BF16), V((HG * 64, TC), BF16), V((2, TC, HG * 64), BF16),
             dma((len(PIECES), len(KINDS))), dma((len(PIECES), len(KINDS))), dma((len(PIECES),)), dma((3, 8)), dma((3, 7)), dma((T // TA,)), dma((3,)), dma((2,)),
         ],
@@ -369,22 +405,24 @@
 
 
 def out_kernel(o_ref, w_ref, x_ref, c_ref, r_ref, y_ref, c_out, r_out):
-    y_ref[...] = (x_ref[...].astype(F32) + dot(o_ref[...], w_ref[...])).astype(BF16)
-
-    @pl.when(pl.program_id(1) == 0)
-    def _():
-        c_out[...] = c_ref[...]
-        r_out[...] = r_ref[...]
-
-
-def outp(o, w, x, c, r, tm=512, tn=512):
+    for n in range(0, y_ref.shape[1], 256):
+        cols = slice(n, n + 256)
+        y_ref[:, cols] = (x_ref[:, cols].astype(F32) + dot(o_ref[...], w_ref[:, cols])).astype(BF16)
+    c_out[...] = c_ref[...]
+    r_out[...] = r_ref[...]
+
+
+def outp(o, w, x, c, r, tm=1024, tn=1280):
+    nt = D // tn
+    cr = T // ((T // tm) * nt)
+    step = lambda j, i: j * (T // tm) + i
     return pl.pallas_call(
-        out_kernel, grid=(T // tm, D // tn), name='outp',
-        in_specs=[pl.BlockSpec((tm, D), lambda i, j: (i, 0)), pl.BlockSpec((D, tn), lambda i, j: (0, j)), pl.BlockSpec((tm, tn), lambda i, j: (i, j)),
-                  pl.BlockSpec((tm, KR), lambda i, j: (i, 0)), pl.BlockSpec((tm, RD), lambda i, j: (i, 0))],
-        out_specs=[pl.BlockSpec((tm, tn), lambda i, j: (i, j)), pl.BlockSpec((tm, KR), lambda i, j: (i, 0)), pl.BlockSpec((tm, RD), lambda i, j: (i, 0))],
-        out_shape=[jax.ShapeDtypeStruct((T, D), BF16), jax.ShapeDtypeStruct((T, KR), BF16), jax.ShapeDtypeStruct((T, RD), BF16)],
-        compiler_params=pltpu.CompilerParams(vmem_limit_bytes=60 << 20),
+        out_kernel, grid=(nt, T // tm), name='outp',
+        in_specs=[pl.BlockSpec((tm, D), lambda j, i: (i, 0)), pl.BlockSpec((D, tn), lambda j, i: (0, j)), pl.BlockSpec((tm, tn), lambda j, i: (i, j)),
+                  pl.BlockSpec((cr, KR), lambda j, i: (step(j, i), 0)), pl.BlockSpec((cr // S, RD, S), lambda j, i: (step(j, i), 0, 0))],
+        out_specs=[pl.BlockSpec((tm, tn), lambda j, i: (i, j)), pl.BlockSpec((cr, KR), lambda j, i: (step(j, i), 0)), pl.BlockSpec((cr // S, RD, S), lambda j, i: (step(j, i), 0, 0))],
+        out_shape=[jax.ShapeDtypeStruct((T, D), BF16), jax.ShapeDtypeStruct((T, KR), BF16), jax.ShapeDtypeStruct((T // S, RD, S), BF16)],
+        compiler_params=pltpu.CompilerParams(vmem_limit_bytes=62 << 20),
     )(o, w, x, c, r)
 
 
@@ -403,7 +441,7 @@
         x = tok.reshape(T, D)
         o, w, c, r = front(x, (g1[None], gq[None], gkv[None]), (wdq, wkv, wuq, wukv, wo), cos, sin)
         y, c, r = outp(o, w, x, c, r)
-        return y.reshape(tok.shape), c.reshape(-1, S, KR), r.reshape(-1, S, RD)
+        return y.reshape(tok.shape), c.reshape(-1, S, KR), jnp.swapaxes(r, 1, 2)
 
     return jax.shard_map(local, mesh=mesh, in_specs=(batch, row, mat, row, mat, mat, row, mat, mat),
                          out_specs=(batch,) * 3, check_vma=False)

time: 178 us -> 154 us (0.87)
  Pallas kernels: 172 us -> 150 us
  local copies, waits for them, and re-layouts: 4.9 us -> 3.03 us
    pallas_call x1, Pallas kernels: 130 us -> 115 us  [front(): pl.pallas_call(front_kernel, name='front', in_specs=[anyspace] + [vm] * 3...]
    pallas_call x1, Pallas kernels: 42.3 us -> 34.7 us  [outp(): pl.pallas_call(out_kernel, grid=(nt, T // tm), name='outp', in_specs=[pl....]
    unnamed x2 -> x1, local copies, waits for them, and re-layouts: 3.66 us -> 1.78 us
where the time goes in v3:
time: 154 us; the launch traced here: 153 us
  Pallas kernels  150 us (97%)
  local copies, waits for them, and re-layouts  3.03 us (2%)
    pallas_call x1, Pallas kernels, front(): pl.pallas_call(front_kernel, name='front', in_specs=[anyspace] + [vm] * 3...  115 us
    pallas_call x1, Pallas kernels, outp(): pl.pallas_call(out_kernel, grid=(nt, T // tm), name='outp', in_specs=[pl....  34.7 us

profile of v3, /device:TPU:0, one launch (start us, length us, event | category | flops | bytes accessed | tf_op | source)
XLA Modules:
  0.0 153.3 jit_solution(10868872230420030325)
XLA Ops:
  0.6 1.2 broadcast_in_dim.9.g1_s
  1.9 1.8 %copy.16.dkv_s = bf16[320,288]{1,0:T(8,128)(2,1)} copy(bf16[320,288]{0,1:T(8,128)(2,1)} %param.18) | data formatting | bytes 368640 | tf_op args[5]
  3.7 115.0 %front.1 = (bf16[2048,2560]{1,0:T(8,128)(2,1)}, bf16[2560,2560]{1,0:T(8,128)(2,1)}, bf16[2048,256]{1,0:T(8,128)(2,1)}, bf16[16,32,128]{2,1,0:T(8,128)(2,1)}) custom-call(bf16[2048,2560]{1,0:T(8,128)(2,1)} %bitcast.6, bf16[1,320]{1,0:T(2,128)(2,1)} %broadcast_in_dim.9.g1_s, bf16[1,96]{1,0:T(2,128)(2,1)} %bitcast.8, bf16[1,32]{1,0:T(2,128)(2,1)} %bitcast.9, ...), custom_call_target="tpu_custom_call" | custom-call | tf_op jit(solution)/shard_map/front/pallas_call | solution.py:391
  118.6 34.7 %outp.1 = (bf16[2048,2560]{1,0:T(8,128)(2,1)}, bf16[2048,256]{1,0:T(8,128)(2,1)}, bf16[16,32,128]{2,1,0:T(8,128)(2,1)}) custom-call(bf16[2048,2560]{1,0:T(8,128)(2,1)} %get-tuple-element.10.o_ref, bf16[2560,2560]{1,0:T(8,128)(2,1)} %get-tuple-element.11.w_ref, bf16[2048,2560]{1,0:T(8,128)(2,1)} %bitcast.7, bf16[2048,256]{1,0:T(8,128)(2,1)} %get-tuple-element.12.c_ref, ...), custom_call_target="tpu_custom_call" | custom-call | tf_op jit(solution)/shard_map/outp/pallas_call | solution.py:419

commit v4 on v3

--- a/solution.py
+++ b/solution.py
@@ -51,10 +51,66 @@
     ('o3', 'o', False, 320, 1920, 640, 112),
 )
 PIDX = {p[0]: i for i, p in enumerate(PIECES)}
-KINDS = ('XE', 'YE', 'XS', 'YS', 'S0', 'Z1', 'Z2', 'DY', 'DX', 'Z3', 'S1', 'S2', 'S3')
+SPLIT = ('S1a', 'S1b', 'S2a', 'S2b', 'S3a', 'S3b')
+KINDS = ('XE', 'YE', 'XS', 'YS', 'S0', 'Z1', 'Z2', 'DY', 'DX', 'Z3', 'S1', 'S2', 'S3') + SPLIT
 KIDX = {k: i for i, k in enumerate(KINDS)}
-D0, U0, U1, U2 = ('dq', 'dkv'), ('uq0', 'ukv0'), ('uq1', 'ukv1'), ('uq2', 'ukv2')
-O0, O1, O2, O3 = ('o0',), ('o1',), ('o2',), ('o3',)
+GROUPS = {'dq': ('dq',), 'dkv': ('dkv',), 'U0': ('uq0', 'ukv0'), 'U1': ('uq1', 'ukv1'), 'U2': ('uq2', 'ukv2'),
+          'O0': ('o0',), 'O1': ('o1',), 'O2': ('o2',), 'O3': ('o3',)}
+STAGES = {
+    'st0': ((), ('XE', 'YE', 'XS', 'YS', 'S0')),
+    'st1': (('XE', 'YE'), ('Z1', 'Z2', 'DY')),
+    'st2': (('XS', 'YS'), ('DX',)),
+    'st4x': (('Z1',), ('S1',)),
+    'st3': (('DY',), ('Z3',)),
+    'st4y': (('Z2',), ('S2',)),
+    'st5': (('DX', 'Z3'), ('S3',)),
+    'fin': (('S0', 'S1', 'S2', 'S3'), ()),
+    'st2d': (('XS', 'YS'), ('DX', 'S1a', 'S2a')),
+    'st4xd': (('Z1',), ('S1b',)),
+    'st4yd': (('Z2',), ('S2b',)),
+    'st5a': (('DX',), ('S3a',)),
+    'st5b': (('Z3',), ('S3b',)),
+    'find': ((), ()),
+}
+SCHED = {
+    'stats0': (('st0', 'dq'),),
+    'norm0': (('st0', 'dkv'),),
+    'part0': (('st1', 'dq'), ('recv', 'dq', 'S0'), ('recv', 'dkv', 'S0')),
+    'part3': (('st0', 'U0'),),
+    'part4': (('st2d', 'dq'), ('st4xd', 'dq'), ('recv', 'dq', 'S1a+S1b'), ('st1', 'dkv'), ('st2d', 'dkv'), ('st4xd', 'dkv'), ('st3', 'dq'), ('st4yd', 'dq'), ('st0', 'U1'), ('recv', 'dkv', 'S1a+S1b')),
+    'part5': (('st1', 'U0'),),
+    'part6': (('st2', 'U0'),),
+    'part7': (('st5a', 'dq'), ('st3', 'dkv'), ('st4yd', 'dkv')),
+    'part8': (('st5b', 'dq'), ('find', 'dq'), ('st5a', 'dkv'), ('st0', 'U2'), ('recv', 'dq', 'S2a+S2b'), ('recv', 'dkv', 'S2a+S2b'), ('st4x', 'U0')),
+    'part10': (('st1', 'U1'),),
+    'part11': (('st5b', 'dkv'), ('find', 'dkv')),
+    'd0': (('recv', 'dq', 'S3a+S3b'), ('recv', 'dkv', 'S3a+S3b')),
+    'd1': (('st3', 'U0'), ('st4y', 'U0'), ('st2', 'U1')),
+    'd2': (('st4x', 'U1'), ('st0', 'O0')),
+    'd3': (('st1', 'U2'),),
+    's0': (('st5', 'U0'), ('st2', 'U2'), ('fin', 'U0'), ('st3', 'U1'), ('st4y', 'U1')),
+    's1': (('st4x', 'U2'), ('st0', 'O1')),
+    's2': (('st1', 'O0'),),
+    's3': (('st5', 'U1'), ('st2', 'O0')),
+    's4': (('fin', 'U1'), ('st3', 'U2'), ('st4y', 'U2'), ('st0', 'O2')),
+    's5': (('st4x', 'O0'), ('st1', 'O1')),
+    's6': (('st2', 'O1'),),
+    's7': (('st5', 'U2'), ('st3', 'O0'), ('st4y', 'O0')),
+    's8': (('fin', 'U2'), ('st4x', 'O1'), ('st0', 'O3')),
+    's9': (('st1', 'O2'), ('st2', 'O2')),
+    's10': (('st5', 'O0'), ('st3', 'O1'), ('st4y', 'O1')),
+    's11': (('fin', 'O0'),),
+    's12': (('st4x', 'O2'), ('st1', 'O3')),
+    's13': (('st3', 'O2'), ('st4y', 'O2'), ('st2', 'O3')),
+    's14': (('st5', 'O1'),),
+    's15': (('fin', 'O1'), ('st4x', 'O3'), ('st3', 'O3')),
+    's16': (('st4y', 'O3'),),
+    's17': (('st5', 'O2'),),
+    's18': (('fin', 'O2'),),
+    's19': (('st5', 'O3'),),
+    'end': (('fin', 'O3'),),
+    'stats1': (),
+}
 
 
 def front_kernel(x_hbm, g1_s, gq_s, gkv_s, dq_s, dkv_s, uq_s, ukv_s, o_s, cos_ref, sin_ref, cosT_ref, sinT_ref,
@@ -77,7 +133,7 @@
     def region(piece, shard, part, base):
         name, arr, bycol, rows, c0, nc, e = piece
         n = nc if bycol else rows
-        off, size = {'E': (z * (n - e), e), 'S': (e, n - 2 * e), 'A': (0, n)}[part]
+        off, size = {'E': (z * (n - e), e), 'S': (e, n - 2 * e), 'A': (0, n), 'B': (z * e, n - e), 'M': ((1 - z) * (n - e), e)}[part]
         if bycol:
             row = shard * rows if base else 0
             return pl.ds(pl.multiple_of(row, 16), rows), pl.ds(pl.multiple_of(c0 + off, 128), size)
@@ -96,7 +152,9 @@
             to = dev[kind[0]]
         else:
             shard, part, to = {'Z1': (fx, 'E', 'Z'), 'Z2': (fy, 'E', 'Z'), 'Z3': (fd, 'E', 'Z'), 'DY': (fx, 'E', 'Y'),
-                               'DX': (fy, 'S', 'X'), 'S1': (fx, 'A', 'S'), 'S2': (fy, 'A', 'S'), 'S3': (fd, 'A', 'S')}[kind]
+                               'DX': (fy, 'S', 'X'), 'S1': (fx, 'A', 'S'), 'S2': (fy, 'A', 'S'), 'S3': (fd, 'A', 'S'),
+                               'S1a': (fx, 'B', 'S'), 'S1b': (fx, 'M', 'S'), 'S2a': (fy, 'B', 'S'), 'S2b': (fy, 'M', 'S'),
+                               'S3a': (fd, 'B', 'S'), 'S3b': (fd, 'M', 'S')}[kind]
             to = dev[to]
             r1, c1 = region(piece, shard, part, True)
             s_ref = d_ref = buf[arr].at[r1, c1]
@@ -120,51 +178,33 @@
             for n in names:
                 copy(n, k).wait_recv()
 
-    def st0(names):
-        start(names, 'XE', 'YE', 'XS', 'YS', 'S0')
-        for n in names:
-            local(n).start()
-
-    def st1(names):
-        recv(names, 'XE', 'YE')
-        start(names, 'Z1', 'Z2', 'DY')
-
-    def st2(names):
-        recv(names, 'XS', 'YS')
-        start(names, 'DX')
-
-    def st3(names):
-        recv(names, 'DY')
-        start(names, 'Z3')
-
-    def st4x(names):
-        recv(names, 'Z1')
-        start(names, 'S1')
-
-    def st4y(names):
-        recv(names, 'Z2')
-        start(names, 'S2')
-
-    def st4(names):
-        st4x(names)
-        st4y(names)
-
-    def st5(names):
-        recv(names, 'DX', 'Z3')
-        start(names, 'S3')
-
-    def stage(names):
-        stage_o.wait()
-
-    def fin(names):
-        for n in names:
-            local(n).wait()
-        recv(names, 'S0', 'S1', 'S2', 'S3')
-
-    def act(*todo):
-        stages = {'st0': st0, 'st1': st1, 'st2': st2, 'st3': st3, 'st4': st4, 'st4x': st4x, 'st4y': st4y, 'st5': st5, 'fin': fin, 'stage': stage}
-        for k in range(0, len(todo), 2):
-            stages[todo[k]](todo[k + 1])
+    def comm(todo):
+        for op in todo:
+            stage, piece = op[0], op[1]
+            names = GROUPS[piece]
+            if stage == 'recv':
+                recv(names, *op[2].split('+'))
+                continue
+            if stage == 'st0' and piece == 'O0':
+                stage_o.wait()
+            waits, starts = STAGES[stage]
+            recv(names, *waits)
+            start(names, *starts)
+            if stage == 'st0':
+                for n in names:
+                    local(n).start()
+            if stage in ('fin', 'find'):
+                for n in names:
+                    if piece not in ('dq', 'dkv'):
+                        local(n).wait()
+
+    def at(seg, i):
+        for name, todo in SCHED.items():
+            if name.startswith(seg) and name[len(seg):].isdigit() and todo:
+                @pl.when(i == int(name[len(seg):]))
+                def _(todo=todo, name=name):
+                    with jax.named_scope('comm_' + name):
+                        comm(todo)
 
     for i in range(T // TA):
         pltpu.make_async_copy(x_hbm.at[pl.ds(i * TA, TA)], xa.at[pl.ds(i * TA, TA)], xsem.at[i]).start()
@@ -187,10 +227,17 @@
         own = pltpu.make_async_copy(gs, gb.at[f], gss.at[j, 7])
         own.start()
         gains.append(own)
-    st0(D0)
+    comm(SCHED['stats0'])
 
     def stat_tile(i, _):
+        @pl.when(i == 4)
+        def _():
+            comm(SCHED['stats1'])
         pltpu.make_async_copy(x_hbm.at[pl.ds(i * TA, TA)], xa.at[pl.ds(i * TA, TA)], xsem.at[i]).wait()
+        zero = jnp.zeros((TA, 128), F32)
+        for j in range(QR // 128):
+            accq[pl.ds(pl.multiple_of(i * TA, TA), TA), 128 * j:128 * j + 128] = zero
+        acck[pl.ds(pl.multiple_of(i * TA, TA), TA), :] = jnp.zeros((TA, KR + RD), F32)
         for h in range(TA // 64):
             rows = pl.ds(pl.multiple_of(i * TA + h * 64, 64), 64)
             inv[rows, :] = jnp.broadcast_to(rms(xa[rows, :].astype(F32)), (64, 128))
@@ -208,6 +255,7 @@
     g1, gq, gkv = row_of(g1b), row_of(gqb), row_of(gkvb)
 
     def norm_tile(i, _):
+        pl.when(i % 2 == 0)(functools.partial(at, 'norm', i // 2))
         for h in range(TA // 64):
             rows = pl.ds(pl.multiple_of(i * TA + h * 64, 64), 64)
             scale = inv[rows, :]
@@ -216,28 +264,25 @@
                 xa[rows, cols] = (xa[rows, cols].astype(F32) * scale * g1[:, cols]).astype(BF16)
         return 0
 
-    def part(quarter, first, lo, hi):
+    def part(i, _):
+        at('part', i)
+        which, t = i // 4, i % 4
+        quarter = ((yy + which // 2) % 2) * 2 + (xx + which % 2) % 2
         cols = pl.ds(pl.multiple_of(quarter * 640, 128), 640)
-
-        def tile(i, _):
-            rows = pl.ds(pl.multiple_of(i * 512, 512), 512)
-            a = xa[rows, cols]
-            pq, pk = dot(a, wdq[cols, :]), dot(a, wdkv[cols, :])
-            if first:
-                accq[rows, :], acck[rows, :] = pq, pk
-            else:
-                accq[rows, :] += pq
-                acck[rows, :] += pk
-            return 0
-        lax.fori_loop(lo, hi, tile, 0)
+        rows = pl.ds(pl.multiple_of(t * 512, 512), 512)
+        a = xa[rows, cols]
+        accq[rows, :] += dot(a, wdq[cols, :])
+        acck[rows, :] += dot(a, wdkv[cols, :])
+        return 0
 
     cos2 = jnp.concatenate([cos_ref[...]] * (TA // S), axis=0)
     sin2 = jnp.concatenate([sin_ref[...]] * (TA // S), axis=0)
 
-    def last_part(quarter, a0, a1):
-        cols = pl.ds(pl.multiple_of(quarter * 640, 128), 640)
+    def last_part():
+        cols = pl.ds(pl.multiple_of((fd // 2) * 640, 128), 640)
 
         def tile(i, _):
+            pl.when(i % 2 == 0)(functools.partial(at, 'd', i // 2))
             rows = pl.ds(pl.multiple_of(i * TA, TA), TA)
             a = xa[rows, cols]
             qd = accq[rows, :] + dot(a, wdq[cols, :])
@@ -252,40 +297,19 @@
             for h in range(TA // S):
                 rT[i * (TA // S) + h] = rbuf[pl.ds(pl.multiple_of(i * TA + h * S, S), S), :].T
             return 0
-        lax.fori_loop(a0, a1, tile, 0)
-
-    def run(name, fn, *args):
-        with jax.named_scope(name):
-            fn(*args)
-
-    run('norm_a', lax.fori_loop, 0, 4, norm_tile, 0)
-    run('c_a', act, 'st1', D0, 'st0', U0)
-    run('norm_b', lax.fori_loop, 4, 8, norm_tile, 0)
-    for n in D0:
+        lax.fori_loop(0, T // TA, tile, 0)
+
+    with jax.named_scope('norm'):
+        lax.fori_loop(0, T // TA, norm_tile, 0)
+    for n in ('dq', 'dkv'):
         local(n).wait()
-    run('c_b', recv, D0, 'S0')
-    run('own_a', part, f // 2, True, 0, 2)
-    run('c_c', act, 'st2', D0, 'st4x', D0)
-    run('own_b', part, f // 2, True, 2, 4)
-    run('c_d', act, 'st0', U1, 'st4y', D0)
-    run('c_e', recv, D0, 'S1')
-    run('x_a', part, fx // 2, False, 0, 2)
-    run('c_f', act, 'st3', D0, 'st1', U0)
-    run('x_b', part, fx // 2, False, 2, 4)
-    run('c_g', recv, D0, 'S2')
-    run('y_a', part, fy // 2, False, 0, 2)
-    run('c_h', act, 'st5', D0, 'st2', U0, 'st0', U2)
-    run('y_b', part, fy // 2, False, 2, 4)
-    run('c_i', act, 'st3', U0, 'st4', U0)
-    run('c_j', recv, D0, 'S3')
-    run('d_a', last_part, fd // 2, 0, 4)
-    run('c_k', act, 'st1', U1, 'stage', O0, 'st0', O0)
-    run('d_b', last_part, fd // 2, 4, 8)
-    run('c_l', act, 'st5', U0, 'st2', U1)
+    with jax.named_scope('parts'):
+        lax.fori_loop(0, 12, part, 0)
+    with jax.named_scope('last'):
+        last_part()
     outs = [pltpu.make_async_copy(cbuf, c_hbm, csem.at[0]), pltpu.make_async_copy(rT, r_hbm, csem.at[1])]
     for o in outs:
         o.start()
-    run('c_m', fin, U0)
 
     keep = lax.broadcasted_iota(jnp.int32, (S, S), 0) <= lax.broadcasted_iota(jnp.int32, (S, S), 1)
     lane = lax.broadcasted_iota(jnp.int32, (S, 128), 1)
@@ -307,26 +331,10 @@
         g, tc = i // NCH, i % NCH
         return pltpu.make_async_copy(obuf.at[i % 2], attn_hbm.at[pl.ds(pl.multiple_of(tc * TC, TC), TC), pl.ds(pl.multiple_of(g * (HG * 64), 128), HG * 64)], osem.at[i % 2])
 
-    sched = {
-        1: ('st3', U1, 'st4', U1, 'st1', U2),
-        2: ('st2', U2, 'st0', O1, 'st5', U1),
-        3: ('fin', U1, 'st3', U2, 'st4', U2),
-        5: ('st1', O0, 'st5', U2, 'st0', O2),
-        6: ('fin', U2, 'st2', O0),
-        8: ('st3', O0, 'st4', O0, 'st1', O1),
-        9: ('st0', O3, 'st2', O1),
-        11: ('st5', O0, 'st3', O1, 'st4', O1),
-        13: ('st1', O2, 'st2', O2, 'st5', O1),
-        15: ('st3', O2, 'st4', O2, 'st1', O3),
-        17: ('st2', O3, 'st5', O2),
-        18: ('st3', O3, 'st4', O3),
-    }
-
     def step(i, _):
         g, tc = i // NCH, i % NCH
         tok = pl.multiple_of(tc * TC, TC)
-        for s, todo in sched.items():
-            pl.when(i == s)(functools.partial(run, f'comm_{s}', act, *todo))
+        at('s', i)
 
         @pl.when(tc == 0)
         def _():
@@ -371,15 +379,15 @@
 
     lax.fori_loop(0, STEPS, step, 0)
     with jax.named_scope('fin_O'):
-        st5(O3)
-        for names in (O0, O1, O2, O3):
-            fin(names)
+        comm(SCHED['end'])
     for i in (STEPS - 2, STEPS - 1):
         out_copy(i).wait()
     for o in outs:
         o.wait()
     for p in PIECES:
         for k in KINDS:
+            if k in (('S1', 'S2', 'S3') if p[1] in ('dq', 'dkv') else SPLIT):
+                continue
             copy(p[0], k).wait_send()
 
 

time: 154 us -> 140 us (0.909)
  Pallas kernels: 150 us -> 137 us
    pallas_call x1, Pallas kernels: 115 us -> 102 us  [front(): pl.pallas_call(front_kernel, name='front', in_specs=[anyspace] + [vm] * 3...]
where the time goes in v4:
time: 140 us
  Pallas kernels  137 us (98%)
  local copies, waits for them, and re-layouts  3.03 us (2%)
    pallas_call x1, Pallas kernels, front(): pl.pallas_call(front_kernel, name='front', in_specs=[anyspace] + [vm] * 3...  102 us
    pallas_call x1, Pallas kernels, outp(): pl.pallas_call(out_kernel, grid=(nt, T // tm), name='outp', in_specs=[pl....  34.7 us

profile of v4, /device:TPU:0, one launch (start us, length us, event | category | flops | bytes accessed | tf_op | source)
XLA Modules:
  0.0 140.3 jit_solution(1887475416031902442)
XLA Ops:
  0.6 1.2 broadcast_in_dim.9.g1_s
  1.9 1.8 %copy.16.dkv_s = bf16[320,288]{1,0:T(8,128)(2,1)} copy(bf16[320,288]{0,1:T(8,128)(2,1)} %param.18) | data formatting | bytes 368640 | tf_op args[5]
  3.7 101.9 %front.1 = (bf16[2048,2560]{1,0:T(8,128)(2,1)}, bf16[2560,2560]{1,0:T(8,128)(2,1)}, bf16[2048,256]{1,0:T(8,128)(2,1)}, bf16[16,32,128]{2,1,0:T(8,128)(2,1)}) custom-call(bf16[2048,2560]{1,0:T(8,128)(2,1)} %bitcast.6, bf16[1,320]{1,0:T(2,128)(2,1)} %broadcast_in_dim.9.g1_s, bf16[1,96]{1,0:T(2,128)(2,1)} %bitcast.8, bf16[1,32]{1,0:T(2,128)(2,1)} %bitcast.9, ...), custom_call_target="tpu_custom_call" | custom-call | tf_op jit(solution)/shard_map/front/pallas_call | solution.py:399
  105.6 34.7 %outp.1 = (bf16[2048,2560]{1,0:T(8,128)(2,1)}, bf16[2048,256]{1,0:T(8,128)(2,1)}, bf16[16,32,128]{2,1,0:T(8,128)(2,1)}) custom-call(bf16[2048,2560]{1,0:T(8,128)(2,1)} %get-tuple-element.10.o_ref, bf16[2560,2560]{1,0:T(8,128)(2,1)} %get-tuple-element.11.w_ref, bf16[2048,2560]{1,0:T(8,128)(2,1)} %bitcast.7, bf16[2048,256]{1,0:T(8,128)(2,1)} %get-tuple-element.12.c_ref, ...), custom_call_target="tpu_custom_call" | custom-call | tf_op jit(solution)/shard_map/outp/pallas_call | solution.py:427

commit v5 on v4

--- a/solution.py
+++ b/solution.py
@@ -37,8 +37,8 @@
 
 
 PIECES = (
-    ('dq', 'dq', False, 320, 0, 768, 96),
-    ('dkv', 'dkv', False, 320, 0, 288, 96),
+    ('dq', 'dq', False, 320, 0, 768, 112),
+    ('dkv', 'dkv', False, 320, 0, 288, 112),
     ('uq0', 'uq', False, 96, 0, 768, 32),
     ('ukv0', 'ukv', True, 32, 0, 1024, 384),
     ('uq1', 'uq', False, 96, 768, 1536, 32),
@@ -53,19 +53,21 @@
 PIDX = {p[0]: i for i, p in enumerate(PIECES)}
 SPLIT = ('S1a', 'S1b', 'S2a', 'S2b', 'S3a', 'S3b')
 KINDS = ('XE', 'YE', 'XS', 'YS', 'S0', 'Z1', 'Z2', 'DY', 'DX', 'Z3', 'S1', 'S2', 'S3') + SPLIT
-KIDX = {k: i for i, k in enumerate(KINDS)}
+RSEM = {'XE': 0, 'YE': 0, 'XS': 1, 'YS': 1, 'Z1': 2, 'Z2': 3, 'DY': 4, 'DX': 5, 'Z3': 5, 'S0': 6, 'S1': 6, 'S2': 6, 'S3': 6}
+RSEM_SPLIT = dict(RSEM, Z3=7, S1a=8, S1b=8, S2a=9, S2b=9, S3a=10, S3b=10)
+SPLIT_ARRS = ('dq', 'dkv')
 GROUPS = {'dq': ('dq',), 'dkv': ('dkv',), 'U0': ('uq0', 'ukv0'), 'U1': ('uq1', 'ukv1'), 'U2': ('uq2', 'ukv2'),
           'O0': ('o0',), 'O1': ('o1',), 'O2': ('o2',), 'O3': ('o3',)}
 STAGES = {
     'st0': ((), ('XE', 'YE', 'XS', 'YS', 'S0')),
-    'st1': (('XE', 'YE'), ('Z1', 'Z2', 'DY')),
-    'st2': (('XS', 'YS'), ('DX',)),
+    'st1': (('XYE',), ('Z1', 'Z2', 'DY')),
+    'st2': (('XYS',), ('DX',)),
     'st4x': (('Z1',), ('S1',)),
     'st3': (('DY',), ('Z3',)),
     'st4y': (('Z2',), ('S2',)),
-    'st5': (('DX', 'Z3'), ('S3',)),
-    'fin': (('S0', 'S1', 'S2', 'S3'), ()),
-    'st2d': (('XS', 'YS'), ('DX', 'S1a', 'S2a')),
+    'st5': (('DXZ',), ('S3',)),
+    'fin': (('SS',), ()),
+    'st2d': (('XYS',), ('DX', 'S1a', 'S2a')),
     'st4xd': (('Z1',), ('S1b',)),
     'st4yd': (('Z2',), ('S2b',)),
     'st5a': (('DX',), ('S3a',)),
@@ -74,41 +76,39 @@
 }
 SCHED = {
     'stats0': (('st0', 'dq'),),
-    'norm0': (('st0', 'dkv'),),
-    'part0': (('st1', 'dq'), ('recv', 'dq', 'S0'), ('recv', 'dkv', 'S0')),
-    'part3': (('st0', 'U0'),),
-    'part4': (('st2d', 'dq'), ('st4xd', 'dq'), ('recv', 'dq', 'S1a+S1b'), ('st1', 'dkv'), ('st2d', 'dkv'), ('st4xd', 'dkv'), ('st3', 'dq'), ('st4yd', 'dq'), ('st0', 'U1'), ('recv', 'dkv', 'S1a+S1b')),
-    'part5': (('st1', 'U0'),),
+    'norm1': (('st0', 'dkv'),),
+    'part0': (('recv', 'dq', 'S0'), ('recv', 'dkv', 'S0')),
+    'part1': (('st1', 'dq'),),
+    'part3': (('st2d', 'dq'),),
+    'part4': (('st4xd', 'dq'), ('st1', 'dkv'), ('recv', 'dq', 'S1a+S1b'), ('st2d', 'dkv'), ('st0', 'U0'), ('st4xd', 'dkv'), ('st3', 'dq'), ('st4yd', 'dq'), ('st5a', 'dq'), ('st0', 'U1'), ('recv', 'dkv', 'S1a+S1b'), ('st3', 'dkv')),
+    'part5': (('st4yd', 'dkv'), ('st5a', 'dkv'), ('st1', 'U0')),
     'part6': (('st2', 'U0'),),
-    'part7': (('st5a', 'dq'), ('st3', 'dkv'), ('st4yd', 'dkv')),
-    'part8': (('st5b', 'dq'), ('find', 'dq'), ('st5a', 'dkv'), ('st0', 'U2'), ('recv', 'dq', 'S2a+S2b'), ('recv', 'dkv', 'S2a+S2b'), ('st4x', 'U0')),
-    'part10': (('st1', 'U1'),),
-    'part11': (('st5b', 'dkv'), ('find', 'dkv')),
-    'd0': (('recv', 'dq', 'S3a+S3b'), ('recv', 'dkv', 'S3a+S3b')),
-    'd1': (('st3', 'U0'), ('st4y', 'U0'), ('st2', 'U1')),
-    'd2': (('st4x', 'U1'), ('st0', 'O0')),
-    'd3': (('st1', 'U2'),),
-    's0': (('st5', 'U0'), ('st2', 'U2'), ('fin', 'U0'), ('st3', 'U1'), ('st4y', 'U1')),
-    's1': (('st4x', 'U2'), ('st0', 'O1')),
-    's2': (('st1', 'O0'),),
-    's3': (('st5', 'U1'), ('st2', 'O0')),
-    's4': (('fin', 'U1'), ('st3', 'U2'), ('st4y', 'U2'), ('st0', 'O2')),
-    's5': (('st4x', 'O0'), ('st1', 'O1')),
-    's6': (('st2', 'O1'),),
-    's7': (('st5', 'U2'), ('st3', 'O0'), ('st4y', 'O0')),
-    's8': (('fin', 'U2'), ('st4x', 'O1'), ('st0', 'O3')),
-    's9': (('st1', 'O2'), ('st2', 'O2')),
-    's10': (('st5', 'O0'), ('st3', 'O1'), ('st4y', 'O1')),
-    's11': (('fin', 'O0'),),
-    's12': (('st4x', 'O2'), ('st1', 'O3')),
-    's13': (('st3', 'O2'), ('st4y', 'O2'), ('st2', 'O3')),
-    's14': (('st5', 'O1'),),
-    's15': (('fin', 'O1'), ('st4x', 'O3'), ('st3', 'O3')),
-    's16': (('st4y', 'O3'),),
-    's17': (('st5', 'O2'),),
-    's18': (('fin', 'O2'),),
+    'part8': (('st0', 'U2'), ('recv', 'dq', 'S2a+S2b'), ('recv', 'dkv', 'S2a+S2b')),
+    'part9': (('st5b', 'dq'), ('st1', 'U1')),
+    'part10': (('st5b', 'dkv'),),
+    'd0': (('st4x', 'U0'), ('st2', 'U1'), ('recv', 'dq', 'S3a+S3b'), ('recv', 'dkv', 'S3a+S3b')),
+    'd1': (('st3', 'U0'), ('st4y', 'U0')),
+    'd2': (('st4x', 'U1'), ('st1', 'U2')),
+    's0': (('st2', 'U2'), ('st0', 'O0'), ('st5', 'U0'), ('fin', 'U0'), ('st3', 'U1'), ('st4y', 'U1')),
+    's1': (('st4x', 'U2'), ('st3', 'U2'), ('st0', 'O1')),
+    's2': (('st4y', 'U2'),),
+    's3': (('st5', 'U1'), ('st1', 'O0')),
+    's4': (('st5', 'U2'), ('st2', 'O0'), ('fin', 'U1')),
+    's5': (('fin', 'U2'), ('st4x', 'O0'), ('st1', 'O1')),
+    's6': (('st2', 'O1'), ('st0', 'O2')),
+    's7': (('st3', 'O0'), ('st4y', 'O0')),
+    's8': (('st4x', 'O1'),),
+    's9': (('st3', 'O1'), ('st4y', 'O1'), ('st0', 'O3')),
+    's10': (('st1', 'O2'),),
+    's11': (('st5', 'O0'), ('st2', 'O2')),
+    's12': (('st5', 'O1'), ('st1', 'O3')),
+    's13': (('fin', 'O0'), ('fin', 'O1'), ('st4x', 'O2'), ('st2', 'O3')),
+    's14': (('st3', 'O2'), ('st4y', 'O2')),
+    's16': (('st4x', 'O3'), ('st3', 'O3')),
+    's17': (('st4y', 'O3'),),
+    's18': (('st5', 'O2'),),
     's19': (('st5', 'O3'),),
-    'end': (('fin', 'O3'),),
+    'end': (('fin', 'O2'), ('fin', 'O3')),
     'stats1': (),
 }
 
@@ -117,7 +117,7 @@
                  attn_hbm, wo_hbm, c_hbm, r_hbm,
                  xa, wdq, wdkv, wuq, wukv, ostage, g1b, gqb, gkvb, accq, acck, inv, cqT, cbuf, cT, rbuf, rT,
                  wqT, wk, wvT, qT, kbuf, vT, obuf,
-                 ssem, rsem, lsem, gss, grs, xsem, osem, csem):
+                 ssem, rsem, dsem, lsem, gss, grs, xsem, osem, csem):
     z, f = lax.axis_index('dp'), lax.axis_index('fsdp')
     core, xx, yy = f % 2, (f // 2) % 2, f // 4
 
@@ -158,9 +158,32 @@
             to = dev[to]
             r1, c1 = region(piece, shard, part, True)
             s_ref = d_ref = buf[arr].at[r1, c1]
-        i, j = PIDX[name], KIDX[kind]
-        return pltpu.make_async_remote_copy(src_ref=s_ref, dst_ref=d_ref, send_sem=ssem.at[i, j], recv_sem=rsem.at[i, j],
+        return pltpu.make_async_remote_copy(src_ref=s_ref, dst_ref=d_ref, send_sem=ssem.at[PIDX[name]], recv_sem=rsem_of(name, kind),
                                             device_id=to, device_id_type=MESH)
+
+    def rsem_of(name, kind):
+        if PIECES[PIDX[name]][1] in SPLIT_ARRS:
+            return dsem.at[PIDX[name], RSEM_SPLIT[kind]]
+        return rsem.at[PIDX[name] - 2, RSEM[kind]]
+
+    def take(name, n, sem, rows_too=True):
+        _, arr, bycol, rows, c0, nc, e = PIECES[PIDX[name]]
+        ref = buf[arr]
+        if bycol:
+            k = max(1, -(-n // nc))
+            assert n % k == 0
+            part = ref.at[pl.ds(0, rows * k), pl.ds(c0, n // k)]
+        else:
+            part = ref.at[pl.ds(0, n), pl.ds(c0, nc)]
+        pltpu.make_async_copy(part, part, sem).wait()
+
+    def units(name, what):
+        _, arr, bycol, rows, c0, nc, e = PIECES[PIDX[name]]
+        n = nc if bycol else rows
+        return {'XYE': 2 * e, 'XYS': 2 * (n - 2 * e), 'Z1': e, 'Z2': e, 'DY': e, 'DX': n - 2 * e, 'Z3': e, 'DXZ': n - e, 'SS': 4 * n,
+                'S0': n, 'S1': n, 'S2': n, 'S3': n, 'sent': 7 * n}[what]
+
+    FIRST = {'XYE': 'XE', 'XYS': 'XS', 'DXZ': 'DX', 'SS': 'S0'}
 
     def local(name):
         piece = PIECES[PIDX[name]]
@@ -176,14 +199,16 @@
     def recv(names, *kinds):
         for k in kinds:
             for n in names:
-                copy(n, k).wait_recv()
+                k = {'S1a+S1b': 'S1', 'S2a+S2b': 'S2', 'S3a+S3b': 'S3'}.get(k, k)
+                first = k + 'a' if k in ('S1', 'S2', 'S3') else FIRST.get(k, k)
+                take(n, units(n, k), rsem_of(n, first))
 
     def comm(todo):
         for op in todo:
             stage, piece = op[0], op[1]
             names = GROUPS[piece]
             if stage == 'recv':
-                recv(names, *op[2].split('+'))
+                recv(names, op[2])
                 continue
             if stage == 'st0' and piece == 'O0':
                 stage_o.wait()
@@ -199,12 +224,18 @@
                         local(n).wait()
 
     def at(seg, i):
-        for name, todo in SCHED.items():
-            if name.startswith(seg) and name[len(seg):].isdigit() and todo:
-                @pl.when(i == int(name[len(seg):]))
-                def _(todo=todo, name=name):
-                    with jax.named_scope('comm_' + name):
-                        comm(todo)
+        marks = sorted((int(n[len(seg):]), n) for n in SCHED if n.startswith(seg) and n[len(seg):].isdigit() and SCHED[n])
+
+        def tree(ms):
+            if len(ms) == 1:
+                @pl.when(i == ms[0][0])
+                def _():
+                    with jax.named_scope('comm_' + ms[0][1]):
+                        comm(SCHED[ms[0][1]])
+            elif ms:
+                h = len(ms) // 2
+                lax.cond(i < ms[h][0], lambda: tree(ms[:h]), lambda: tree(ms[h:]))
+        tree(marks)
 
     for i in range(T // TA):
         pltpu.make_async_copy(x_hbm.at[pl.ds(i * TA, TA)], xa.at[pl.ds(i * TA, TA)], xsem.at[i]).start()
@@ -218,15 +249,11 @@
         pl.semaphore_signal(barrier, inc=1, device_id=dev['Z'], device_id_type=MESH)
         pl.semaphore_wait(barrier, 8)
 
-    gains = []
     for j, (gs, gb) in enumerate(((g1_s, g1b), (gq_s, gqb), (gkv_s, gkvb))):
-        for i, p in enumerate(plane):
-            gains.append(pltpu.make_async_remote_copy(src_ref=gs, dst_ref=gb.at[f], send_sem=gss.at[j, i], recv_sem=grs.at[j, i],
-                                                      device_id=(z, p), device_id_type=MESH))
-            gains[-1].start()
-        own = pltpu.make_async_copy(gs, gb.at[f], gss.at[j, 7])
-        own.start()
-        gains.append(own)
+        for p in plane:
+            pltpu.make_async_remote_copy(src_ref=gs, dst_ref=gb.at[f], send_sem=gss.at[j], recv_sem=grs.at[j],
+                                         device_id=(z, p), device_id_type=MESH).start()
+        pltpu.make_async_copy(gs, gb.at[f], grs.at[j]).start()
     comm(SCHED['stats0'])
 
     def stat_tile(i, _):
@@ -246,8 +273,8 @@
     with jax.named_scope('stats'):
         lax.fori_loop(0, T // TA, stat_tile, 0)
     with jax.named_scope('gains'):
-        for g in gains:
-            g.wait()
+        for j, gb in enumerate((g1b, gqb, gkvb)):
+            pltpu.make_async_copy(gb, gb, grs.at[j]).wait()
 
     def row_of(gb):
         return jnp.concatenate([gb[i].astype(F32) for i in range(8)], axis=-1)
@@ -380,15 +407,16 @@
     lax.fori_loop(0, STEPS, step, 0)
     with jax.named_scope('fin_O'):
         comm(SCHED['end'])
-    for i in (STEPS - 2, STEPS - 1):
-        out_copy(i).wait()
-    for o in outs:
-        o.wait()
-    for p in PIECES:
-        for k in KINDS:
-            if k in (('S1', 'S2', 'S3') if p[1] in ('dq', 'dkv') else SPLIT):
-                continue
-            copy(p[0], k).wait_send()
+    with jax.named_scope('tail_out'):
+        for i in (STEPS - 2, STEPS - 1):
+            out_copy(i).wait()
+        for o in outs:
+            o.wait()
+    with jax.named_scope('tail_sends'):
+        for j, gb in enumerate((g1b, gqb, gkvb)):
+            pltpu.make_async_copy(gb.at[pl.ds(0, 7)], gb.at[pl.ds(0, 7)], gss.at[j]).wait()
+        for p in PIECES:
+            take(p[0], units(p[0], 'sent'), ssem.at[PIDX[p[0]]])
 
 
 def front(x, gains, ws, cos, sin):
@@ -406,7 +434,7 @@
             V((8, 1, 320), BF16), V((8, 1, 96), BF16), V((8, 1, 32), BF16), V((T, QR), F32), V((T, KR + RD), F32), V((T, 128), F32),
             V((QR, T), BF16), V((T, KR), BF16), V((KR, T), BF16), V((T, RD), BF16), V((T // S, RD, S), BF16),
             V((HG * 96, QR), BF16), V((KR, HG * 64), BF16), V((HG * 64, KR), BF16), V((HG * 128, TC), BF16), V((TC, HG * 64), BF16), V((HG * 64, TC), BF16), V((2, TC, HG * 64), BF16),
-            dma((len(PIECES), len(KINDS))), dma((len(PIECES), len(KINDS))), dma((len(PIECES),)), dma((3, 8)), dma((3, 7)), dma((T // TA,)), dma((3,)), dma((2,)),
+            dma((len(PIECES),)), dma((len(PIECES) - 2, 7)), dma((2, 11)), dma((len(PIECES),)), dma((3,)), dma((3,)), dma((T // TA,)), dma((3,)), dma((2,)),
         ],
         compiler_params=pltpu.CompilerParams(collective_id=0, has_side_effects=True, vmem_limit_bytes=63 << 20),
     )(x, *gains, *ws, *(jnp.asarray(t) for t in tab))

time: 140 us -> 134 us (0.957)
  Pallas kernels: 137 us -> 130 us
    pallas_call x1, Pallas kernels: 102 us -> 95.5 us  [front(): pl.pallas_call(front_kernel, name='front', in_specs=[anyspace] + [vm] * 3...]
where the time goes in v5:
time: 134 us
  Pallas kernels  130 us (97%)
  local copies, waits for them, and re-layouts  3.03 us (2%)
    pallas_call x1, Pallas kernels, front(): pl.pallas_call(front_kernel, name='front', in_specs=[anyspace] + [vm] * 3...  95.5 us
    pallas_call x1, Pallas kernels, outp(): pl.pallas_call(out_kernel, grid=(nt, T // tm), name='outp', in_specs=[pl....  34.7 us

profile of v5, /device:TPU:0, one launch (start us, length us, event | category | flops | bytes accessed | tf_op | source)
XLA Modules:
  0.0 133.9 jit_solution(17052869152971810472)
XLA Ops:
  0.6 1.2 broadcast_in_dim.9.g1_s
  1.9 1.8 %copy.16.dkv_s = bf16[320,288]{1,0:T(8,128)(2,1)} copy(bf16[320,288]{0,1:T(8,128)(2,1)} %param.18) | data formatting | bytes 368640 | tf_op args[5]
  3.7 95.5 %front.1 = (bf16[2048,2560]{1,0:T(8,128)(2,1)}, bf16[2560,2560]{1,0:T(8,128)(2,1)}, bf16[2048,256]{1,0:T(8,128)(2,1)}, bf16[16,32,128]{2,1,0:T(8,128)(2,1)}) custom-call(bf16[2048,2560]{1,0:T(8,128)(2,1)} %bitcast.6, bf16[1,320]{1,0:T(2,128)(2,1)} %broadcast_in_dim.9.g1_s, bf16[1,96]{1,0:T(2,128)(2,1)} %bitcast.8, bf16[1,32]{1,0:T(2,128)(2,1)} %bitcast.9, ...), custom_call_target="tpu_custom_call" | custom-call | tf_op jit(solution)/shard_map/front/pallas_call | solution.py:427
  99.2 34.7 %outp.1 = (bf16[2048,2560]{1,0:T(8,128)(2,1)}, bf16[2048,256]{1,0:T(8,128)(2,1)}, bf16[16,32,128]{2,1,0:T(8,128)(2,1)}) custom-call(bf16[2048,2560]{1,0:T(8,128)(2,1)} %get-tuple-element.10.o_ref, bf16[2560,2560]{1,0:T(8,128)(2,1)} %get-tuple-element.11.w_ref, bf16[2048,2560]{1,0:T(8,128)(2,1)} %bitcast.7, bf16[2048,256]{1,0:T(8,128)(2,1)} %get-tuple-element.12.c_ref, ...), custom_call_target="tpu_custom_call" | custom-call | tf_op jit(solution)/shard_map/outp/pallas_call | solution.py:455

commit v6 on v5

--- a/solution.py
+++ b/solution.py
@@ -37,18 +37,19 @@
 
 
 PIECES = (
-    ('dq', 'dq', False, 320, 0, 768, 112),
-    ('dkv', 'dkv', False, 320, 0, 288, 112),
+    ('dq', 'dq', False, 320, 0, 768, 96),
+    ('dkv', 'dkv', False, 320, 0, 288, 96),
     ('uq0', 'uq', False, 96, 0, 768, 32),
     ('ukv0', 'ukv', True, 32, 0, 1024, 384),
     ('uq1', 'uq', False, 96, 768, 1536, 32),
-    ('ukv1', 'ukv', True, 32, 1024, 2048, 640),
+    ('ukv1', 'ukv', True, 32, 1024, 2048, 512),
     ('uq2', 'uq', False, 96, 2304, 1536, 32),
-    ('ukv2', 'ukv', True, 32, 3072, 2048, 640),
-    ('o0', 'o', False, 320, 0, 640, 112),
-    ('o1', 'o', False, 320, 640, 640, 112),
-    ('o2', 'o', False, 320, 1280, 640, 112),
-    ('o3', 'o', False, 320, 1920, 640, 112),
+    ('ukv2', 'ukv', True, 32, 3072, 2048, 512),
+    ('o0', 'o', False, 320, 0, 512, 96),
+    ('o1', 'o', False, 320, 512, 512, 96),
+    ('o2', 'o', False, 320, 1024, 512, 96),
+    ('o3', 'o', False, 320, 1536, 512, 96),
+    ('o4', 'o', False, 320, 2048, 512, 96),
 )
 PIDX = {p[0]: i for i, p in enumerate(PIECES)}
 SPLIT = ('S1a', 'S1b', 'S2a', 'S2b', 'S3a', 'S3b')
@@ -56,8 +57,8 @@
 RSEM = {'XE': 0, 'YE': 0, 'XS': 1, 'YS': 1, 'Z1': 2, 'Z2': 3, 'DY': 4, 'DX': 5, 'Z3': 5, 'S0': 6, 'S1': 6, 'S2': 6, 'S3': 6}
 RSEM_SPLIT = dict(RSEM, Z3=7, S1a=8, S1b=8, S2a=9, S2b=9, S3a=10, S3b=10)
 SPLIT_ARRS = ('dq', 'dkv')
-GROUPS = {'dq': ('dq',), 'dkv': ('dkv',), 'U0': ('uq0', 'ukv0'), 'U1': ('uq1', 'ukv1'), 'U2': ('uq2', 'ukv2'),
-          'O0': ('o0',), 'O1': ('o1',), 'O2': ('o2',), 'O3': ('o3',)}
+GROUPS = {'K': ('dkv',), 'D': ('dq',), 'U0': ('uq0', 'ukv0'), 'U1': ('uq1', 'ukv1'), 'U2': ('uq2', 'ukv2'),
+          'O0': ('o0',), 'O1': ('o1',), 'O2': ('o2',), 'O3': ('o3',), 'O4': ('o4',)}
 STAGES = {
     'st0': ((), ('XE', 'YE', 'XS', 'YS', 'S0')),
     'st1': (('XYE',), ('Z1', 'Z2', 'DY')),
@@ -75,42 +76,46 @@
     'find': ((), ()),
 }
 SCHED = {
-    'stats0': (('st0', 'dq'),),
-    'norm1': (('st0', 'dkv'),),
-    'part0': (('recv', 'dq', 'S0'), ('recv', 'dkv', 'S0')),
-    'part1': (('st1', 'dq'),),
-    'part3': (('st2d', 'dq'),),
-    'part4': (('st4xd', 'dq'), ('st1', 'dkv'), ('recv', 'dq', 'S1a+S1b'), ('st2d', 'dkv'), ('st0', 'U0'), ('st4xd', 'dkv'), ('st3', 'dq'), ('st4yd', 'dq'), ('st5a', 'dq'), ('st0', 'U1'), ('recv', 'dkv', 'S1a+S1b'), ('st3', 'dkv')),
-    'part5': (('st4yd', 'dkv'), ('st5a', 'dkv'), ('st1', 'U0')),
-    'part6': (('st2', 'U0'),),
-    'part8': (('st0', 'U2'), ('recv', 'dq', 'S2a+S2b'), ('recv', 'dkv', 'S2a+S2b')),
-    'part9': (('st5b', 'dq'), ('st1', 'U1')),
-    'part10': (('st5b', 'dkv'),),
-    'd0': (('st4x', 'U0'), ('st2', 'U1'), ('recv', 'dq', 'S3a+S3b'), ('recv', 'dkv', 'S3a+S3b')),
-    'd1': (('st3', 'U0'), ('st4y', 'U0')),
+    'stats0': (('st0', 'K'),),
+    'stats1': (('st0', 'D'),),
+    'norm1': (('st1', 'K'),),
+    'part0': (('st2d', 'K'), ('recv', 'K', 'S0'), ('recv', 'D', 'S0')),
+    'part2': (('st4xd', 'K'), ('st0', 'U0'), ('st1', 'D')),
+    'k0': (('recv', 'K', 'S1a+S1b'),),
+    'k2': (('st2d', 'D'), ('st3', 'K'), ('st4yd', 'K'), ('st4xd', 'D'), ('recv', 'K', 'S2a+S2b'), ('st5a', 'K')),
+    'k3': (('st1', 'U0'),),
+    'k4': (('st5b', 'K'), ('st2', 'U0'), ('recv', 'K', 'S3a+S3b'), ('st0', 'U1'), ('st0', 'U2')),
+    'k5': (('st3', 'D'), ('st4yd', 'D'), ('st4x', 'U0')),
+    'q0': (('st5a', 'D'), ('recv', 'D', 'S1a+S1b')),
+    'q1': (('st3', 'U0'), ('st4y', 'U0')),
+    'q4': (('st1', 'U1'), ('st5b', 'D'), ('recv', 'D', 'S2a+S2b')),
+    'q6': (('st5', 'U0'),),
+    'd0': (('st2', 'U1'), ('recv', 'D', 'S3a+S3b')),
+    'd1': (('fin', 'U0'),),
     'd2': (('st4x', 'U1'), ('st1', 'U2')),
-    's0': (('st2', 'U2'), ('st0', 'O0'), ('st5', 'U0'), ('fin', 'U0'), ('st3', 'U1'), ('st4y', 'U1')),
-    's1': (('st4x', 'U2'), ('st3', 'U2'), ('st0', 'O1')),
-    's2': (('st4y', 'U2'),),
-    's3': (('st5', 'U1'), ('st1', 'O0')),
-    's4': (('st5', 'U2'), ('st2', 'O0'), ('fin', 'U1')),
-    's5': (('fin', 'U2'), ('st4x', 'O0'), ('st1', 'O1')),
-    's6': (('st2', 'O1'), ('st0', 'O2')),
+    's0': (('st2', 'U2'),),
+    's1': (('st3', 'U1'), ('st4y', 'U1'), ('st4x', 'U2'), ('st0', 'O0'), ('st0', 'O1')),
+    's2': (('st3', 'U2'), ('st4y', 'U2')),
+    's3': (('st5', 'U1'),),
+    's4': (('st1', 'O0'), ('fin', 'U1')),
+    's5': (('st5', 'U2'), ('st2', 'O0'), ('st1', 'O1')),
+    's6': (('fin', 'U2'), ('st4x', 'O0'), ('st2', 'O1'), ('st0', 'O2')),
     's7': (('st3', 'O0'), ('st4y', 'O0')),
-    's8': (('st4x', 'O1'),),
-    's9': (('st3', 'O1'), ('st4y', 'O1'), ('st0', 'O3')),
-    's10': (('st1', 'O2'),),
-    's11': (('st5', 'O0'), ('st2', 'O2')),
-    's12': (('st5', 'O1'), ('st1', 'O3')),
-    's13': (('fin', 'O0'), ('fin', 'O1'), ('st4x', 'O2'), ('st2', 'O3')),
-    's14': (('st3', 'O2'), ('st4y', 'O2')),
-    's16': (('st4x', 'O3'), ('st3', 'O3')),
-    's17': (('st4y', 'O3'),),
-    's18': (('st5', 'O2'),),
-    's19': (('st5', 'O3'),),
-    'end': (('fin', 'O2'), ('fin', 'O3')),
-    'stats1': (),
+    's8': (('st4x', 'O1'), ('st3', 'O1'), ('st0', 'O3')),
+    's9': (('st5', 'O0'), ('st4y', 'O1'), ('st1', 'O2')),
+    's10': (('fin', 'O0'), ('st5', 'O1'), ('st2', 'O2')),
+    's11': (('fin', 'O1'), ('st4x', 'O2'), ('st1', 'O3')),
+    's12': (('st2', 'O3'), ('st0', 'O4')),
+    's13': (('st3', 'O2'), ('st4y', 'O2'), ('st4x', 'O3')),
+    's14': (('st3', 'O3'), ('st4y', 'O3')),
+    's15': (('st5', 'O2'), ('st1', 'O4')),
+    's16': (('fin', 'O2'), ('st5', 'O3'), ('st2', 'O4')),
+    's17': (('fin', 'O3'), ('st4x', 'O4'), ('st3', 'O4')),
+    's18': (('st4y', 'O4'),),
+    's19': (('st5', 'O4'),),
+    'end': (('fin', 'O4'),),
 }
+SWAPPED = ('dkv', 'uq1', 'ukv1', 'o0', 'o3', 'o4')
 
 
 def front_kernel(x_hbm, g1_s, gq_s, gkv_s, dq_s, dkv_s, uq_s, ukv_s, o_s, cos_ref, sin_ref, cosT_ref, sinT_ref,
@@ -155,6 +160,8 @@
                                'DX': (fy, 'S', 'X'), 'S1': (fx, 'A', 'S'), 'S2': (fy, 'A', 'S'), 'S3': (fd, 'A', 'S'),
                                'S1a': (fx, 'B', 'S'), 'S1b': (fx, 'M', 'S'), 'S2a': (fy, 'B', 'S'), 'S2b': (fy, 'M', 'S'),
                                'S3a': (fd, 'B', 'S'), 'S3b': (fd, 'M', 'S')}[kind]
+            if name in SWAPPED and kind in ('DX', 'DY'):
+                shard, to = {'DX': (fx, 'Y'), 'DY': (fy, 'X')}[kind]
             to = dev[to]
             r1, c1 = region(piece, shard, part, True)
             s_ref = d_ref = buf[arr].at[r1, c1]
@@ -220,7 +227,7 @@
                     local(n).start()
             if stage in ('fin', 'find'):
                 for n in names:
-                    if piece not in ('dq', 'dkv'):
+                    if piece not in ('K', 'D'):
                         local(n).wait()
 
     def at(seg, i):
@@ -261,10 +268,6 @@
         def _():
             comm(SCHED['stats1'])
         pltpu.make_async_copy(x_hbm.at[pl.ds(i * TA, TA)], xa.at[pl.ds(i * TA, TA)], xsem.at[i]).wait()
-        zero = jnp.zeros((TA, 128), F32)
-        for j in range(QR // 128):
-            accq[pl.ds(pl.multiple_of(i * TA, TA), TA), 128 * j:128 * j + 128] = zero
-        acck[pl.ds(pl.multiple_of(i * TA, TA), TA), :] = jnp.zeros((TA, KR + RD), F32)
         for h in range(TA // 64):
             rows = pl.ds(pl.multiple_of(i * TA + h * 64, 64), 64)
             inv[rows, :] = jnp.broadcast_to(rms(xa[rows, :].astype(F32)), (64, 128))
@@ -291,47 +294,78 @@
                 xa[rows, cols] = (xa[rows, cols].astype(F32) * scale * g1[:, cols]).astype(BF16)
         return 0
 
-    def part(i, _):
+    def quarter_cols(dy, dx):
+        quarter = ((yy + dy) % 2) * 2 + (xx + dx) % 2
+        return pl.ds(pl.multiple_of(quarter * 640, 128), 640)
+
+    def own_part(i, _):
         at('part', i)
-        which, t = i // 4, i % 4
-        quarter = ((yy + which // 2) % 2) * 2 + (xx + which % 2) % 2
-        cols = pl.ds(pl.multiple_of(quarter * 640, 128), 640)
-        rows = pl.ds(pl.multiple_of(t * 512, 512), 512)
+        cols, rows = quarter_cols(0, 0), pl.ds(pl.multiple_of(i * 512, 512), 512)
         a = xa[rows, cols]
-        accq[rows, :] += dot(a, wdq[cols, :])
-        acck[rows, :] += dot(a, wdkv[cols, :])
+        accq[rows, :] = dot(a, wdq[cols, :])
+        acck[rows, :] = dot(a, wdkv[cols, :])
+        return 0
+
+    def kv_part(i, _):
+        at('k', i)
+        q = i // 2 + 1
+        cols, rows = quarter_cols(q // 2, q % 2), pl.ds(pl.multiple_of((i % 2) * 1024, 1024), 1024)
+        acck[rows, :] += dot(xa[rows, cols], wdkv[cols, :])
+        return 0
+
+    def q_part(x_not_y, i, _):
+        at('q', i if x_not_y else i + 4)
+        if x_not_y:
+            finish_kv(2 * i)
+            finish_kv(2 * i + 1)
+        cols, rows = quarter_cols(0, 1) if x_not_y else quarter_cols(1, 0), pl.ds(pl.multiple_of(i * 512, 512), 512)
+        accq[rows, :] += dot(xa[rows, cols], wdq[cols, :])
         return 0
 
     cos2 = jnp.concatenate([cos_ref[...]] * (TA // S), axis=0)
     sin2 = jnp.concatenate([sin_ref[...]] * (TA // S), axis=0)
 
+    def finish_kv(i):
+        rows = pl.ds(pl.multiple_of(i * TA, TA), TA)
+        kd = acck[rows, :]
+        kc = kd[:, :KR]
+        c = (kc * rms(kc) * gkv).astype(BF16)
+        cbuf[rows, :] = c
+        cT[:, rows] = c.T
+        lo, hi = kd[:, KR:KR + 16], kd[:, KR + 16:]
+        r = jnp.concatenate([lo * cos2 - hi * sin2, hi * cos2 + lo * sin2], axis=-1).astype(BF16)
+        rbuf[rows, :] = r
+        for h in range(TA // S):
+            rT[i * (TA // S) + h] = r[h * S:h * S + S].T
+
+    def finish_q(i):
+        rows = pl.ds(pl.multiple_of(i * TA, TA), TA)
+        qd = accq[rows, :]
+        cqT[:, rows] = (qd * rms(qd) * gq).astype(BF16).T
+
     def last_part():
         cols = pl.ds(pl.multiple_of((fd // 2) * 640, 128), 640)
 
         def tile(i, _):
             pl.when(i % 2 == 0)(functools.partial(at, 'd', i // 2))
-            rows = pl.ds(pl.multiple_of(i * TA, TA), TA)
-            a = xa[rows, cols]
-            qd = accq[rows, :] + dot(a, wdq[cols, :])
-            kd = acck[rows, :] + dot(a, wdkv[cols, :])
-            cqT[:, rows] = (qd * rms(qd) * gq).astype(BF16).T
-            kc = kd[:, :KR]
-            c = (kc * rms(kc) * gkv).astype(BF16)
-            cbuf[rows, :] = c
-            cT[:, rows] = c.T
-            lo, hi = kd[:, KR:KR + 16], kd[:, KR + 16:]
-            rbuf[rows, :] = jnp.concatenate([lo * cos2 - hi * sin2, hi * cos2 + lo * sin2], axis=-1).astype(BF16)
-            for h in range(TA // S):
-                rT[i * (TA // S) + h] = rbuf[pl.ds(pl.multiple_of(i * TA + h * S, S), S), :].T
+            finish_q(jnp.maximum(i - 1, 0))
+            rows = pl.ds(pl.multiple_of(jnp.minimum(i, T // TA - 1) * TA, TA), TA)
+            accq[rows, :] += dot(xa[rows, cols], wdq[cols, :])
             return 0
-        lax.fori_loop(0, T // TA, tile, 0)
+        lax.fori_loop(0, T // TA + 1, tile, 0)
 
     with jax.named_scope('norm'):
         lax.fori_loop(0, T // TA, norm_tile, 0)
     for n in ('dq', 'dkv'):
         local(n).wait()
-    with jax.named_scope('parts'):
-        lax.fori_loop(0, 12, part, 0)
+    with jax.named_scope('own'):
+        lax.fori_loop(0, 4, own_part, 0)
+    with jax.named_scope('kv'):
+        lax.fori_loop(0, 6, kv_part, 0)
+    with jax.named_scope('qx'):
+        lax.fori_loop(0, 4, functools.partial(q_part, True), 0)
+    with jax.named_scope('qy'):
+        lax.fori_loop(0, 4, functools.partial(q_part, False), 0)
     with jax.named_scope('last'):
         last_part()
     outs = [pltpu.make_async_copy(cbuf, c_hbm, csem.at[0]), pltpu.make_async_copy(rT, r_hbm, csem.at[1])]

time: 134 us -> 133 us (level)
  no operation moved by 1% of the time
where the time goes in v6:
time: 133 us
  Pallas kernels  129 us (97%)
  local copies, waits for them, and re-layouts  3.03 us (2%)
    pallas_call x1, Pallas kernels, front(): pl.pallas_call(front_kernel, name='front', in_specs=[anyspace] + [vm] * 3...  94.4 us
    pallas_call x1, Pallas kernels, outp(): pl.pallas_call(out_kernel, grid=(nt, T // tm), name='outp', in_specs=[pl....  34.7 us

profile of v6, /device:TPU:0, one launch (start us, length us, event | category | flops | bytes accessed | tf_op | source)
XLA Modules:
  0.0 132.7 jit_solution(13403012147882274937)
XLA Ops:
  0.6 1.2 broadcast_in_dim.9.g1_s
  1.9 1.8 %copy.16.dkv_s = bf16[320,288]{1,0:T(8,128)(2,1)} copy(bf16[320,288]{0,1:T(8,128)(2,1)} %param.18) | data formatting | bytes 368640 | tf_op args[5]
  3.7 94.4 %front.1 = (bf16[2048,2560]{1,0:T(8,128)(2,1)}, bf16[2560,2560]{1,0:T(8,128)(2,1)}, bf16[2048,256]{1,0:T(8,128)(2,1)}, bf16[16,32,128]{2,1,0:T(8,128)(2,1)}) custom-call(bf16[2048,2560]{1,0:T(8,128)(2,1)} %bitcast.6, bf16[1,320]{1,0:T(2,128)(2,1)} %broadcast_in_dim.9.g1_s, bf16[1,96]{1,0:T(2,128)(2,1)} %bitcast.8, bf16[1,32]{1,0:T(2,128)(2,1)} %bitcast.9, ...), custom_call_target="tpu_custom_call" | custom-call | tf_op jit(solution)/shard_map/front/pallas_call | solution.py:461
  98.1 34.7 %outp.1 = (bf16[2048,2560]{1,0:T(8,128)(2,1)}, bf16[2048,256]{1,0:T(8,128)(2,1)}, bf16[16,32,128]{2,1,0:T(8,128)(2,1)}) custom-call(bf16[2048,2560]{1,0:T(8,128)(2,1)} %get-tuple-element.10.o_ref, bf16[2560,2560]{1,0:T(8,128)(2,1)} %get-tuple-element.11.w_ref, bf16[2048,2560]{1,0:T(8,128)(2,1)} %bitcast.7, bf16[2048,256]{1,0:T(8,128)(2,1)} %get-tuple-element.12.c_ref, ...), custom_call_target="tpu_custom_call" | custom-call | tf_op jit(solution)/shard_map/outp/pallas_call | solution.py:489

commit v7 on v6

--- a/solution.py
+++ b/solution.py
@@ -37,19 +37,19 @@
 
 
 PIECES = (
-    ('dq', 'dq', False, 320, 0, 768, 96),
-    ('dkv', 'dkv', False, 320, 0, 288, 96),
-    ('uq0', 'uq', False, 96, 0, 768, 32),
-    ('ukv0', 'ukv', True, 32, 0, 1024, 384),
-    ('uq1', 'uq', False, 96, 768, 1536, 32),
-    ('ukv1', 'ukv', True, 32, 1024, 2048, 512),
-    ('uq2', 'uq', False, 96, 2304, 1536, 32),
-    ('ukv2', 'ukv', True, 32, 3072, 2048, 512),
-    ('o0', 'o', False, 320, 0, 512, 96),
-    ('o1', 'o', False, 320, 512, 512, 96),
+    ('dq', 'dq', False, 320, 0, 768, 112),
+    ('dkv', 'dkv', False, 320, 0, 288, 128),
+    ('uq0', 'uq', False, 96, 0, 1536, 32),
+    ('ukv0', 'ukv', True, 32, 0, 2048, 768),
+    ('uq1', 'uq', False, 96, 1536, 1536, 32),
+    ('ukv1', 'ukv', True, 32, 2048, 2048, 768),
+    ('uq2', 'uq', False, 96, 3072, 768, 16),
+    ('ukv2', 'ukv', True, 32, 4096, 1024, 256),
+    ('o0', 'o', False, 320, 0, 512, 128),
+    ('o1', 'o', False, 320, 512, 512, 128),
     ('o2', 'o', False, 320, 1024, 512, 96),
-    ('o3', 'o', False, 320, 1536, 512, 96),
-    ('o4', 'o', False, 320, 2048, 512, 96),
+    ('o3', 'o', False, 320, 1536, 512, 80),
+    ('o4', 'o', False, 320, 2048, 512, 64),
 )
 PIDX = {p[0]: i for i, p in enumerate(PIECES)}
 SPLIT = ('S1a', 'S1b', 'S2a', 'S2b', 'S3a', 'S3b')
@@ -76,46 +76,48 @@
     'find': ((), ()),
 }
 SCHED = {
-    'stats0': (('st0', 'K'),),
-    'stats1': (('st0', 'D'),),
+    'stats0': (('st0', 'K'), ('st0', 'D')),
     'norm1': (('st1', 'K'),),
-    'part0': (('st2d', 'K'), ('recv', 'K', 'S0'), ('recv', 'D', 'S0')),
-    'part2': (('st4xd', 'K'), ('st0', 'U0'), ('st1', 'D')),
-    'k0': (('recv', 'K', 'S1a+S1b'),),
-    'k2': (('st2d', 'D'), ('st3', 'K'), ('st4yd', 'K'), ('st4xd', 'D'), ('recv', 'K', 'S2a+S2b'), ('st5a', 'K')),
-    'k3': (('st1', 'U0'),),
-    'k4': (('st5b', 'K'), ('st2', 'U0'), ('recv', 'K', 'S3a+S3b'), ('st0', 'U1'), ('st0', 'U2')),
-    'k5': (('st3', 'D'), ('st4yd', 'D'), ('st4x', 'U0')),
+    'norm2': (('st2d', 'K'),),
+    'part0': (('recv', 'K', 'S0'), ('recv', 'D', 'S0')),
+    'part2': (('st4xd', 'K'), ('st1', 'D')),
+    'k0': (('st0', 'U0'), ('recv', 'K', 'S1a+S1b')),
+    'k1': (('st2d', 'D'),),
+    'k2': (('st3', 'K'), ('st4yd', 'K'), ('st5a', 'K'), ('recv', 'K', 'S2a+S2b'), ('st4xd', 'D')),
+    'k4': (('st3', 'D'), ('st5b', 'K'), ('st4yd', 'D'), ('st1', 'U0'), ('recv', 'K', 'S3a+S3b'), ('st0', 'U1')),
+    'k5': (('st2', 'U0'),),
     'q0': (('st5a', 'D'), ('recv', 'D', 'S1a+S1b')),
-    'q1': (('st3', 'U0'), ('st4y', 'U0')),
-    'q4': (('st1', 'U1'), ('st5b', 'D'), ('recv', 'D', 'S2a+S2b')),
-    'q6': (('st5', 'U0'),),
+    'q1': (('st5b', 'D'),),
+    'q4': (('st4x', 'U0'), ('st3', 'U0'), ('recv', 'D', 'S2a+S2b')),
+    'q5': (('st1', 'U1'),),
+    'q7': (('st4y', 'U0'), ('st0', 'U2')),
     'd0': (('st2', 'U1'), ('recv', 'D', 'S3a+S3b')),
-    'd1': (('fin', 'U0'),),
-    'd2': (('st4x', 'U1'), ('st1', 'U2')),
-    's0': (('st2', 'U2'),),
-    's1': (('st3', 'U1'), ('st4y', 'U1'), ('st4x', 'U2'), ('st0', 'O0'), ('st0', 'O1')),
-    's2': (('st3', 'U2'), ('st4y', 'U2')),
-    's3': (('st5', 'U1'),),
-    's4': (('st1', 'O0'), ('fin', 'U1')),
-    's5': (('st5', 'U2'), ('st2', 'O0'), ('st1', 'O1')),
-    's6': (('fin', 'U2'), ('st4x', 'O0'), ('st2', 'O1'), ('st0', 'O2')),
-    's7': (('st3', 'O0'), ('st4y', 'O0')),
-    's8': (('st4x', 'O1'), ('st3', 'O1'), ('st0', 'O3')),
-    's9': (('st5', 'O0'), ('st4y', 'O1'), ('st1', 'O2')),
-    's10': (('fin', 'O0'), ('st5', 'O1'), ('st2', 'O2')),
-    's11': (('fin', 'O1'), ('st4x', 'O2'), ('st1', 'O3')),
-    's12': (('st2', 'O3'), ('st0', 'O4')),
-    's13': (('st3', 'O2'), ('st4y', 'O2'), ('st4x', 'O3')),
-    's14': (('st3', 'O3'), ('st4y', 'O3')),
-    's15': (('st5', 'O2'), ('st1', 'O4')),
-    's16': (('fin', 'O2'), ('st5', 'O3'), ('st2', 'O4')),
-    's17': (('fin', 'O3'), ('st4x', 'O4'), ('st3', 'O4')),
-    's18': (('st4y', 'O4'),),
-    's19': (('st5', 'O4'),),
+    'd2': (('st5', 'U0'), ('st0', 'O0'), ('st0', 'O1')),
+    'd4': (('fin', 'U0'), ('st1', 'U2')),
+    's0': (('st4x', 'U1'), ('st3', 'U1')),
+    's1': (('st4y', 'U1'), ('st2', 'U2')),
+    's2': (('st4x', 'U2'), ('st1', 'O0'), ('st0', 'O2')),
+    's3': (('st5', 'U1'), ('st2', 'O0')),
+    's4': (('st1', 'O1'), ('fin', 'U1')),
+    's5': (('st3', 'U2'), ('st4y', 'U2'), ('st4x', 'O0'), ('st2', 'O1')),
+    's6': (('st3', 'O0'), ('st4y', 'O0')),
+    's7': (('st4x', 'O1'), ('st1', 'O2')),
+    's8': (('st2', 'O2'),),
+    's9': (('st5', 'U2'), ('st3', 'O1'), ('st4y', 'O1'), ('st0', 'O3'), ('st0', 'O4')),
+    's10': (('fin', 'U2'), ('st5', 'O0')),
+    's11': (('fin', 'O0'), ('st4x', 'O2'), ('st3', 'O2'), ('st1', 'O3')),
+    's12': (('st4y', 'O2'),),
+    's13': (('st5', 'O1'), ('st2', 'O3')),
+    's14': (('fin', 'O1'), ('st5', 'O2'), ('st1', 'O4')),
+    's15': (('fin', 'O2'), ('st4x', 'O3')),
+    's16': (('st3', 'O3'), ('st4y', 'O3'), ('st2', 'O4')),
+    's17': (('st4x', 'O4'), ('st3', 'O4'), ('st4y', 'O4')),
+    's18': (('st5', 'O3'),),
+    's19': (('fin', 'O3'), ('st5', 'O4')),
     'end': (('fin', 'O4'),),
+    'stats1': (),
 }
-SWAPPED = ('dkv', 'uq1', 'ukv1', 'o0', 'o3', 'o4')
+SWAPPED = ('dq', 'uq0', 'ukv0', 'uq1', 'ukv1', 'uq2', 'ukv2', 'o0', 'o1')
 
 
 def front_kernel(x_hbm, g1_s, gq_s, gkv_s, dq_s, dkv_s, uq_s, ukv_s, o_s, cos_ref, sin_ref, cosT_ref, sinT_ref,
@@ -249,11 +251,18 @@
     stage_o = pltpu.make_async_copy(o_s, ostage, osem.at[2])
     stage_o.start()
 
+    def stat_tile(i, _):
+        pltpu.make_async_copy(x_hbm.at[pl.ds(i * TA, TA)], xa.at[pl.ds(i * TA, TA)], xsem.at[i]).wait()
+        for h in range(TA // 64):
+            rows = pl.ds(pl.multiple_of(i * TA + h * 64, 64), 64)
+            inv[rows, :] = jnp.broadcast_to(rms(xa[rows, :].astype(F32)), (64, 128))
+        return 0
+
     barrier = pltpu.get_barrier_semaphore()
+    for p in plane:
+        pl.semaphore_signal(barrier, inc=1, device_id=(z, p), device_id_type=MESH)
+    pl.semaphore_signal(barrier, inc=1, device_id=dev['Z'], device_id_type=MESH)
     with jax.named_scope('barrier'):
-        for p in plane:
-            pl.semaphore_signal(barrier, inc=1, device_id=(z, p), device_id_type=MESH)
-        pl.semaphore_signal(barrier, inc=1, device_id=dev['Z'], device_id_type=MESH)
         pl.semaphore_wait(barrier, 8)
 
     for j, (gs, gb) in enumerate(((g1_s, g1b), (gq_s, gqb), (gkv_s, gkvb))):
@@ -263,18 +272,9 @@
         pltpu.make_async_copy(gs, gb.at[f], grs.at[j]).start()
     comm(SCHED['stats0'])
 
-    def stat_tile(i, _):
-        @pl.when(i == 4)
-        def _():
-            comm(SCHED['stats1'])
-        pltpu.make_async_copy(x_hbm.at[pl.ds(i * TA, TA)], xa.at[pl.ds(i * TA, TA)], xsem.at[i]).wait()
-        for h in range(TA // 64):
-            rows = pl.ds(pl.multiple_of(i * TA + h * 64, 64), 64)
-            inv[rows, :] = jnp.broadcast_to(rms(xa[rows, :].astype(F32)), (64, 128))
-        return 0
-
-    with jax.named_scope('stats'):
+    with jax.named_scope('stats_b'):
         lax.fori_loop(0, T // TA, stat_tile, 0)
+    comm(SCHED['stats1'])
     with jax.named_scope('gains'):
         for j, gb in enumerate((g1b, gqb, gkvb)):
             pltpu.make_async_copy(gb, gb, grs.at[j]).wait()
@@ -379,14 +379,14 @@
         zr = 128 * h + (96 if h % 2 == 0 else 32)
         qT[zr:zr + 32, :] = jnp.zeros((32, TC), BF16)
 
-    def load_group(g):
-        uc = pl.ds(pl.multiple_of(g * (HG * 96), 128), HG * 96)
-        wqT[...] = wuq[:, uc].T
-        for j in range(HG // 2):
-            t0 = wukv[:, pl.ds(pl.multiple_of(g * (HG * 128) + 256 * j, 128), 128)]
-            t1 = wukv[:, pl.ds(pl.multiple_of(g * (HG * 128) + 256 * j + 128, 128), 128)]
-            wk[:, 128 * j:128 * j + 128] = jnp.concatenate([t0[:, :64], t1[:, :64]], axis=1)
-            wvT[128 * j:128 * j + 128, :] = jnp.concatenate([t0[:, 64:], t1[:, 64:]], axis=1).T
+    def prepare(g, k, slot):
+        col = 256 * jnp.minimum(k, 2)
+        wqT[slot, pl.ds(pl.multiple_of(col, 256), 256), :] = wuq[:, pl.ds(pl.multiple_of(g * (HG * 96) + col, 128), 256)].T
+        t0 = wukv[:, pl.ds(pl.multiple_of(g * (HG * 128) + 256 * k, 128), 128)]
+        t1 = wukv[:, pl.ds(pl.multiple_of(g * (HG * 128) + 256 * k + 128, 128), 128)]
+        lanes = pl.ds(pl.multiple_of(128 * k, 128), 128)
+        wk[slot, :, lanes] = jnp.concatenate([t0[:, :64], t1[:, :64]], axis=1)
+        wvT[slot, lanes, :] = jnp.concatenate([t0[:, 64:], t1[:, 64:]], axis=1).T
 
     def out_copy(i):
         g, tc = i // NCH, i % NCH
@@ -397,18 +397,20 @@
         tok = pl.multiple_of(tc * TC, TC)
         at('s', i)
 
-        @pl.when(tc == 0)
+        @pl.when(i == 0)
         def _():
-            with jax.named_scope('load_group'):
-                load_group(g)
-
+            with jax.named_scope('prepare'):
+                for k in range(4):
+                    prepare(0, k, 0)
+
+        here = g % 2
         @pl.when(i >= 2)
         def _():
             out_copy(i - 2).wait()
 
         slot = i % 2
         for n in range(TC // 256):
-            q = dot(wqT[...], cqT[:, pl.ds(tok + 256 * n, 256)])
+            q = dot(wqT[here], cqT[:, pl.ds(tok + 256 * n, 256)])
             cols = slice(256 * n, 256 * n + 256)
             for h in range(HG):
                 nope = q[96 * h:96 * h + 64]
@@ -418,8 +420,9 @@
                 qT[qn:qn + 64, cols] = nope.astype(BF16)
                 qT[qp:qp + 16, cols] = (lo * co - hi * si).astype(BF16)
                 qT[qp + 16:qp + 32, cols] = (hi * co + lo * si).astype(BF16)
-        kbuf[...] = dot(cbuf[pl.ds(tok, TC), :], wk[...]).astype(BF16)
-        vT[...] = dot(wvT[...], cT[:, pl.ds(tok, TC)]).astype(BF16)
+        kbuf[...] = dot(cbuf[pl.ds(tok, TC), :], wk[here]).astype(BF16)
+        vT[...] = dot(wvT[here], cT[:, pl.ds(tok, TC)]).astype(BF16)
+        prepare(jnp.minimum(g + 1, H // HG - 1), tc, 1 - here)
 
         for p in range(TC // S):
             row = p * S
@@ -467,7 +470,7 @@
             V((T, D), BF16), V((D, QR), BF16), V((D, KR + RD), BF16), V((QR, H * 96), BF16), V((KR, H * 128), BF16), V((320, D), BF16),
             V((8, 1, 320), BF16), V((8, 1, 96), BF16), V((8, 1, 32), BF16), V((T, QR), F32), V((T, KR + RD), F32), V((T, 128), F32),
             V((QR, T), BF16), V((T, KR), BF16), V((KR, T), BF16), V((T, RD), BF16), V((T // S, RD, S), BF16),
-            V((HG * 96, QR), BF16), V((KR, HG * 64), BF16), V((HG * 64, KR), BF16), V((HG * 128, TC), BF16), V((TC, HG * 64), BF16), V((HG * 64, TC), BF16), V((2, TC, HG * 64), BF16),
+            V((2, HG * 96, QR), BF16), V((2, KR, HG * 64), BF16), V((2, HG * 64, KR), BF16), V((HG * 128, TC), BF16), V((TC, HG * 64), BF16), V((HG * 64, TC), BF16), V((2, TC, HG * 64), BF16),
             dma((len(PIECES),)), dma((len(PIECES) - 2, 7)), dma((2, 11)), dma((len(PIECES),)), dma((3,)), dma((3,)), dma((T // TA,)), dma((3,)), dma((2,)),
         ],
         compiler_params=pltpu.CompilerParams(collective_id=0, has_side_effects=True, vmem_limit_bytes=63 << 20),

time: 133 us -> 129 us (0.970)
  Pallas kernels: 129 us -> 125 us
    pallas_call x1, Pallas kernels: 94.4 us -> 90.4 us  [front(): pl.pallas_call(front_kernel, name='front', in_specs=[anyspace] + [vm] * 3...]
where the time goes in v7:
time: 129 us
  Pallas kernels  125 us (97%)
  local copies, waits for them, and re-layouts  3.03 us (2%)
    pallas_call x1, Pallas kernels, front(): pl.pallas_call(front_kernel, name='front', in_specs=[anyspace] + [vm] * 3...  90.4 us
    pallas_call x1, Pallas kernels, outp(): pl.pallas_call(out_kernel, grid=(nt, T // tm), name='outp', in_specs=[pl....  34.7 us

profile of v7, /device:TPU:0, one launch (start us, length us, event | category | flops | bytes accessed | tf_op | source)
XLA Modules:
  0.0 128.8 jit_solution(1360015148156812005)
XLA Ops:
  0.6 1.2 broadcast_in_dim.9.g1_s
  1.9 1.8 %copy.16.dkv_s = bf16[320,288]{1,0:T(8,128)(2,1)} copy(bf16[320,288]{0,1:T(8,128)(2,1)} %param.18) | data formatting | bytes 368640 | tf_op args[5]
  3.7 90.4 %front.1 = (bf16[2048,2560]{1,0:T(8,128)(2,1)}, bf16[2560,2560]{1,0:T(8,128)(2,1)}, bf16[2048,256]{1,0:T(8,128)(2,1)}, bf16[16,32,128]{2,1,0:T(8,128)(2,1)}) custom-call(bf16[2048,2560]{1,0:T(8,128)(2,1)} %bitcast.6, bf16[1,320]{1,0:T(2,128)(2,1)} %broadcast_in_dim.9.g1_s, bf16[1,96]{1,0:T(2,128)(2,1)} %bitcast.8, bf16[1,32]{1,0:T(2,128)(2,1)} %bitcast.9, ...), custom_call_target="tpu_custom_call" | custom-call | tf_op jit(solution)/shard_map/front/pallas_call | solution.py:464
  94.1 34.7 %outp.1 = (bf16[2048,2560]{1,0:T(8,128)(2,1)}, bf16[2048,256]{1,0:T(8,128)(2,1)}, bf16[16,32,128]{2,1,0:T(8,128)(2,1)}) custom-call(bf16[2048,2560]{1,0:T(8,128)(2,1)} %get-tuple-element.10.o_ref, bf16[2560,2560]{1,0:T(8,128)(2,1)} %get-tuple-element.11.w_ref, bf16[2048,2560]{1,0:T(8,128)(2,1)} %bitcast.7, bf16[2048,256]{1,0:T(8,128)(2,1)} %get-tuple-element.12.c_ref, ...), custom_call_target="tpu_custom_call" | custom-call | tf_op jit(solution)/shard_map/outp/pallas_call | solution.py:492

commit v8 on v7

--- a/solution.py
+++ b/solution.py
@@ -120,10 +120,11 @@
 SWAPPED = ('dq', 'uq0', 'ukv0', 'uq1', 'ukv1', 'uq2', 'ukv2', 'o0', 'o1')
 
 
-def front_kernel(x_hbm, g1_s, gq_s, gkv_s, dq_s, dkv_s, uq_s, ukv_s, o_s, cos_ref, sin_ref, cosT_ref, sinT_ref,
+def front_kernel(x_hbm, g1_s, gq_s, gkv_s, dq_s, dkv_t, uq_s, ukv_s, o_s, cos_ref, sin_ref, cosT_ref, sinT_ref,
                  attn_hbm, wo_hbm, c_hbm, r_hbm,
                  xa, wdq, wdkv, wuq, wukv, ostage, g1b, gqb, gkvb, accq, acck, inv, cqT, cbuf, cT, rbuf, rT,
                  wqT, wk, wvT, qT, kbuf, vT, obuf,
+                 dkv_in, dkv_s,
                  ssem, rsem, dsem, lsem, gss, grs, xsem, osem, csem):
     z, f = lax.axis_index('dp'), lax.axis_index('fsdp')
     core, xx, yy = f % 2, (f // 2) % 2, f // 4
@@ -258,10 +259,14 @@
             inv[rows, :] = jnp.broadcast_to(rms(xa[rows, :].astype(F32)), (64, 128))
         return 0
 
+    turn = pltpu.make_async_copy(dkv_t, dkv_in, csem.at[2])
+    turn.start()
     barrier = pltpu.get_barrier_semaphore()
     for p in plane:
         pl.semaphore_signal(barrier, inc=1, device_id=(z, p), device_id_type=MESH)
     pl.semaphore_signal(barrier, inc=1, device_id=dev['Z'], device_id_type=MESH)
+    turn.wait()
+    dkv_s[...] = dkv_in[...].T
     with jax.named_scope('barrier'):
         pl.semaphore_wait(barrier, 8)
 
@@ -471,7 +476,8 @@
             V((8, 1, 320), BF16), V((8, 1, 96), BF16), V((8, 1, 32), BF16), V((T, QR), F32), V((T, KR + RD), F32), V((T, 128), F32),
             V((QR, T), BF16), V((T, KR), BF16), V((KR, T), BF16), V((T, RD), BF16), V((T // S, RD, S), BF16),
             V((2, HG * 96, QR), BF16), V((2, KR, HG * 64), BF16), V((2, HG * 64, KR), BF16), V((HG * 128, TC), BF16), V((TC, HG * 64), BF16), V((HG * 64, TC), BF16), V((2, TC, HG * 64), BF16),
-            dma((len(PIECES),)), dma((len(PIECES) - 2, 7)), dma((2, 11)), dma((len(PIECES),)), dma((3,)), dma((3,)), dma((T // TA,)), dma((3,)), dma((2,)),
+            V((KR + RD, 320), BF16), V((320, KR + RD), BF16),
+            dma((len(PIECES),)), dma((len(PIECES) - 2, 7)), dma((2, 11)), dma((len(PIECES),)), dma((3,)), dma((3,)), dma((T // TA,)), dma((3,)), dma((3,)),
         ],
         compiler_params=pltpu.CompilerParams(collective_id=0, has_side_effects=True, vmem_limit_bytes=63 << 20),
     )(x, *gains, *ws, *(jnp.asarray(t) for t in tab))
@@ -512,7 +518,7 @@
     def local(tok, g1, wdq, gq, wuq, wkv, gkv, wukv, wo):
         cos, sin = tables()
         x = tok.reshape(T, D)
-        o, w, c, r = front(x, (g1[None], gq[None], gkv[None]), (wdq, wkv, wuq, wukv, wo), cos, sin)
+        o, w, c, r = front(x, (g1[None], gq[None], gkv[None]), (wdq, wkv.T, wuq, wukv, wo), cos, sin)
         y, c, r = outp(o, w, x, c, r)
         return y.reshape(tok.shape), c.reshape(-1, S, KR), jnp.swapaxes(r, 1, 2)
 

time: 129 us -> 131 us (1.016)
  Pallas kernels: 125 us -> 129 us
  local copies, waits for them, and re-layouts: 3.03 us -> 1.24 us
    pallas_call x1, Pallas kernels: 90.4 us -> 93.9 us  [front(): pl.pallas_call(front_kernel, name='front', in_specs=[anyspace] + [vm] * 3...]
    unnamed x1 -> x0, local copies, waits for them, and re-layouts: 1.78 us -> none
where the time goes in v8:
time: 131 us; the launch traced here: 130 us
  Pallas kernels  129 us (98%)
    pallas_call x1, Pallas kernels, front(): pl.pallas_call(front_kernel, name='front', in_specs=[anyspace] + [vm] * 3...  93.9 us
    pallas_call x1, Pallas kernels, outp(): pl.pallas_call(out_kernel, grid=(nt, T // tm), name='outp', in_specs=[pl....  34.7 us

profile of v8, /device:TPU:0, one launch (start us, length us, event | category | flops | bytes accessed | tf_op | source)
XLA Modules:
  0.0 130.5 jit_solution(9132822635096357279)
XLA Ops:
  0.6 1.2 broadcast_in_dim.9.g1_s
  1.9 93.9 %front.1 = (bf16[2048,2560]{1,0:T(8,128)(2,1)}, bf16[2560,2560]{1,0:T(8,128)(2,1)}, bf16[2048,256]{1,0:T(8,128)(2,1)}, bf16[16,32,128]{2,1,0:T(8,128)(2,1)}) custom-call(bf16[2048,2560]{1,0:T(8,128)(2,1)} %bitcast.7, bf16[1,320]{1,0:T(2,128)(2,1)} %broadcast_in_dim.9.g1_s, bf16[1,96]{1,0:T(2,128)(2,1)} %bitcast.10, bf16[1,32]{1,0:T(2,128)(2,1)} %bitcast.11, ...), custom_call_target="tpu_custom_call" | custom-call | tf_op jit(solution)/shard_map/front/pallas_call | solution.py:469
  95.8 34.7 %outp.1 = (bf16[2048,2560]{1,0:T(8,128)(2,1)}, bf16[2048,256]{1,0:T(8,128)(2,1)}, bf16[16,32,128]{2,1,0:T(8,128)(2,1)}) custom-call(bf16[2048,2560]{1,0:T(8,128)(2,1)} %get-tuple-element.10.o_ref, bf16[2560,2560]{1,0:T(8,128)(2,1)} %get-tuple-element.11.w_ref, bf16[2048,2560]{1,0:T(8,128)(2,1)} %bitcast.8, bf16[2048,256]{1,0:T(8,128)(2,1)} %get-tuple-element.12.c_ref, ...), custom_call_target="tpu_custom_call" | custom-call | tf_op jit(solution)/shard_map/outp/pallas_call | solution.py:498

commit v9 on v8

--- a/solution.py
+++ b/solution.py
@@ -247,10 +247,19 @@
                 lax.cond(i < ms[h][0], lambda: tree(ms[:h]), lambda: tree(ms[h:]))
         tree(marks)
 
-    for i in range(T // TA):
-        pltpu.make_async_copy(x_hbm.at[pl.ds(i * TA, TA)], xa.at[pl.ds(i * TA, TA)], xsem.at[i]).start()
+    barrier = pltpu.get_barrier_semaphore()
+    for p in plane:
+        pl.semaphore_signal(barrier, inc=1, device_id=(z, p), device_id_type=MESH)
+    pl.semaphore_signal(barrier, inc=1, device_id=dev['Z'], device_id_type=MESH)
+    turn = pltpu.make_async_copy(dkv_t, dkv_in, csem.at[2])
+    turn.start()
     stage_o = pltpu.make_async_copy(o_s, ostage, osem.at[2])
-    stage_o.start()
+
+    def load_x(lo, hi):
+        for i in range(lo, hi):
+            pltpu.make_async_copy(x_hbm.at[pl.ds(i * TA, TA)], xa.at[pl.ds(i * TA, TA)], xsem.at[i]).start()
+
+    load_x(0, 1)
 
     def stat_tile(i, _):
         pltpu.make_async_copy(x_hbm.at[pl.ds(i * TA, TA)], xa.at[pl.ds(i * TA, TA)], xsem.at[i]).wait()
@@ -259,13 +268,8 @@
             inv[rows, :] = jnp.broadcast_to(rms(xa[rows, :].astype(F32)), (64, 128))
         return 0
 
-    turn = pltpu.make_async_copy(dkv_t, dkv_in, csem.at[2])
-    turn.start()
-    barrier = pltpu.get_barrier_semaphore()
-    for p in plane:
-        pl.semaphore_signal(barrier, inc=1, device_id=(z, p), device_id_type=MESH)
-    pl.semaphore_signal(barrier, inc=1, device_id=dev['Z'], device_id_type=MESH)
     turn.wait()
+    load_x(1, T // TA)
     dkv_s[...] = dkv_in[...].T
     with jax.named_scope('barrier'):
         pl.semaphore_wait(barrier, 8)
@@ -277,6 +281,7 @@
         pltpu.make_async_copy(gs, gb.at[f], grs.at[j]).start()
     comm(SCHED['stats0'])
 
+    stage_o.start()
     with jax.named_scope('stats_b'):
         lax.fori_loop(0, T // TA, stat_tile, 0)
     comm(SCHED['stats1'])

time: 131 us -> 127 us (0.969)
  Pallas kernels: 129 us -> 125 us
    pallas_call x1, Pallas kernels: 93.9 us -> 90.6 us  [front(): pl.pallas_call(front_kernel, name='front', in_specs=[anyspace] + [vm] * 3...]
where the time goes in v9:
time: 127 us
  Pallas kernels  125 us (98%)
    pallas_call x1, Pallas kernels, front(): pl.pallas_call(front_kernel, name='front', in_specs=[anyspace] + [vm] * 3...  90.6 us
    pallas_call x1, Pallas kernels, outp(): pl.pallas_call(out_kernel, grid=(nt, T // tm), name='outp', in_specs=[pl....  34.7 us

profile of v9, /device:TPU:0, one launch (start us, length us, event | category | flops | bytes accessed | tf_op | source)
XLA Modules:
  0.0 127.2 jit_solution(16778540622859560515)
XLA Ops:
  0.6 1.2 broadcast_in_dim.9.g1_s
  1.9 90.6 %front.1 = (bf16[2048,2560]{1,0:T(8,128)(2,1)}, bf16[2560,2560]{1,0:T(8,128)(2,1)}, bf16[2048,256]{1,0:T(8,128)(2,1)}, bf16[16,32,128]{2,1,0:T(8,128)(2,1)}) custom-call(bf16[2048,2560]{1,0:T(8,128)(2,1)} %bitcast.7, bf16[1,320]{1,0:T(2,128)(2,1)} %broadcast_in_dim.9.g1_s, bf16[1,96]{1,0:T(2,128)(2,1)} %bitcast.10, bf16[1,32]{1,0:T(2,128)(2,1)} %bitcast.11, ...), custom_call_target="tpu_custom_call" | custom-call | tf_op jit(solution)/shard_map/front/pallas_call | solution.py:474
  92.5 34.7 %outp.1 = (bf16[2048,2560]{1,0:T(8,128)(2,1)}, bf16[2048,256]{1,0:T(8,128)(2,1)}, bf16[16,32,128]{2,1,0:T(8,128)(2,1)}) custom-call(bf16[2048,2560]{1,0:T(8,128)(2,1)} %get-tuple-element.10.o_ref, bf16[2560,2560]{1,0:T(8,128)(2,1)} %get-tuple-element.11.w_ref, bf16[2048,2560]{1,0:T(8,128)(2,1)} %bitcast.8, bf16[2048,256]{1,0:T(8,128)(2,1)} %get-tuple-element.12.c_ref, ...), custom_call_target="tpu_custom_call" | custom-call | tf_op jit(solution)/shard_map/outp/pallas_call | solution.py:503

commit v10 on v9

--- a/solution.py
+++ b/solution.py
@@ -38,18 +38,18 @@
 
 PIECES = (
     ('dq', 'dq', False, 320, 0, 768, 112),
-    ('dkv', 'dkv', False, 320, 0, 288, 128),
-    ('uq0', 'uq', False, 96, 0, 1536, 32),
-    ('ukv0', 'ukv', True, 32, 0, 2048, 768),
-    ('uq1', 'uq', False, 96, 1536, 1536, 32),
-    ('ukv1', 'ukv', True, 32, 2048, 2048, 768),
-    ('uq2', 'uq', False, 96, 3072, 768, 16),
-    ('ukv2', 'ukv', True, 32, 4096, 1024, 256),
+    ('dkv', 'dkv', False, 320, 0, 288, 112),
+    ('uq0', 'uq', False, 96, 0, 768, 32),
+    ('ukv0', 'ukv', True, 32, 0, 1024, 128),
+    ('uq1', 'uq', False, 96, 768, 1536, 32),
+    ('ukv1', 'ukv', True, 32, 1024, 2048, 768),
+    ('uq2', 'uq', False, 96, 2304, 1536, 32),
+    ('ukv2', 'ukv', True, 32, 3072, 2048, 768),
     ('o0', 'o', False, 320, 0, 512, 128),
-    ('o1', 'o', False, 320, 512, 512, 128),
-    ('o2', 'o', False, 320, 1024, 512, 96),
-    ('o3', 'o', False, 320, 1536, 512, 80),
-    ('o4', 'o', False, 320, 2048, 512, 64),
+    ('o1', 'o', False, 320, 512, 512, 112),
+    ('o2', 'o', False, 320, 1024, 512, 80),
+    ('o3', 'o', False, 320, 1536, 512, 64),
+    ('o4', 'o', False, 320, 2048, 512, 96),
 )
 PIDX = {p[0]: i for i, p in enumerate(PIECES)}
 SPLIT = ('S1a', 'S1b', 'S2a', 'S2b', 'S3a', 'S3b')
@@ -78,46 +78,49 @@
 SCHED = {
     'stats0': (('st0', 'K'), ('st0', 'D')),
     'norm1': (('st1', 'K'),),
-    'norm2': (('st2d', 'K'),),
+    'norm3': (('st2d', 'K'),),
     'part0': (('recv', 'K', 'S0'), ('recv', 'D', 'S0')),
+    'part1': (('st0', 'U0'),),
     'part2': (('st4xd', 'K'), ('st1', 'D')),
-    'k0': (('st0', 'U0'), ('recv', 'K', 'S1a+S1b')),
+    'k0': (('recv', 'K', 'S1a+S1b'),),
     'k1': (('st2d', 'D'),),
-    'k2': (('st3', 'K'), ('st4yd', 'K'), ('st5a', 'K'), ('recv', 'K', 'S2a+S2b'), ('st4xd', 'D')),
-    'k4': (('st3', 'D'), ('st5b', 'K'), ('st4yd', 'D'), ('st1', 'U0'), ('recv', 'K', 'S3a+S3b'), ('st0', 'U1')),
-    'k5': (('st2', 'U0'),),
-    'q0': (('st5a', 'D'), ('recv', 'D', 'S1a+S1b')),
-    'q1': (('st5b', 'D'),),
-    'q4': (('st4x', 'U0'), ('st3', 'U0'), ('recv', 'D', 'S2a+S2b')),
-    'q5': (('st1', 'U1'),),
-    'q7': (('st4y', 'U0'), ('st0', 'U2')),
-    'd0': (('st2', 'U1'), ('recv', 'D', 'S3a+S3b')),
-    'd2': (('st5', 'U0'), ('st0', 'O0'), ('st0', 'O1')),
-    'd4': (('fin', 'U0'), ('st1', 'U2')),
-    's0': (('st4x', 'U1'), ('st3', 'U1')),
-    's1': (('st4y', 'U1'), ('st2', 'U2')),
-    's2': (('st4x', 'U2'), ('st1', 'O0'), ('st0', 'O2')),
-    's3': (('st5', 'U1'), ('st2', 'O0')),
-    's4': (('st1', 'O1'), ('fin', 'U1')),
-    's5': (('st3', 'U2'), ('st4y', 'U2'), ('st4x', 'O0'), ('st2', 'O1')),
-    's6': (('st3', 'O0'), ('st4y', 'O0')),
-    's7': (('st4x', 'O1'), ('st1', 'O2')),
-    's8': (('st2', 'O2'),),
-    's9': (('st5', 'U2'), ('st3', 'O1'), ('st4y', 'O1'), ('st0', 'O3'), ('st0', 'O4')),
-    's10': (('fin', 'U2'), ('st5', 'O0')),
-    's11': (('fin', 'O0'), ('st4x', 'O2'), ('st3', 'O2'), ('st1', 'O3')),
-    's12': (('st4y', 'O2'),),
+    'k2': (('st0', 'U1'), ('st3', 'K'), ('st4yd', 'K'), ('st5a', 'K'), ('recv', 'K', 'S2a+S2b'), ('st4xd', 'D'), ('st1', 'U0')),
+    'k3': (('st2', 'U0'),),
+    'q0': (('recv', 'D', 'S1a+S1b'),),
+    'q3': (('st5b', 'K'), ('st3', 'D'), ('st4yd', 'D'), ('st5a', 'D')),
+    'k4': (('st4x', 'U0'), ('recv', 'K', 'S3a+S3b')),
+    'q4': (('st1', 'U1'), ('recv', 'D', 'S2a+S2b')),
+    'q5': (('st0', 'U2'),),
+    'q6': (('st0', 'O0'), ('st5b', 'D')),
+    'q7': (('st3', 'U0'), ('st4y', 'U0'), ('st2', 'U1')),
+    'd0': (('recv', 'D', 'S3a+S3b'),),
+    'd1': (('st4x', 'U1'),),
+    'd2': (('st3', 'U1'),),
+    'd4': (('st4y', 'U1'),),
+    's0': (('st1', 'U2'), ('st5', 'U0'), ('fin', 'U0')),
+    's1': (('st2', 'U2'), ('st0', 'O1')),
+    's2': (('st4x', 'U2'), ('st1', 'O0'), ('st2', 'O0')),
+    's3': (('st5', 'U1'),),
+    's4': (('st3', 'U2'), ('st4y', 'U2'), ('st0', 'O2'), ('fin', 'U1')),
+    's5': (('st4x', 'O0'), ('st1', 'O1')),
+    's6': (('st2', 'O1'),),
+    's7': (('st5', 'U2'), ('st3', 'O0'), ('st4y', 'O0'), ('st1', 'O2')),
+    's8': (('st4x', 'O1'), ('st0', 'O3'), ('st0', 'O4'), ('fin', 'U2')),
+    's9': (('st2', 'O2'),),
+    's10': (('st3', 'O1'), ('st4y', 'O1')),
+    's11': (('st5', 'O0'), ('st4x', 'O2'), ('st3', 'O2'), ('st1', 'O3')),
+    's12': (('fin', 'O0'), ('st4y', 'O2')),
     's13': (('st5', 'O1'), ('st2', 'O3')),
-    's14': (('fin', 'O1'), ('st5', 'O2'), ('st1', 'O4')),
-    's15': (('fin', 'O2'), ('st4x', 'O3')),
-    's16': (('st3', 'O3'), ('st4y', 'O3'), ('st2', 'O4')),
-    's17': (('st4x', 'O4'), ('st3', 'O4'), ('st4y', 'O4')),
+    's14': (('fin', 'O1'), ('st1', 'O4')),
+    's15': (('st4x', 'O3'), ('st2', 'O4')),
+    's16': (('st5', 'O2'), ('st3', 'O3'), ('st4y', 'O3'), ('st4x', 'O4')),
+    's17': (('fin', 'O2'), ('st3', 'O4'), ('st4y', 'O4')),
     's18': (('st5', 'O3'),),
     's19': (('fin', 'O3'), ('st5', 'O4')),
     'end': (('fin', 'O4'),),
     'stats1': (),
 }
-SWAPPED = ('dq', 'uq0', 'ukv0', 'uq1', 'ukv1', 'uq2', 'ukv2', 'o0', 'o1')
+SWAPPED = ('uq0', 'ukv0', 'uq1', 'ukv1', 'uq2', 'ukv2', 'o0')
 
 
 def front_kernel(x_hbm, g1_s, gq_s, gkv_s, dq_s, dkv_t, uq_s, ukv_s, o_s, cos_ref, sin_ref, cosT_ref, sinT_ref,
@@ -325,7 +328,7 @@
 
     def q_part(x_not_y, i, _):
         at('q', i if x_not_y else i + 4)
-        if x_not_y:
+        if not x_not_y:
             finish_kv(2 * i)
             finish_kv(2 * i + 1)
         cols, rows = quarter_cols(0, 1) if x_not_y else quarter_cols(1, 0), pl.ds(pl.multiple_of(i * 512, 512), 512)
@@ -371,9 +374,11 @@
     with jax.named_scope('own'):
         lax.fori_loop(0, 4, own_part, 0)
     with jax.named_scope('kv'):
-        lax.fori_loop(0, 6, kv_part, 0)
+        lax.fori_loop(0, 4, kv_part, 0)
     with jax.named_scope('qx'):
         lax.fori_loop(0, 4, functools.partial(q_part, True), 0)
+    with jax.named_scope('kd'):
+        lax.fori_loop(4, 6, kv_part, 0)
     with jax.named_scope('qy'):
         lax.fori_loop(0, 4, functools.partial(q_part, False), 0)
     with jax.named_scope('last'):
@@ -407,11 +412,11 @@
         tok = pl.multiple_of(tc * TC, TC)
         at('s', i)
 
-        @pl.when(i == 0)
+        @pl.when(i * (4 - i) == 0)
         def _():
             with jax.named_scope('prepare'):
                 for k in range(4):
-                    prepare(0, k, 0)
+                    prepare(g, k, g % 2)
 
         here = g % 2
         @pl.when(i >= 2)
@@ -432,7 +437,7 @@
                 qT[qp + 16:qp + 32, cols] = (hi * co + lo * si).astype(BF16)
         kbuf[...] = dot(cbuf[pl.ds(tok, TC), :], wk[here]).astype(BF16)
         vT[...] = dot(wvT[here], cT[:, pl.ds(tok, TC)]).astype(BF16)
-        prepare(jnp.minimum(g + 1, H // HG - 1), tc, 1 - here)
+        prepare(jnp.minimum(g + jnp.minimum(g, 1), H // HG - 1), tc, 1 - here)
 
         for p in range(TC // S):
             row = p * S

time: 127 us -> 127 us (level)
  no operation moved by 1% of the time
where the time goes in v10:
time: 127 us
  Pallas kernels  125 us (98%)
    pallas_call x1, Pallas kernels, front(): pl.pallas_call(front_kernel, name='front', in_specs=[anyspace] + [vm] * 3...  89.8 us
    pallas_call x1, Pallas kernels, outp(): pl.pallas_call(out_kernel, grid=(nt, T // tm), name='outp', in_specs=[pl....  34.9 us

profile of v10, /device:TPU:0, one launch (start us, length us, event | category | flops | bytes accessed | tf_op | source)
XLA Modules:
  0.0 126.5 jit_solution(8024252955144128890)
XLA Ops:
  0.6 1.2 broadcast_in_dim.9.g1_s
  1.9 89.8 %front.1 = (bf16[2048,2560]{1,0:T(8,128)(2,1)}, bf16[2560,2560]{1,0:T(8,128)(2,1)}, bf16[2048,256]{1,0:T(8,128)(2,1)}, bf16[16,32,128]{2,1,0:T(8,128)(2,1)}) custom-call(bf16[2048,2560]{1,0:T(8,128)(2,1)} %bitcast.7, bf16[1,320]{1,0:T(2,128)(2,1)} %broadcast_in_dim.9.g1_s, bf16[1,96]{1,0:T(2,128)(2,1)} %bitcast.10, bf16[1,32]{1,0:T(2,128)(2,1)} %bitcast.11, ...), custom_call_target="tpu_custom_call" | custom-call | tf_op jit(solution)/shard_map/front/pallas_call | solution.py:479
  91.6 34.9 %outp.1 = (bf16[2048,2560]{1,0:T(8,128)(2,1)}, bf16[2048,256]{1,0:T(8,128)(2,1)}, bf16[16,32,128]{2,1,0:T(8,128)(2,1)}) custom-call(bf16[2048,2560]{1,0:T(8,128)(2,1)} %get-tuple-element.10.o_ref, bf16[2560,2560]{1,0:T(8,128)(2,1)} %get-tuple-element.11.w_ref, bf16[2048,2560]{1,0:T(8,128)(2,1)} %bitcast.8, bf16[2048,256]{1,0:T(8,128)(2,1)} %get-tuple-element.12.c_ref, ...), custom_call_target="tpu_custom_call" | custom-call | tf_op jit(solution)/shard_map/outp/pallas_call | solution.py:508

commit v11 on v10

--- a/solution.py
+++ b/solution.py
@@ -127,9 +127,10 @@
                  attn_hbm, wo_hbm, c_hbm, r_hbm,
                  xa, wdq, wdkv, wuq, wukv, ostage, g1b, gqb, gkvb, accq, acck, inv, cqT, cbuf, cT, rbuf, rT,
                  wqT, wk, wvT, qT, kbuf, vT, obuf,
-                 dkv_in, dkv_s,
+                 dkv_in, dkv_s, g1sem, g1r0, g1r1, g1r2, g1r3, g1r4, g1r5, g1r6, g1r7,
                  ssem, rsem, dsem, lsem, gss, grs, xsem, osem, csem):
     z, f = lax.axis_index('dp'), lax.axis_index('fsdp')
+    g1r = (g1r0, g1r1, g1r2, g1r3, g1r4, g1r5, g1r6, g1r7)
     core, xx, yy = f % 2, (f // 2) % 2, f // 4
 
     def idx(dx, dy, dc):
@@ -277,7 +278,15 @@
     with jax.named_scope('barrier'):
         pl.semaphore_wait(barrier, 8)
 
-    for j, (gs, gb) in enumerate(((g1_s, g1b), (gq_s, gqb), (gkv_s, gkvb))):
+    def g1_copies():
+        for r, p in enumerate(plane):
+            yield pltpu.make_async_remote_copy(src_ref=g1_s, dst_ref=g1r[r + 1], send_sem=g1sem.at[0, r], recv_sem=g1sem.at[1, r],
+                                               device_id=(z, p), device_id_type=MESH)
+        yield pltpu.make_async_copy(g1_s, g1r[0], g1sem.at[0, 7])
+
+    for g in g1_copies():
+        g.start()
+    for j, (gs, gb) in enumerate(((gq_s, gqb), (gkv_s, gkvb))):
         for p in plane:
             pltpu.make_async_remote_copy(src_ref=gs, dst_ref=gb.at[f], send_sem=gss.at[j], recv_sem=grs.at[j],
                                          device_id=(z, p), device_id_type=MESH).start()
@@ -289,8 +298,12 @@
         lax.fori_loop(0, T // TA, stat_tile, 0)
     comm(SCHED['stats1'])
     with jax.named_scope('gains'):
-        for j, gb in enumerate((g1b, gqb, gkvb)):
+        for g in g1_copies():
+            g.wait()
+        for j, gb in enumerate((gqb, gkvb)):
             pltpu.make_async_copy(gb, gb, grs.at[j]).wait()
+        for r, p in enumerate([f] + plane):
+            g1b[p] = g1r[r][...].astype(F32).reshape(1, 320)
 
     def row_of(gb):
         return jnp.concatenate([gb[i].astype(F32) for i in range(8)], axis=-1)
@@ -465,7 +478,7 @@
         for o in outs:
             o.wait()
     with jax.named_scope('tail_sends'):
-        for j, gb in enumerate((g1b, gqb, gkvb)):
+        for j, gb in enumerate((gqb, gkvb)):
             pltpu.make_async_copy(gb.at[pl.ds(0, 7)], gb.at[pl.ds(0, 7)], gss.at[j]).wait()
         for p in PIECES:
             take(p[0], units(p[0], 'sent'), ssem.at[PIDX[p[0]]])
@@ -483,10 +496,11 @@
         out_shape=[jax.ShapeDtypeStruct((T, H * VD), BF16), jax.ShapeDtypeStruct((H * VD, D), BF16), jax.ShapeDtypeStruct((T, KR), BF16), jax.ShapeDtypeStruct((T // S, RD, S), BF16)],
         scratch_shapes=[
             V((T, D), BF16), V((D, QR), BF16), V((D, KR + RD), BF16), V((QR, H * 96), BF16), V((KR, H * 128), BF16), V((320, D), BF16),
-            V((8, 1, 320), BF16), V((8, 1, 96), BF16), V((8, 1, 32), BF16), V((T, QR), F32), V((T, KR + RD), F32), V((T, 128), F32),
+            V((8, 1, 320), F32), V((8, 1, 96), BF16), V((8, 1, 32), BF16), V((T, QR), F32), V((T, KR + RD), F32), V((T, 128), F32),
             V((QR, T), BF16), V((T, KR), BF16), V((KR, T), BF16), V((T, RD), BF16), V((T // S, RD, S), BF16),
             V((2, HG * 96, QR), BF16), V((2, KR, HG * 64), BF16), V((2, HG * 64, KR), BF16), V((HG * 128, TC), BF16), V((TC, HG * 64), BF16), V((HG * 64, TC), BF16), V((2, TC, HG * 64), BF16),
-            V((KR + RD, 320), BF16), V((320, KR + RD), BF16),
+            V((KR + RD, 320), BF16), V((320, KR + RD), BF16), dma((2, 8)),
+            *[V((320,), BF16)] * 8,
             dma((len(PIECES),)), dma((len(PIECES) - 2, 7)), dma((2, 11)), dma((len(PIECES),)), dma((3,)), dma((3,)), dma((T // TA,)), dma((3,)), dma((3,)),
         ],
         compiler_params=pltpu.CompilerParams(collective_id=0, has_side_effects=True, vmem_limit_bytes=63 << 20),
@@ -528,7 +542,7 @@
     def local(tok, g1, wdq, gq, wuq, wkv, gkv, wukv, wo):
         cos, sin = tables()
         x = tok.reshape(T, D)
-        o, w, c, r = front(x, (g1[None], gq[None], gkv[None]), (wdq, wkv.T, wuq, wukv, wo), cos, sin)
+        o, w, c, r = front(x, (g1, gq[None], gkv[None]), (wdq, wkv.T, wuq, wukv, wo), cos, sin)
         y, c, r = outp(o, w, x, c, r)
         return y.reshape(tok.shape), c.reshape(-1, S, KR), jnp.swapaxes(r, 1, 2)
 

time: 127 us -> 126 us (level)
  no operation moved by 1% of the time
where the time goes in v11:
time: 126 us
  Pallas kernels  125 us (99%)
    pallas_call x1, Pallas kernels, front(): pl.pallas_call(front_kernel, name='front', in_specs=[anyspace] + [vm] * 3...  90 us
    pallas_call x1, Pallas kernels, outp(): pl.pallas_call(out_kernel, grid=(nt, T // tm), name='outp', in_specs=[pl....  34.9 us

profile of v11, /device:TPU:0, one launch (start us, length us, event | category | flops | bytes accessed | tf_op | source)
XLA Modules:
  0.0 125.5 jit_solution(5753507146299812335)
XLA Ops:
  0.6 90.0 %front.1 = (bf16[2048,2560]{1,0:T(8,128)(2,1)}, bf16[2560,2560]{1,0:T(8,128)(2,1)}, bf16[2048,256]{1,0:T(8,128)(2,1)}, bf16[16,32,128]{2,1,0:T(8,128)(2,1)}) custom-call(bf16[2048,2560]{1,0:T(8,128)(2,1)} %bitcast.7, bf16[320]{0:T(512)(128)(2,1)} %g1_s.1, bf16[1,96]{1,0:T(2,128)(2,1)} %bitcast.10, bf16[1,32]{1,0:T(2,128)(2,1)} %bitcast.11, ...), custom_call_target="tpu_custom_call" | custom-call | tf_op jit(solution)/shard_map/front/pallas_call | solution.py:492
  90.7 34.9 %outp.1 = (bf16[2048,2560]{1,0:T(8,128)(2,1)}, bf16[2048,256]{1,0:T(8,128)(2,1)}, bf16[16,32,128]{2,1,0:T(8,128)(2,1)}) custom-call(bf16[2048,2560]{1,0:T(8,128)(2,1)} %get-tuple-element.10.o_ref, bf16[2560,2560]{1,0:T(8,128)(2,1)} %get-tuple-element.11.w_ref, bf16[2048,2560]{1,0:T(8,128)(2,1)} %bitcast.8, bf16[2048,256]{1,0:T(8,128)(2,1)} %get-tuple-element.12.c_ref, ...), custom_call_target="tpu_custom_call" | custom-call | tf_op jit(solution)/shard_map/outp/pallas_call | solution.py:522

commit v12 on v11

--- a/solution.py
+++ b/solution.py
@@ -373,12 +373,14 @@
         cols = pl.ds(pl.multiple_of((fd // 2) * 640, 128), 640)
 
         def tile(i, _):
-            pl.when(i % 2 == 0)(functools.partial(at, 'd', i // 2))
-            finish_q(jnp.maximum(i - 1, 0))
-            rows = pl.ds(pl.multiple_of(jnp.minimum(i, T // TA - 1) * TA, TA), TA)
+            at('d', i)
+            before = jnp.maximum(i - 1, 0)
+            finish_q(2 * before)
+            finish_q(2 * before + 1)
+            rows = pl.ds(pl.multiple_of(jnp.minimum(i, T // 512 - 1) * 512, 512), 512)
             accq[rows, :] += dot(xa[rows, cols], wdq[cols, :])
             return 0
-        lax.fori_loop(0, T // TA + 1, tile, 0)
+        lax.fori_loop(0, T // 512 + 1, tile, 0)
 
     with jax.named_scope('norm'):
         lax.fori_loop(0, T // TA, norm_tile, 0)
@@ -472,16 +474,16 @@
     lax.fori_loop(0, STEPS, step, 0)
     with jax.named_scope('fin_O'):
         comm(SCHED['end'])
+    with jax.named_scope('tail_sends'):
+        for j, gb in enumerate((gqb, gkvb)):
+            pltpu.make_async_copy(gb.at[pl.ds(0, 7)], gb.at[pl.ds(0, 7)], gss.at[j]).wait()
+        for p in PIECES:
+            take(p[0], units(p[0], 'sent'), ssem.at[PIDX[p[0]]])
     with jax.named_scope('tail_out'):
         for i in (STEPS - 2, STEPS - 1):
             out_copy(i).wait()
         for o in outs:
             o.wait()
-    with jax.named_scope('tail_sends'):
-        for j, gb in enumerate((gqb, gkvb)):
-            pltpu.make_async_copy(gb.at[pl.ds(0, 7)], gb.at[pl.ds(0, 7)], gss.at[j]).wait()
-        for p in PIECES:
-            take(p[0], units(p[0], 'sent'), ssem.at[PIDX[p[0]]])
 
 
 def front(x, gains, ws, cos, sin):

time: 126 us -> 126 us (level)
  no operation moved by 1% of the time
where the time goes in v12:
time: 126 us
  Pallas kernels  125 us (99%)
    pallas_call x1, Pallas kernels, front(): pl.pallas_call(front_kernel, name='front', in_specs=[anyspace] + [vm] * 3...  90 us
    pallas_call x1, Pallas kernels, outp(): pl.pallas_call(out_kernel, grid=(nt, T // tm), name='outp', in_specs=[pl....  34.9 us

profile of v12, /device:TPU:0, one launch (start us, length us, event | category | flops | bytes accessed | tf_op | source)
XLA Modules:
  0.0 125.5 jit_solution(1672231093060129182)
XLA Ops:
  0.6 90.0 %front.1 = (bf16[2048,2560]{1,0:T(8,128)(2,1)}, bf16[2560,2560]{1,0:T(8,128)(2,1)}, bf16[2048,256]{1,0:T(8,128)(2,1)}, bf16[16,32,128]{2,1,0:T(8,128)(2,1)}) custom-call(bf16[2048,2560]{1,0:T(8,128)(2,1)} %bitcast.7, bf16[320]{0:T(512)(128)(2,1)} %g1_s.1, bf16[1,96]{1,0:T(2,128)(2,1)} %bitcast.10, bf16[1,32]{1,0:T(2,128)(2,1)} %bitcast.11, ...), custom_call_target="tpu_custom_call" | custom-call | tf_op jit(solution)/shard_map/front/pallas_call | solution.py:494
  90.7 34.9 %outp.1 = (bf16[2048,2560]{1,0:T(8,128)(2,1)}, bf16[2048,256]{1,0:T(8,128)(2,1)}, bf16[16,32,128]{2,1,0:T(8,128)(2,1)}) custom-call(bf16[2048,2560]{1,0:T(8,128)(2,1)} %get-tuple-element.10.o_ref, bf16[2560,2560]{1,0:T(8,128)(2,1)} %get-tuple-element.11.w_ref, bf16[2048,2560]{1,0:T(8,128)(2,1)} %bitcast.8, bf16[2048,256]{1,0:T(8,128)(2,1)} %get-tuple-element.12.c_ref, ...), custom_call_target="tpu_custom_call" | custom-call | tf_op jit(solution)/shard_map/outp/pallas_call | solution.py:524
